TPU v7x, 32 devices: a whole 2x2x4 slice. The times are simulated.
32 devices in a mesh: seq: 8 (over z, y), opt: 4 (over x, core).
Axes of the slice: x: 2, y: 2, z: 4, core: 2. Of those that a mesh axis runs over, the one named last changes fastest.
Arguments:
- layer_in: bfloat16 [4, 4096, 4096], P('opt', 'seq'), may hold values from -48 to 48, as said below
- ssm_input: bfloat16 [4, 4096, 4096], P('opt', 'seq'), may hold values from -0.119628906 to 0.119628906
- grad_out: bfloat16 [4, 4096, 4096], P('opt', 'seq'), may hold values from -0.59765625 to 0.59765625
- log_decay: float32 [4, 32, 4096], P('opt', None, 'seq'), may hold values from -1 to 0, as said below
- skip_gain: float32 [32], replicated, may hold values from 0.5 to 2
- w_bc: float32 [4096, 256], P(('seq', 'opt')), may hold values from -0.0078125 to 0.0078125
- m_code: bfloat16 [4096, 256], P(('seq', 'opt')), may hold values from -1 to 1
- m_scale: float32 [256], replicated, may hold values from 0.0001 to 0.001
- row_stat: float32 [4096], P(('seq', 'opt')), may hold values from 3e-07 to 3e-06
- col_stat: float32 [256], replicated, may hold values from 3e-07 to 3e-06
Outputs:
- grad_input: bfloat16 [4, 4096, 4096], P('opt', 'seq')
- update: float32 [4096, 256], P(('seq', 'opt'))
- code_next: bfloat16 [4096, 256], P(('seq', 'opt'))
- scale_next: float32 [256], replicated
- row_next: float32 [4096], P(('seq', 'opt'))
- col_next: float32 [256], replicated
Inputs may be any that keep to these rules, and one draw needn't show every extreme that they name: `layer_in`: real-valued rows of order one. `log_decay`: negative log decays.
All inputs are finite; a program needn't handle non-finite values.
Results may differ from a plain program's by a relative error of at most 0.0095.
Values may be sent and summed in bfloat16 or wider, within the bound.
A program may use at most 256 MiB of HBM per device.

v0:
```python
import functools

import jax
import jax.numpy as jnp
from jax import lax
from jax.experimental import pallas as pl
from jax.experimental.pallas import tpu as pltpu
from jax.sharding import PartitionSpec as P

BLOCK = 256
LANES = 128

beta_one = 0.9
beta_two = 0.95
weight_decay = 0.1
clip_norm = 1.0
tiny_square = 1e-30
adam_floor = 1e-08
peak_floor = 1e-06
norm_floor = 1e-06
highest = lax.Precision.HIGHEST
MESH = pl.DeviceIdType.MESH
VMEM_LIMIT = 60 * 1024 * 1024
f32 = jnp.float32
bf16 = jnp.bfloat16


def dot_nn(a, b):
    return lax.dot_general(a, b, (((1,), (0,)), ((), ())), preferred_element_type=f32)


def dot_nt(a, b):
    return lax.dot_general(a, b, (((1,), (1,)), ((), ())), preferred_element_type=f32)


def dot_tn(a, b):
    return lax.dot_general(a, b, (((0,), (0,)), ((), ())), preferred_element_type=f32)


def as_column(row):
    return jnp.transpose(jnp.broadcast_to(row, (LANES, row.shape[1])))


def widened(column, length):
    return jnp.concatenate([column] * (length // LANES), axis=1)


def mixing_kernel(
    count, n_seq, n_opt, w_ref, x_ref, dy_ref, run_ref, mix_ref, w_out,
    got, send_a, recv_a, send_b, recv_b,
):
    seq = lax.axis_index("seq")
    opt = lax.axis_index("opt")
    h = pl.program_id(0)
    last = pl.num_programs(0) - 1

    def over_seq():
        return swap_all(
            n_seq, seq, lambda s: w_ref, lambda s: got.at[opt, s],
            lambda s: (s, opt), send_a, recv_a,
        )

    def over_opt():
        return swap_all(
            n_opt, opt, lambda o: got.at[opt], lambda o: got.at[o],
            lambda o: (seq, o), send_b, recv_b,
        )

    @pl.when(h == 0)
    def _():
        greet(n_seq * n_opt, seq * n_opt + opt, lambda i: (i // n_opt, lax.rem(i, n_opt)))
        over_seq()[0]()
        got[opt, seq] = w_ref[...]
        mix_ref[...] = jnp.zeros_like(mix_ref)

    @pl.when(h == last // 2)
    def _():
        over_seq()[1]()
        over_opt()[0]()

    row_pos = lax.broadcasted_iota(jnp.int32, (BLOCK, BLOCK), 0)
    col_pos = lax.broadcasted_iota(jnp.int32, (BLOCK, BLOCK), 1)
    for b in range(count):
        rows = slice(b * BLOCK, (b + 1) * BLOCK)
        row = run_ref[0, b : b + 1, :]
        spread = widened(as_column(row), BLOCK) - row
        decays = jnp.exp(jnp.where(row_pos >= col_pos, spread, -jnp.inf))
        mix_ref[b] += decays * dot_nt(dy_ref[rows, :], x_ref[rows, :])

    @pl.when(h == last)
    def _():
        over_opt()[1]()

        def place(s, carry):
            for o in range(n_opt):
                w_out[s, o] = got[o, s]
            return carry

        lax.fori_loop(0, n_seq, place, 0)


def local_kernel(
    count, x_ref, dy_ref, b_ref, c_ref, run_ref, send_ref, starts_ref, outs_ref, b_turned, c_turned
):
    @pl.when(pl.program_id(0) == 0)
    def _():
        b_turned[...] = jnp.transpose(b_ref[...].astype(f32))
        c_turned[...] = jnp.transpose(c_ref[...].astype(f32))

    adds = []
    for b in range(count):
        rows = slice(b * BLOCK, (b + 1) * BLOCK)
        row = run_ref[0, b : b + 1, :]
        closing = row[:, BLOCK - 1 : BLOCK]
        b_scaled = (b_turned[:, rows] * jnp.exp(closing - row)).astype(bf16)
        c_scaled = (c_turned[:, rows] * jnp.exp(row)).astype(bf16)
        adds.append(
            (jnp.exp(closing), dot_nn(b_scaled, x_ref[rows, :]), dot_nn(c_scaled, dy_ref[rows, :]))
        )
    state = None
    for b in range(count):
        starts_ref[0, b] = (jnp.zeros_like(adds[b][1]) if state is None else state).astype(bf16)
        state = adds[b][1] if state is None else adds[b][0] * state + adds[b][1]
    send_ref[0, 0, 0] = state.astype(bf16)
    carried = None
    for b in reversed(range(count)):
        outs_ref[0, b] = (jnp.zeros_like(adds[b][2]) if carried is None else carried).astype(bf16)
        carried = adds[b][2] if carried is None else adds[b][0] * carried + adds[b][2]
    send_ref[0, 1, 0] = carried.astype(bf16)


def grads_kernel(
    count, skip_ref, x_ref, dy_ref, b_ref, c_ref, run_ref, starts_ref, outs_ref, far_ref, mix_ref,
    gx_ref, gbc_ref, affinity, acc_b, acc_c,
):
    h = pl.program_id(0)
    state_dim = b_ref.shape[1]

    @pl.when(h == 0)
    def _():
        acc_b[...] = jnp.zeros_like(acc_b)
        acc_c[...] = jnp.zeros_like(acc_c)
        for b in range(count):
            rows = slice(b * BLOCK, (b + 1) * BLOCK)
            affinity[b] = dot_nt(b_ref[rows, :], c_ref[rows, :])

    row_pos = lax.broadcasted_iota(jnp.int32, (BLOCK, BLOCK), 0)
    col_pos = lax.broadcasted_iota(jnp.int32, (BLOCK, BLOCK), 1)
    closings = [run_ref[0, b : b + 1, BLOCK - 1 : BLOCK] for b in range(count)]
    for b in range(count):
        rows = slice(b * BLOCK, (b + 1) * BLOCK)
        row = run_ref[0, b : b + 1, :]
        column = as_column(row)
        before = sum(closings[:b], jnp.zeros((1, 1), f32))
        after = sum(closings[b + 1 :], jnp.zeros((1, 1), f32))
        far_state = far_ref[0, 0, 0].astype(f32)
        far_grad = far_ref[0, 1, 0].astype(f32)
        state_in = (starts_ref[0, b].astype(f32) + jnp.exp(before) * far_state).astype(bf16)
        grad_in = (outs_ref[0, b].astype(f32) + jnp.exp(after) * far_grad).astype(bf16)
        grow = jnp.exp(column)
        shrink = jnp.exp(closings[b] - column)
        x_blk = x_ref[rows, :]
        dy_blk = dy_ref[rows, :]
        spread = row - widened(column, BLOCK)
        decays = jnp.exp(jnp.where(col_pos >= row_pos, spread, -jnp.inf))
        weighted = (decays * affinity[b]).astype(bf16)
        inner = dot_nn(weighted, dy_blk)
        outer = dot_nn(b_ref[rows, :], grad_in) * shrink
        gx_ref[rows, :] = (inner + outer + skip_ref[h] * dy_blk.astype(f32)).astype(bf16)
        acc_c[rows, :] += grow * dot_nt(dy_blk, state_in)
        acc_b[rows, :] += shrink * dot_nt(x_blk, grad_in)

    @pl.when(h == pl.num_programs(0) - 1)
    def _():
        for b in range(count):
            rows = slice(b * BLOCK, (b + 1) * BLOCK)
            mixing = mix_ref[b].astype(bf16)
            gbc_ref[rows, :state_dim] = (acc_b[rows, :] + dot_tn(mixing, c_ref[rows, :])).astype(bf16)
            gbc_ref[rows, state_dim:] = (acc_c[rows, :] + dot_nn(mixing, b_ref[rows, :])).astype(bf16)


def swap_all(n, me, src_of, dst_of, device_of, send_sem, recv_sem):
    def copy_to(distance):
        other = lax.rem(me + distance, n)
        return pltpu.make_async_remote_copy(
            src_ref=src_of(other), dst_ref=dst_of(me), send_sem=send_sem.at[other],
            recv_sem=recv_sem.at[me], device_id=device_of(other), device_id_type=MESH,
        )

    def copy_from(distance):
        other = lax.rem(me + distance, n)
        return pltpu.make_async_remote_copy(
            src_ref=src_of(other), dst_ref=dst_of(other), send_sem=send_sem.at[other],
            recv_sem=recv_sem.at[other], device_id=device_of(other), device_id_type=MESH,
        )

    def start(distance, carry):
        copy_to(distance).start()
        return carry

    def finish(distance, carry):
        copy = copy_from(distance)
        copy.wait_send()
        copy.wait_recv()
        return carry

    return lambda: lax.fori_loop(1, n, start, 0), lambda: lax.fori_loop(1, n, finish, 0)


def begin_swap(*args):
    start, finish = swap_all(*args)
    start()
    return finish


def greet(n, me, device_of):
    barrier = pltpu.get_barrier_semaphore()

    def signal(distance, carry):
        other = lax.rem(me + distance, n)
        pl.semaphore_signal(barrier, inc=1, device_id=device_of(other), device_id_type=MESH)
        return carry

    lax.fori_loop(1, n, signal, 0)
    pl.semaphore_wait(barrier, n - 1)


def carry_kernel(
    n, send_ref, decay_ref, out_ref, got, got_decay, prefix, landed, run,
    send_a, recv_a, send_d, recv_d, send_b, recv_b,
):
    me = lax.axis_index("seq")
    opt = lax.axis_index("opt")

    def device_of(s):
        return (s, opt)

    greet(n, me, device_of)
    end_d = begin_swap(
        n, me, lambda s: decay_ref.at[s], lambda s: got_decay.at[s], device_of, send_d, recv_d
    )
    end_a = begin_swap(n, me, lambda s: send_ref.at[s], lambda s: got.at[s], device_of, send_a, recv_a)
    end_d()
    end_a()
    got[me] = send_ref[me]
    got_decay[me] = decay_ref[me]

    run[...] = jnp.zeros_like(run)

    def forward(s, carry):
        state = run[0]
        prefix[s, 0] = state.astype(bf16)
        run[0] = got_decay[s] * state + got[s, 0].astype(f32)
        return carry

    def backward(lap, carry):
        s = n - 1 - lap
        state = run[1]
        prefix[s, 1] = state.astype(bf16)
        run[1] = got_decay[s] * state + got[s, 1].astype(f32)
        return carry

    lax.fori_loop(0, n, forward, 0)
    lax.fori_loop(0, n, backward, 0)
    begin_swap(n, me, lambda s: prefix.at[s], lambda s: landed.at[s], device_of, send_b, recv_b)()
    landed[me] = prefix[me]
    out_ref[...] = landed[...]


def step_kernel(
    n_seq, n_opt, part_ref, w_ref, code_ref, scale_ref, row_ref, col_ref,
    update_ref, code_out, scale_out, row_out, col_out,
    got_a, mid, got_b, stats, all_stats, peak, all_peaks,
    send_a, recv_a, send_b, recv_b, send_c, recv_c, send_d, recv_d,
):
    seq = lax.axis_index("seq")
    opt = lax.axis_index("opt")
    n = n_seq * n_opt
    me = seq * n_opt + opt

    def any_device(i):
        return (i // n_opt, lax.rem(i, n_opt))

    greet(n, me, any_device)
    begin_swap(
        n_opt, opt, lambda o: part_ref.at[o], lambda o: got_a.at[o],
        lambda o: (seq, o), send_a, recv_a,
    )()
    got_a[opt] = part_ref[opt]

    def fold(s, carry):
        total = got_a[0, s].astype(f32)
        for o in range(1, n_opt):
            total += got_a[o, s].astype(f32)
        mid[s] = total.astype(bf16)
        return carry

    lax.fori_loop(0, n_seq, fold, 0)
    begin_swap(
        n_seq, seq, lambda s: mid.at[s], lambda s: got_b.at[s],
        lambda s: (s, opt), send_b, recv_b,
    )()
    got_b[seq] = mid[seq]
    grad = got_b[0].astype(f32)
    for s in range(1, n_seq):
        grad += got_b[s].astype(f32)

    rows, cols = grad.shape
    width = n * rows
    squares_raw = grad * grad
    stats[:, :cols] = jnp.sum(squares_raw, axis=0, keepdims=True)
    row_stat = row_ref[...]
    stats[:, cols:] = jnp.broadcast_to(jnp.sum(row_stat, axis=0, keepdims=True), (1, LANES))
    begin_swap(
        n, me, lambda i: stats, lambda i: all_stats.at[i], any_device, send_c, recv_c
    )()
    all_stats[me] = stats[...]
    sums = all_stats[0]
    for i in range(1, n):
        sums += all_stats[i]
    col_raw = sums[:, :cols]
    old_total = sums[:, cols : cols + 1]
    raw_total = jnp.sum(col_raw, axis=1, keepdims=True)
    factor = jnp.minimum(1.0, clip_norm / jnp.sqrt(raw_total + norm_floor))
    scaled = grad * factor
    moment = beta_one * code_ref[...].astype(f32) * scale_ref[...] + (1.0 - beta_one) * scaled
    peak[...] = jnp.max(jnp.abs(moment), axis=0, keepdims=True)
    end_peaks = begin_swap(
        n, me, lambda i: peak, lambda i: all_peaks.at[i], any_device, send_d, recv_d
    )
    col_next = beta_two * col_ref[...] + (1.0 - beta_two) * (
        factor * factor * col_raw / width + tiny_square
    )
    row_next = beta_two * row_stat + (1.0 - beta_two) * (
        jnp.sum(scaled * scaled, axis=1, keepdims=True) / cols + tiny_square
    )
    row_mean = (
        beta_two * old_total
        + (1.0 - beta_two) * (factor * factor * raw_total / cols + width * tiny_square)
    ) / width
    second = row_next * col_next / row_mean
    update_ref[...] = moment / (jnp.sqrt(second) + adam_floor) + weight_decay * w_ref[...]
    row_out[...] = row_next
    col_out[...] = col_next
    end_peaks()
    all_peaks[me] = peak[...]
    scale_next = all_peaks[0]
    for i in range(1, n):
        scale_next = jnp.maximum(scale_next, all_peaks[i])
    scale_next = scale_next + peak_floor
    scale_out[...] = scale_next
    code_out[...] = (moment / scale_next).astype(bf16)


def params(**more):
    return pltpu.CompilerParams(vmem_limit_bytes=VMEM_LIMIT, **more)


def whole():
    return pl.BlockSpec(memory_space=pltpu.VMEM)


def dma(*counts):
    return [pltpu.SemaphoreType.DMA((count,)) for count in counts for _ in range(2)]


def per_device(
    n_seq, n_opt, layer_in, ssm_input, grad_out, log_decay, skip_gain, w_bc, m_code, m_scale,
    row_stat, col_stat,
):
    layer_rows = layer_in[0]
    x = ssm_input[0]
    dy = grad_out[0]
    length, width = layer_rows.shape
    heads = skip_gain.shape[0]
    head_dim = x.shape[1] // heads
    state_dim = w_bc.shape[1] // 2
    count = length // BLOCK
    group = heads // n_seq
    own_rows = w_bc.shape[0]

    ones = (
        lax.broadcasted_iota(jnp.int32, (BLOCK, BLOCK), 0)
        <= lax.broadcasted_iota(jnp.int32, (BLOCK, BLOCK), 1)
    ).astype(f32)
    running = jnp.dot(
        log_decay[0].reshape(heads * count, BLOCK), ones, precision=highest
    ).reshape(heads, count, BLOCK)
    decay = jnp.exp(jnp.sum(running[:, :, BLOCK - 1], axis=1))
    decay = jnp.broadcast_to(decay[:, None], (heads, LANES)).reshape(n_seq, group, 1, LANES)

    tokens = pl.BlockSpec((length, head_dim), lambda h: (0, h))
    run_spec = pl.BlockSpec((1, count, BLOCK), lambda h: (h, 0, 0))
    mix_spec = pl.BlockSpec((count, BLOCK, BLOCK), lambda h: (0, 0, 0))
    state_spec = pl.BlockSpec((1, count, state_dim, head_dim), lambda h: (h, 0, 0, 0))
    far_spec = pl.BlockSpec(
        (1, 2, 1, state_dim, head_dim), lambda h: (h // group, 0, h % group, 0, 0)
    )
    b_spec = pl.BlockSpec((length, state_dim), lambda h: (0, 0))
    c_spec = pl.BlockSpec((length, state_dim), lambda h: (0, 1))
    far_shape = (n_seq, 2, group, state_dim, head_dim)

    w_shape = (own_rows, 2 * state_dim)
    mixing, w_all = pl.pallas_call(
        functools.partial(mixing_kernel, count, n_seq, n_opt),
        grid=(heads,),
        in_specs=[whole(), tokens, tokens, run_spec],
        out_specs=[mix_spec, whole()],
        out_shape=[
            jax.ShapeDtypeStruct((count, BLOCK, BLOCK), f32),
            jax.ShapeDtypeStruct((n_seq, n_opt) + w_shape, bf16),
        ],
        scratch_shapes=[pltpu.VMEM((n_opt, n_seq) + w_shape, bf16)] + dma(n_seq, n_opt),
        compiler_params=params(collective_id=2, has_side_effects=True),
        name="gather_and_mixing",
    )(w_bc.astype(bf16), x, dy, running)
    w_all = w_all.reshape(width, 2 * state_dim)

    proj = jnp.dot(layer_rows, w_all, preferred_element_type=f32).astype(bf16)

    sent, starts, outs = pl.pallas_call(
        functools.partial(local_kernel, count),
        grid=(heads,),
        in_specs=[tokens, tokens, b_spec, c_spec, run_spec],
        out_specs=[far_spec, state_spec, state_spec],
        out_shape=[
            jax.ShapeDtypeStruct(far_shape, bf16),
            jax.ShapeDtypeStruct((heads, count, state_dim, head_dim), bf16),
            jax.ShapeDtypeStruct((heads, count, state_dim, head_dim), bf16),
        ],
        scratch_shapes=[pltpu.VMEM((state_dim, length), f32)] * 2,
        compiler_params=params(),
        name="local_states",
    )(x, dy, proj, proj, running)

    far = pl.pallas_call(
        functools.partial(carry_kernel, n_seq),
        in_specs=[whole(), whole()],
        out_specs=whole(),
        out_shape=jax.ShapeDtypeStruct(far_shape, bf16),
        scratch_shapes=[
            pltpu.VMEM(far_shape, bf16),
            pltpu.VMEM((n_seq, group, 1, LANES), f32),
            pltpu.VMEM(far_shape, bf16),
            pltpu.VMEM(far_shape, bf16),
            pltpu.VMEM(far_shape[1:], f32),
        ]
        + dma(n_seq, n_seq, n_seq),
        compiler_params=params(collective_id=0, has_side_effects=True),
        name="carry_states",
    )(sent, decay)

    grad_input, grad_bc = pl.pallas_call(
        functools.partial(grads_kernel, count),
        grid=(heads,),
        in_specs=[
            pl.BlockSpec(memory_space=pltpu.SMEM), tokens, tokens, b_spec, c_spec, run_spec,
            state_spec, state_spec, far_spec, mix_spec,
        ],
        out_specs=[tokens, pl.BlockSpec((length, 2 * state_dim), lambda h: (0, 0))],
        out_shape=[
            jax.ShapeDtypeStruct(x.shape, bf16),
            jax.ShapeDtypeStruct((length, 2 * state_dim), bf16),
        ],
        scratch_shapes=[
            pltpu.VMEM((count, BLOCK, BLOCK), f32),
            pltpu.VMEM((length, state_dim), f32),
            pltpu.VMEM((length, state_dim), f32),
        ],
        compiler_params=params(),
        name="grads",
    )(skip_gain, x, dy, proj, proj, running, starts, outs, far, mixing)

    cols = 2 * state_dim
    part = lax.dot_general(
        layer_rows, grad_bc, (((0,), (0,)), ((), ())), preferred_element_type=f32
    ).astype(bf16)
    part = jnp.transpose(part.reshape(n_seq, n_opt, own_rows, cols), (1, 0, 2, 3))

    n = n_seq * n_opt
    update, code_next, scale_next, row_next, col_next = pl.pallas_call(
        functools.partial(step_kernel, n_seq, n_opt),
        in_specs=[whole()] * 6,
        out_specs=[whole()] * 5,
        out_shape=[
            jax.ShapeDtypeStruct((own_rows, cols), f32),
            jax.ShapeDtypeStruct((own_rows, cols), bf16),
            jax.ShapeDtypeStruct((1, cols), f32),
            jax.ShapeDtypeStruct((own_rows, 1), f32),
            jax.ShapeDtypeStruct((1, cols), f32),
        ],
        scratch_shapes=[
            pltpu.VMEM((n_opt, n_seq, own_rows, cols), bf16),
            pltpu.VMEM((n_seq, own_rows, cols), bf16),
            pltpu.VMEM((n_seq, own_rows, cols), bf16),
            pltpu.VMEM((1, cols + LANES), f32),
            pltpu.VMEM((n, 1, cols + LANES), f32),
            pltpu.VMEM((1, cols), f32),
            pltpu.VMEM((n, 1, cols), f32),
        ]
        + dma(n_opt, n_seq, n, n),
        compiler_params=params(collective_id=1, has_side_effects=True),
        name="sum_and_step",
    )(part, w_bc, m_code, m_scale[None, :], row_stat[:, None], col_stat[None, :])
    return (grad_input[None], update, code_next, scale_next[0], row_next[:, 0], col_next[0])


def solution(mesh):
    return jax.shard_map(
        functools.partial(per_device, mesh.shape["seq"], mesh.shape["opt"]),
        mesh=mesh,
        in_specs=(
            P("opt", "seq", None),
            P("opt", "seq", None),
            P("opt", "seq", None),
            P("opt", None, "seq"),
            P(),
            P(("seq", "opt"), None),
            P(("seq", "opt"), None),
            P(),
            P(("seq", "opt")),
            P(),
        ),
        out_specs=(
            P("opt", "seq", None),
            P(("seq", "opt"), None),
            P(("seq", "opt"), None),
            P(),
            P(("seq", "opt")),
            P(),
        ),
        check_vma=False,
    )
```

profile of v0, /device:TPU:0, one launch (start us, length us, event | category | flops | bytes accessed | tf_op | source)
XLA Modules:
  0.0 283.8 jit_solution(8944640571909554380)
XLA Ops:
  0.6 0.9 reshape_squeeze.3
  1.5 0.2 convolution_bitcast_fusion
  1.7 0.7 reshape.32.run_ref
  2.4 1.5 convert_element_type.15.w_ref
  3.9 42.2 %gather_and_mixing.1 = (f32[2,256,256]{2,1,0:T(8,128)}, bf16[8,4,128,256]{3,2,1,0:T(8,128)(2,1)}) custom-call(bf16[128,256]{1,0:T(8,128)(2,1)} %convert_element_type.15.w_ref, bf16[512,4096]{1,0:T(8,128)(2,1)} %bitcast.31, bf16[512,4096]{1,0:T(8,128)(2,1)} %bitcast.34, f32[32,2,256]{2,1,0:T(2,128)} %reshape.32.run_ref), custom_call_target="tpu_custom_call" | custom-call | tf_op jit(solution)/shard_map/gather_and_mixing/pallas_call | solution.py:404
  46.1 4.9 %fusion.7.b_ref.c_ref = bf16[512,256]{1,0:T(8,128)(2,1)} fusion(bf16[4096,256]{1,0:T(8,128)(2,1)} %bitcast.45, bf16[1,512,4096]{2,1,0:T(8,128)(2,1)} %param.10), kind=kOutput, calls=%fused_computation.7 | convolution fusion | flops 1073872896 | bytes 6553600 | tf_op jit(solution)/shard_map/dot_general | solution.py:419
  50.9 23.3 %local_states.1 = (bf16[8,2,4,128,128]{4,3,2,1,0:T(8,128)(2,1)}, bf16[32,2,128,128]{3,2,1,0:T(8,128)(2,1)}, bf16[32,2,128,128]{3,2,1,0:T(8,128)(2,1)}) custom-call(bf16[512,4096]{1,0:T(8,128)(2,1)} %bitcast.32, bf16[512,4096]{1,0:T(8,128)(2,1)} %bitcast.35, bf16[512,256]{1,0:T(8,128)(2,1)} %fusion.7.b_ref.c_ref, bf16[512,256]{1,0:T(8,128)(2,1)} %fusion.7.b_ref.c_ref, ...), custom_call_target="tpu_custom_call" | custom-call | tf_op jit(solution)/shard_map/local_states/pallas_call | solution.py:421
  74.2 0.0 copy-done
  74.2 0.5 slice_reduce_fusion
  74.7 0.1 exp.11
  74.8 0.7 broadcast_in_dim.18.decay_ref
  75.5 97.4 %carry_states.1.far_ref = bf16[8,2,4,128,128]{4,3,2,1,0:T(8,128)(2,1)} custom-call(bf16[8,2,4,128,128]{4,3,2,1,0:T(8,128)(2,1)} %get-tuple-element.21.send_ref, f32[8,4,1,128]{3,2,1,0:T(1,128)} %broadcast_in_dim.18.decay_ref), custom_call_target="tpu_custom_call" | custom-call | tf_op jit(solution)/shard_map/carry_states/pallas_call | solution.py:436
  172.9 27.7 %grads.1 = (bf16[512,4096]{1,0:T(8,128)(2,1)}, bf16[512,256]{1,0:T(8,128)(2,1)}) custom-call(f32[32]{0:T(128)} %skip_ref.1, bf16[512,4096]{1,0:T(8,128)(2,1)} %bitcast.33, bf16[512,4096]{1,0:T(8,128)(2,1)} %bitcast.36, bf16[512,256]{1,0:T(8,128)(2,1)} %fusion.7.b_ref.c_ref, bf16[512,256]{1,0:T(8,128)(2,1)} %fusion.7.b_ref.c_ref, ...), custom_call_target="tpu_custom_call" | custom-call | tf_op jit(solution)/shard_map/grads/pallas_call | solution.py:453
  200.6 3.6 %fusion = bf16[4096,256]{0,1:T(8,128)(2,1)S(1)} fusion(bf16[512,256]{1,0:T(8,128)(2,1)} %get-tuple-element.24, bf16[1,512,4096]{2,1,0:T(8,128)(2,1)} %param.10), kind=kOutput, calls=%fused_computation.1 | convolution fusion | flops 1074790400 | bytes 6553600 | tf_op jit(solution)/shard_map/dot_general | solution.py:475
  204.2 2.5 copy.19
  206.7 3.2 %copy.24 = bf16[8,4,128,256]{3,2,0,1:T(8,128)(2,1)} copy(bf16[8,4,128,256]{3,2,1,0:T(8,128)(2,1)} %bitcast.38) | data formatting | bytes 4194304 | tf_op jit(solution)/shard_map/reshape | solution.py:478
  209.9 0.0 copy-done.1
  209.9 0.7 copy.21.row_ref
  210.6 66.2 %sum_and_step.1 = (f32[128,256]{1,0:T(8,128)}, bf16[128,256]{1,0:T(8,128)(2,1)}, f32[1,256]{1,0:T(1,128)}, f32[128,1]{1,0:T(8,128)}, f32[1,256]{1,0:T(1,128)}) custom-call(bf16[4,8,128,256]{3,2,1,0:T(8,128)(2,1)} %bitcast.37, f32[128,256]{1,0:T(8,128)} %w_ref.1, bf16[128,256]{1,0:T(8,128)(2,1)} %code_ref.1, f32[1,256]{1,0:T(1,128)} %bitcast.39, ...), custom_call_target="tpu_custom_call" | custom-call | tf_op jit(solution)/shard_map/sum_and_step/pallas_call | solution.py:481
  276.8 1.5 reduce.1
  278.3 1.6 copy.29
  279.9 1.5 copy.30
  281.4 1.2 copy.31
  282.6 1.2 copy.32
  (3 shorter events, 0.0 us)
Async XLA Ops:
  50.9 23.3 %copy-start = (f32[32,2,256]{2,1,0:T(2,128)S(1)}, f32[32,2,256]{2,1,0:T(2,128)}, u32[]{:S(2)}) copy-start(f32[32,2,256]{2,1,0:T(2,128)} %reshape.32.run_ref) | copy-start | bytes 196612
  206.7 3.2 %copy-start.1 = (f32[128]{0:T(128)S(1)}, f32[128]{0:T(128)}, u32[]{:S(2)}) copy-start(f32[128]{0:T(128)} %param.18) | copy-start | bytes 1540
where the time goes:
time: 286 us; the launch traced here: 284 us
  Pallas kernels  257 us (90%)
  local copies, waits for them, and re-layouts  14.3 us (5%)
  matrix products  8.62 us (3%)
  other arithmetic  3.48 us (1%)
    pallas_call x1, Pallas kernels, per_device(): pl.pallas_call(functools.partial(carry_kernel, n_seq), in_specs=[whole(),...  97.4 us
    pallas_call x1, Pallas kernels, per_device(): pl.pallas_call(functools.partial(step_kernel, n_seq, n_opt), in_specs=[wh...  66.2 us
    pallas_call x1, Pallas kernels, per_device(): pl.pallas_call(functools.partial(mixing_kernel, count, n_seq, n_opt), gri...  42.2 us
    pallas_call x1, Pallas kernels, per_device(): pl.pallas_call(functools.partial(grads_kernel, count), grid=(heads,), in_...  27.7 us
    pallas_call x1, Pallas kernels, per_device(): pl.pallas_call(functools.partial(local_kernel, count), grid=(heads,), in_...  23.3 us

commit v1 on v0

--- a/solution.py
+++ b/solution.py
@@ -9,6 +9,8 @@
 
 BLOCK = 256
 LANES = 128
+LAG_SWAP = 3
+LAG_CHAIN = 2
 
 beta_one = 0.9
 beta_two = 0.95
@@ -99,84 +101,199 @@
         lax.fori_loop(0, n_seq, place, 0)
 
 
-def local_kernel(
-    count, x_ref, dy_ref, b_ref, c_ref, run_ref, send_ref, starts_ref, outs_ref, b_turned, c_turned
+def remote(src, dst, send_sem, recv_sem, device):
+    return pltpu.make_async_remote_copy(
+        src_ref=src, dst_ref=dst, send_sem=send_sem, recv_sem=recv_sem,
+        device_id=device, device_id_type=MESH,
+    )
+
+
+def states_kernel(
+    count, heads, n_pairs, skip_ref, x_ref, dy_ref, x_far, dy_far, b_ref, c_ref, run_ref, mix_ref,
+    gx_ref, gbc_ref,
+    b_turned, c_turned, affinity, acc_b, acc_c, starts, outs, mine, got, chain_in, chain_out,
+    decay, decay_far, send_d, recv_d, send_y, recv_y, send_c, recv_c,
 ):
-    @pl.when(pl.program_id(0) == 0)
-    def _():
+    i = pl.program_id(0)
+    seq = lax.axis_index("seq")
+    opt = lax.axis_index("opt")
+    pair = seq // 2
+    side = lax.rem(seq, 2)
+    lag = LAG_SWAP + LAG_CHAIN * (n_pairs - 1)
+    state_dim = b_ref.shape[1]
+    twin = (seq + 1 - 2 * side, opt)
+    ahead = (seq + 2, opt)
+    behind = (seq - 2, opt)
+
+    def closings_of(h):
+        return [run_ref[h, b : b + 1, BLOCK - 1 : BLOCK] for b in range(count)]
+
+    def swap(h):
+        return remote(mine.at[h], got.at[h], send_y.at[h], recv_y.at[h], twin)
+
+    def swap_decay():
+        return remote(decay, decay_far, send_d, recv_d, twin)
+
+    def pass_on(way, h):
+        return remote(
+            chain_out.at[way, h], chain_in.at[way, h], send_c.at[way, h], recv_c.at[way, h],
+            (ahead, behind)[way],
+        )
+
+    has_source = (pair > 0, pair < n_pairs - 1)
+    has_target = (pair < n_pairs - 1, pair > 0)
+
+    @pl.when(i == 0)
+    def _():
+        barrier = pltpu.get_barrier_semaphore()
+        pl.semaphore_signal(barrier, inc=1, device_id=twin, device_id_type=MESH)
+        for way in range(2):
+            @pl.when(has_target[way])
+            def _():
+                pl.semaphore_signal(
+                    barrier, inc=1, device_id=(ahead, behind)[way], device_id_type=MESH
+                )
+
+        def decay_of(h, carry):
+            total = sum(closings_of(h), jnp.zeros((1, 1), f32))
+            decay[h] = jnp.broadcast_to(jnp.exp(total), (1, LANES))
+            return carry
+
+        lax.fori_loop(0, heads, decay_of, 0)
+        acc_b[...] = jnp.zeros_like(acc_b)
+        acc_c[...] = jnp.zeros_like(acc_c)
         b_turned[...] = jnp.transpose(b_ref[...].astype(f32))
         c_turned[...] = jnp.transpose(c_ref[...].astype(f32))
-
-    adds = []
-    for b in range(count):
-        rows = slice(b * BLOCK, (b + 1) * BLOCK)
-        row = run_ref[0, b : b + 1, :]
-        closing = row[:, BLOCK - 1 : BLOCK]
-        b_scaled = (b_turned[:, rows] * jnp.exp(closing - row)).astype(bf16)
-        c_scaled = (c_turned[:, rows] * jnp.exp(row)).astype(bf16)
-        adds.append(
-            (jnp.exp(closing), dot_nn(b_scaled, x_ref[rows, :]), dot_nn(c_scaled, dy_ref[rows, :]))
-        )
-    state = None
-    for b in range(count):
-        starts_ref[0, b] = (jnp.zeros_like(adds[b][1]) if state is None else state).astype(bf16)
-        state = adds[b][1] if state is None else adds[b][0] * state + adds[b][1]
-    send_ref[0, 0, 0] = state.astype(bf16)
-    carried = None
-    for b in reversed(range(count)):
-        outs_ref[0, b] = (jnp.zeros_like(adds[b][2]) if carried is None else carried).astype(bf16)
-        carried = adds[b][2] if carried is None else adds[b][0] * carried + adds[b][2]
-    send_ref[0, 1, 0] = carried.astype(bf16)
-
-
-def grads_kernel(
-    count, skip_ref, x_ref, dy_ref, b_ref, c_ref, run_ref, starts_ref, outs_ref, far_ref, mix_ref,
-    gx_ref, gbc_ref, affinity, acc_b, acc_c,
-):
-    h = pl.program_id(0)
-    state_dim = b_ref.shape[1]
-
-    @pl.when(h == 0)
-    def _():
-        acc_b[...] = jnp.zeros_like(acc_b)
-        acc_c[...] = jnp.zeros_like(acc_c)
         for b in range(count):
             rows = slice(b * BLOCK, (b + 1) * BLOCK)
             affinity[b] = dot_nt(b_ref[rows, :], c_ref[rows, :])
-
-    row_pos = lax.broadcasted_iota(jnp.int32, (BLOCK, BLOCK), 0)
-    col_pos = lax.broadcasted_iota(jnp.int32, (BLOCK, BLOCK), 1)
-    closings = [run_ref[0, b : b + 1, BLOCK - 1 : BLOCK] for b in range(count)]
-    for b in range(count):
-        rows = slice(b * BLOCK, (b + 1) * BLOCK)
-        row = run_ref[0, b : b + 1, :]
-        column = as_column(row)
-        before = sum(closings[:b], jnp.zeros((1, 1), f32))
-        after = sum(closings[b + 1 :], jnp.zeros((1, 1), f32))
-        far_state = far_ref[0, 0, 0].astype(f32)
-        far_grad = far_ref[0, 1, 0].astype(f32)
-        state_in = (starts_ref[0, b].astype(f32) + jnp.exp(before) * far_state).astype(bf16)
-        grad_in = (outs_ref[0, b].astype(f32) + jnp.exp(after) * far_grad).astype(bf16)
-        grow = jnp.exp(column)
-        shrink = jnp.exp(closings[b] - column)
-        x_blk = x_ref[rows, :]
-        dy_blk = dy_ref[rows, :]
-        spread = row - widened(column, BLOCK)
-        decays = jnp.exp(jnp.where(col_pos >= row_pos, spread, -jnp.inf))
-        weighted = (decays * affinity[b]).astype(bf16)
-        inner = dot_nn(weighted, dy_blk)
-        outer = dot_nn(b_ref[rows, :], grad_in) * shrink
-        gx_ref[rows, :] = (inner + outer + skip_ref[h] * dy_blk.astype(f32)).astype(bf16)
-        acc_c[rows, :] += grow * dot_nt(dy_blk, state_in)
-        acc_b[rows, :] += shrink * dot_nt(x_blk, grad_in)
-
-    @pl.when(h == pl.num_programs(0) - 1)
+        for way in range(2):
+            @pl.when(jnp.logical_not(has_source[way]))
+            def _():
+                chain_in[way] = jnp.zeros_like(chain_in[way])
+        neighbours = 1 + (pair > 0).astype(jnp.int32) + (pair < n_pairs - 1).astype(jnp.int32)
+        pl.semaphore_wait(barrier, neighbours)
+        swap_decay().start()
+
+    @pl.when(i < heads)
+    def _():
+        h = i
+        adds = []
+        for b in range(count):
+            rows = slice(b * BLOCK, (b + 1) * BLOCK)
+            row = run_ref[h, b : b + 1, :]
+            closing = row[:, BLOCK - 1 : BLOCK]
+            b_scaled = (b_turned[:, rows] * jnp.exp(closing - row)).astype(bf16)
+            c_scaled = (c_turned[:, rows] * jnp.exp(row)).astype(bf16)
+            adds.append(
+                (jnp.exp(closing), dot_nn(b_scaled, x_ref[rows, :]), dot_nn(c_scaled, dy_ref[rows, :]))
+            )
+        state = adds[0][1]
+        for b in range(1, count):
+            starts[h, b - 1] = state.astype(bf16)
+            state = adds[b][0] * state + adds[b][1]
+        mine[h, 0] = state.astype(bf16)
+        carried = adds[count - 1][2]
+        for b in reversed(range(count - 1)):
+            outs[h, b] = carried.astype(bf16)
+            carried = adds[b][0] * carried + adds[b][2]
+        mine[h, 1] = carried.astype(bf16)
+        swap(h).start()
+
+    @pl.when(i == LAG_SWAP)
+    def _():
+        swap_decay().wait_recv()
+
+    j = i - LAG_SWAP
+
+    @pl.when(jnp.logical_and(j >= 0, j < heads))
+    def _():
+        swap(j).wait_recv()
+
+    for way in range(2):
+        place = pair if way == 0 else n_pairs - 1 - pair
+        hop = j - LAG_CHAIN * place
+
+        @pl.when(jnp.logical_and(hop >= 0, hop < heads))
+        def _():
+            @pl.when(has_source[way])
+            def _():
+                pass_on(way, hop).wait_recv()
+
+            @pl.when(has_target[way])
+            def _():
+                own_decay = decay[hop]
+                other_decay = decay_far[hop]
+                first = side == way
+                own_scale = jnp.where(first, other_decay, 1.0)
+                other_scale = jnp.where(first, 1.0, own_decay)
+                total = (
+                    own_decay * other_decay * chain_in[way, hop].astype(f32)
+                    + own_scale * mine[hop, way].astype(f32)
+                    + other_scale * got[hop, way].astype(f32)
+                )
+                chain_out[way, hop] = total.astype(bf16)
+                pass_on(way, hop).start()
+
+    @pl.when(i >= lag)
+    def _():
+        h = i - lag
+        row_pos = lax.broadcasted_iota(jnp.int32, (BLOCK, BLOCK), 0)
+        col_pos = lax.broadcasted_iota(jnp.int32, (BLOCK, BLOCK), 1)
+        closings = closings_of(h)
+        other_decay = decay_far[h]
+        fars = []
+        for way in range(2):
+            second = side != way
+            scale = jnp.where(second, other_decay, 1.0)
+            extra = jnp.where(second, jnp.ones((1, LANES), f32), 0.0)
+            fars.append(scale * chain_in[way, h].astype(f32) + extra * got[h, way].astype(f32))
+        far_state, far_grad = fars
+        for b in range(count):
+            rows = slice(b * BLOCK, (b + 1) * BLOCK)
+            row = run_ref[h, b : b + 1, :]
+            column = as_column(row)
+            before = sum(closings[:b], jnp.zeros((1, 1), f32))
+            after = sum(closings[b + 1 :], jnp.zeros((1, 1), f32))
+            if b == 0:
+                state_in = far_state.astype(bf16)
+            else:
+                state_in = (starts[h, b - 1].astype(f32) + jnp.exp(before) * far_state).astype(bf16)
+            if b == count - 1:
+                grad_in = far_grad.astype(bf16)
+            else:
+                grad_in = (outs[h, b].astype(f32) + jnp.exp(after) * far_grad).astype(bf16)
+            grow = jnp.exp(column)
+            shrink = jnp.exp(closings[b] - column)
+            x_blk = x_far[rows, :]
+            dy_blk = dy_far[rows, :]
+            spread = row - widened(column, BLOCK)
+            decays = jnp.exp(jnp.where(col_pos >= row_pos, spread, -jnp.inf))
+            weighted = (decays * affinity[b]).astype(bf16)
+            inner = dot_nn(weighted, dy_blk)
+            outer = dot_nn(b_ref[rows, :], grad_in) * shrink
+            gx_ref[rows, :] = (inner + outer + skip_ref[h] * dy_blk.astype(f32)).astype(bf16)
+            acc_c[rows, :] += grow * dot_nt(dy_blk, state_in)
+            acc_b[rows, :] += shrink * dot_nt(x_blk, grad_in)
+
+    @pl.when(i == pl.num_programs(0) - 1)
     def _():
         for b in range(count):
             rows = slice(b * BLOCK, (b + 1) * BLOCK)
             mixing = mix_ref[b].astype(bf16)
             gbc_ref[rows, :state_dim] = (acc_b[rows, :] + dot_tn(mixing, c_ref[rows, :])).astype(bf16)
             gbc_ref[rows, state_dim:] = (acc_c[rows, :] + dot_nn(mixing, b_ref[rows, :])).astype(bf16)
+        swap_decay().wait_send()
+
+        def sent(h, carry):
+            swap(h).wait_send()
+            for way in range(2):
+                @pl.when(has_target[way])
+                def _():
+                    pass_on(way, h).wait_send()
+            return carry
+
+        lax.fori_loop(0, heads, sent, 0)
 
 
 def swap_all(n, me, src_of, dst_of, device_of, send_sem, recv_sem):
@@ -223,48 +340,6 @@
 
     lax.fori_loop(1, n, signal, 0)
     pl.semaphore_wait(barrier, n - 1)
-
-
-def carry_kernel(
-    n, send_ref, decay_ref, out_ref, got, got_decay, prefix, landed, run,
-    send_a, recv_a, send_d, recv_d, send_b, recv_b,
-):
-    me = lax.axis_index("seq")
-    opt = lax.axis_index("opt")
-
-    def device_of(s):
-        return (s, opt)
-
-    greet(n, me, device_of)
-    end_d = begin_swap(
-        n, me, lambda s: decay_ref.at[s], lambda s: got_decay.at[s], device_of, send_d, recv_d
-    )
-    end_a = begin_swap(n, me, lambda s: send_ref.at[s], lambda s: got.at[s], device_of, send_a, recv_a)
-    end_d()
-    end_a()
-    got[me] = send_ref[me]
-    got_decay[me] = decay_ref[me]
-
-    run[...] = jnp.zeros_like(run)
-
-    def forward(s, carry):
-        state = run[0]
-        prefix[s, 0] = state.astype(bf16)
-        run[0] = got_decay[s] * state + got[s, 0].astype(f32)
-        return carry
-
-    def backward(lap, carry):
-        s = n - 1 - lap
-        state = run[1]
-        prefix[s, 1] = state.astype(bf16)
-        run[1] = got_decay[s] * state + got[s, 1].astype(f32)
-        return carry
-
-    lax.fori_loop(0, n, forward, 0)
-    lax.fori_loop(0, n, backward, 0)
-    begin_swap(n, me, lambda s: prefix.at[s], lambda s: landed.at[s], device_of, send_b, recv_b)()
-    landed[me] = prefix[me]
-    out_ref[...] = landed[...]
 
 
 def step_kernel(
@@ -376,7 +451,7 @@
     head_dim = x.shape[1] // heads
     state_dim = w_bc.shape[1] // 2
     count = length // BLOCK
-    group = heads // n_seq
+    n_pairs = n_seq // 2
     own_rows = w_bc.shape[0]
 
     ones = (
@@ -386,19 +461,11 @@
     running = jnp.dot(
         log_decay[0].reshape(heads * count, BLOCK), ones, precision=highest
     ).reshape(heads, count, BLOCK)
-    decay = jnp.exp(jnp.sum(running[:, :, BLOCK - 1], axis=1))
-    decay = jnp.broadcast_to(decay[:, None], (heads, LANES)).reshape(n_seq, group, 1, LANES)
-
     tokens = pl.BlockSpec((length, head_dim), lambda h: (0, h))
     run_spec = pl.BlockSpec((1, count, BLOCK), lambda h: (h, 0, 0))
     mix_spec = pl.BlockSpec((count, BLOCK, BLOCK), lambda h: (0, 0, 0))
-    state_spec = pl.BlockSpec((1, count, state_dim, head_dim), lambda h: (h, 0, 0, 0))
-    far_spec = pl.BlockSpec(
-        (1, 2, 1, state_dim, head_dim), lambda h: (h // group, 0, h % group, 0, 0)
-    )
     b_spec = pl.BlockSpec((length, state_dim), lambda h: (0, 0))
     c_spec = pl.BlockSpec((length, state_dim), lambda h: (0, 1))
-    far_shape = (n_seq, 2, group, state_dim, head_dim)
 
     w_shape = (own_rows, 2 * state_dim)
     mixing, w_all = pl.pallas_call(
@@ -418,58 +485,48 @@
 
     proj = jnp.dot(layer_rows, w_all, preferred_element_type=f32).astype(bf16)
 
-    sent, starts, outs = pl.pallas_call(
-        functools.partial(local_kernel, count),
-        grid=(heads,),
-        in_specs=[tokens, tokens, b_spec, c_spec, run_spec],
-        out_specs=[far_spec, state_spec, state_spec],
-        out_shape=[
-            jax.ShapeDtypeStruct(far_shape, bf16),
-            jax.ShapeDtypeStruct((heads, count, state_dim, head_dim), bf16),
-            jax.ShapeDtypeStruct((heads, count, state_dim, head_dim), bf16),
+    lag = LAG_SWAP + LAG_CHAIN * (n_pairs - 1)
+    near = pl.BlockSpec((length, head_dim), lambda i: (0, jnp.minimum(i, heads - 1)))
+    late = pl.BlockSpec((length, head_dim), lambda i: (0, jnp.maximum(i - lag, 0)))
+    all_run = pl.BlockSpec((heads, count, BLOCK), lambda i: (0, 0, 0))
+    per_head = (heads, 2, state_dim, head_dim)
+    per_way = (2, heads, state_dim, head_dim)
+    grad_input, grad_bc = pl.pallas_call(
+        functools.partial(states_kernel, count, heads, n_pairs),
+        grid=(heads + lag,),
+        in_specs=[
+            pl.BlockSpec(memory_space=pltpu.SMEM), near, near, late, late, b_spec, c_spec, all_run,
+            mix_spec,
         ],
-        scratch_shapes=[pltpu.VMEM((state_dim, length), f32)] * 2,
-        compiler_params=params(),
-        name="local_states",
-    )(x, dy, proj, proj, running)
-
-    far = pl.pallas_call(
-        functools.partial(carry_kernel, n_seq),
-        in_specs=[whole(), whole()],
-        out_specs=whole(),
-        out_shape=jax.ShapeDtypeStruct(far_shape, bf16),
-        scratch_shapes=[
-            pltpu.VMEM(far_shape, bf16),
-            pltpu.VMEM((n_seq, group, 1, LANES), f32),
-            pltpu.VMEM(far_shape, bf16),
-            pltpu.VMEM(far_shape, bf16),
-            pltpu.VMEM(far_shape[1:], f32),
-        ]
-        + dma(n_seq, n_seq, n_seq),
-        compiler_params=params(collective_id=0, has_side_effects=True),
-        name="carry_states",
-    )(sent, decay)
-
-    grad_input, grad_bc = pl.pallas_call(
-        functools.partial(grads_kernel, count),
-        grid=(heads,),
-        in_specs=[
-            pl.BlockSpec(memory_space=pltpu.SMEM), tokens, tokens, b_spec, c_spec, run_spec,
-            state_spec, state_spec, far_spec, mix_spec,
-        ],
-        out_specs=[tokens, pl.BlockSpec((length, 2 * state_dim), lambda h: (0, 0))],
+        out_specs=[late, pl.BlockSpec((length, 2 * state_dim), lambda h: (0, 0))],
         out_shape=[
             jax.ShapeDtypeStruct(x.shape, bf16),
             jax.ShapeDtypeStruct((length, 2 * state_dim), bf16),
         ],
         scratch_shapes=[
+            pltpu.VMEM((state_dim, length), f32),
+            pltpu.VMEM((state_dim, length), f32),
             pltpu.VMEM((count, BLOCK, BLOCK), f32),
             pltpu.VMEM((length, state_dim), f32),
             pltpu.VMEM((length, state_dim), f32),
+            pltpu.VMEM((heads, max(count - 1, 1), state_dim, head_dim), bf16),
+            pltpu.VMEM((heads, max(count - 1, 1), state_dim, head_dim), bf16),
+            pltpu.VMEM(per_head, bf16),
+            pltpu.VMEM(per_head, bf16),
+            pltpu.VMEM(per_way, bf16),
+            pltpu.VMEM(per_way, bf16),
+            pltpu.VMEM((heads, 1, LANES), f32),
+            pltpu.VMEM((heads, 1, LANES), f32),
+            pltpu.SemaphoreType.DMA,
+            pltpu.SemaphoreType.DMA,
+            pltpu.SemaphoreType.DMA((heads,)),
+            pltpu.SemaphoreType.DMA((heads,)),
+            pltpu.SemaphoreType.DMA((2, heads)),
+            pltpu.SemaphoreType.DMA((2, heads)),
         ],
-        compiler_params=params(),
-        name="grads",
-    )(skip_gain, x, dy, proj, proj, running, starts, outs, far, mixing)
+        compiler_params=params(collective_id=0, has_side_effects=True),
+        name="states_and_grads",
+    )(skip_gain, x, dy, x, dy, proj, proj, running, mixing)
 
     cols = 2 * state_dim
     part = lax.dot_general(

time: 286 us -> 191 us (0.67)
  Pallas kernels: 257 us -> 163 us
    pallas_call x3 -> x1, Pallas kernels: 148 us -> 69.6 us  [per_device(): pl.pallas_call(functools.partial(states_kernel, count, heads, n_pairs), g...]
    pallas_call x1, Pallas kernels: 66.2 us -> 51.5 us  [per_device(): pl.pallas_call(functools.partial(step_kernel, n_seq, n_opt), in_specs=[wh...]
    unnamed x8 -> x15, local copies, waits for them, and re-layouts: 5.52 us -> 7.17 us
where the time goes in v1:
time: 191 us
  Pallas kernels  163 us (85%)
  local copies, waits for them, and re-layouts  15 us (8%)
  matrix products  8.59 us (4%)
  other arithmetic  3.01 us (2%)
    pallas_call x1, Pallas kernels, per_device(): pl.pallas_call(functools.partial(states_kernel, count, heads, n_pairs), g...  69.6 us
    pallas_call x1, Pallas kernels, per_device(): pl.pallas_call(functools.partial(step_kernel, n_seq, n_opt), in_specs=[wh...  51.5 us
    pallas_call x1, Pallas kernels, per_device(): pl.pallas_call(functools.partial(mixing_kernel, count, n_seq, n_opt), gri...  42.1 us
    unnamed x15, local copies, waits for them, and re-layouts  7.17 us
    dot_general x1, matrix products, per_device(): proj = jnp.dot(layer_rows, w_all, preferred_element_type=f32).astype(bf16)  4.82 us

profile of v1, /device:TPU:0, one launch (start us, length us, event | category | flops | bytes accessed | tf_op | source)
XLA Modules:
  0.0 190.5 jit_solution(9038291968190994405)
XLA Ops:
  0.6 0.9 reshape_squeeze.3
  1.5 0.2 convolution_bitcast_fusion
  1.7 0.7 reshape.21.run_ref
  2.4 1.5 convert_element_type.15.w_ref
  3.9 42.1 %gather_and_mixing.1 = (f32[2,256,256]{2,1,0:T(8,128)}, bf16[8,4,128,256]{3,2,1,0:T(8,128)(2,1)}) custom-call(bf16[128,256]{1,0:T(8,128)(2,1)} %convert_element_type.15.w_ref, bf16[512,4096]{1,0:T(8,128)(2,1)} %bitcast.31, bf16[512,4096]{1,0:T(8,128)(2,1)} %bitcast.34, f32[32,2,256]{2,1,0:T(2,128)} %reshape.21.run_ref), custom_call_target="tpu_custom_call" | custom-call | tf_op jit(solution)/shard_map/gather_and_mixing/pallas_call | solution.py:471
  46.0 4.8 %fusion.7.b_ref.c_ref = bf16[512,256]{1,0:T(8,128)(2,1)} fusion(bf16[4096,256]{1,0:T(8,128)(2,1)} %bitcast.45, bf16[1,512,4096]{2,1,0:T(8,128)(2,1)} %param.10), kind=kOutput, calls=%fused_computation.7 | convolution fusion | flops 1073872896 | bytes 6553600 | tf_op jit(solution)/shard_map/dot_general | solution.py:486
  50.9 69.6 %states_and_grads.1 = (bf16[512,4096]{1,0:T(8,128)(2,1)}, bf16[512,256]{1,0:T(8,128)(2,1)}) custom-call(f32[32]{0:T(128)} %skip_ref.1, bf16[512,4096]{1,0:T(8,128)(2,1)} %bitcast.32, bf16[512,4096]{1,0:T(8,128)(2,1)} %bitcast.35, bf16[512,4096]{1,0:T(8,128)(2,1)} %bitcast.33, bf16[512,4096]{1,0:T(8,128)(2,1)} %bitcast.36, ...), custom_call_target="tpu_custom_call" | custom-call | tf_op jit(solution)/shard_map/states_and_grads/pallas_call | solution.py:494
  120.5 3.6 %fusion = bf16[4096,256]{0,1:T(8,128)(2,1)S(1)} fusion(bf16[512,256]{1,0:T(8,128)(2,1)} %get-tuple-element.18, bf16[1,512,4096]{2,1,0:T(8,128)(2,1)} %param.10), kind=kOutput, calls=%fused_computation.1 | convolution fusion | flops 1074790400 | bytes 6553600 | tf_op jit(solution)/shard_map/dot_general | solution.py:532
  124.0 0.0 copy-start.4
  124.1 2.5 %copy.19 = bf16[4096,256]{1,0:T(8,128)(2,1)} copy(bf16[4096,256]{0,1:T(8,128)(2,1)S(1)} %fusion) | data formatting | bytes 4194304 | tf_op jit(solution)/shard_map/convert_element_type | solution.py:534
  126.5 3.1 %copy.24 = bf16[8,4,128,256]{3,2,0,1:T(8,128)(2,1)} copy(bf16[8,4,128,256]{3,2,1,0:T(8,128)(2,1)} %bitcast.38) | data formatting | bytes 4194304 | tf_op jit(solution)/shard_map/reshape | solution.py:535
  129.6 0.0 copy-done.4
  129.7 0.7 copy.21.row_ref
  130.4 51.5 %sum_and_step.1 = (f32[128,256]{1,0:T(8,128)}, bf16[128,256]{1,0:T(8,128)(2,1)}, f32[1,256]{1,0:T(1,128)}, f32[128,1]{1,0:T(8,128)}, f32[1,256]{1,0:T(1,128)}) custom-call(bf16[4,8,128,256]{3,2,1,0:T(8,128)(2,1)} %bitcast.37, f32[128,256]{1,0:T(8,128)} %w_ref.1, bf16[128,256]{1,0:T(8,128)(2,1)} %code_ref.1, f32[1,256]{1,0:T(1,128)} %bitcast.40, ...), custom_call_target="tpu_custom_call" | custom-call | tf_op jit(solution)/shard_map/sum_and_step/pallas_call | solution.py:538
  181.9 1.5 reduce
  183.4 4.7 %copy.30 = bf16[1,512,4096]{2,1,0:T(8,128)(2,1)} copy(bf16[1,512,4096]{2,1,0:T(8,128)(2,1)} %bitcast.39) | data formatting | bytes 8388608
  188.1 0.0 copy-done
  188.1 0.7 copy.31
  188.8 0.0 copy-done.1
  188.8 0.6 copy.32
  189.4 0.0 copy-done.3
  189.4 0.6 copy.33
  190.0 0.0 copy-done.2
  190.0 0.6 copy.34
  (4 shorter events, 0.0 us)
Async XLA Ops:
  124.0 5.6 %copy-start.4 = (f32[128]{0:T(128)S(1)}, f32[128]{0:T(128)}, u32[]{:S(2)}) copy-start(f32[128]{0:T(128)} %param.18) | copy-start | bytes 1540
  183.4 4.7 %copy-start = (f32[128,256]{1,0:T(8,128)S(1)}, f32[128,256]{1,0:T(8,128)}, u32[]{:S(2)}) copy-start(f32[128,256]{1,0:T(8,128)} %get-tuple-element.31) | copy-start | bytes 393220
  183.4 5.4 %copy-start.1 = (bf16[128,256]{1,0:T(8,128)(2,1)S(1)}, bf16[128,256]{1,0:T(8,128)(2,1)}, u32[]{:S(2)}) copy-start(bf16[128,256]{1,0:T(8,128)(2,1)} %get-tuple-element.32) | copy-start | bytes 196612
  183.4 6.0 %copy-start.3 = (f32[1,256]{1,0:T(1,128)S(1)}, f32[1,256]{1,0:T(1,128)}, u32[]{:S(2)}) copy-start(f32[1,256]{1,0:T(1,128)} %get-tuple-element.21) | copy-start | bytes 3076
  183.4 6.6 %copy-start.2 = (f32[1,256]{1,0:T(1,128)S(1)}, f32[1,256]{1,0:T(1,128)}, u32[]{:S(2)}) copy-start(f32[1,256]{1,0:T(1,128)} %get-tuple-element.23) | copy-start | bytes 3076

commit v2 on v1

--- a/solution.py
+++ b/solution.py
@@ -11,6 +11,8 @@
 LANES = 128
 LAG_SWAP = 3
 LAG_CHAIN = 2
+STEP_B = 20
+STEP_C = 30
 
 beta_one = 0.9
 beta_two = 0.95
@@ -48,37 +50,87 @@
 
 
 def mixing_kernel(
-    count, n_seq, n_opt, w_ref, x_ref, dy_ref, run_ref, mix_ref, w_out,
-    got, send_a, recv_a, send_b, recv_b,
+    count, n_seq, n_opt, w_ref, layer_ref, x_ref, dy_ref, run_ref, mix_ref, proj_ref,
+    got, layer, load, send_a, recv_a, send_b, recv_b, send_c, recv_c, send_d, recv_d,
 ):
     seq = lax.axis_index("seq")
     opt = lax.axis_index("opt")
     h = pl.program_id(0)
     last = pl.num_programs(0) - 1
-
-    def over_seq():
+    n_pairs = n_seq // 2
+    pair, side, cross, core, twins = place_of(seq, opt)
+    core_twin, cross_twin, side_twin = twins
+    half = w_ref.shape[0] // 2
+    low, high = slice(0, half), slice(half, 2 * half)
+
+    def same(part, send_sem, recv_sem, k, device):
+        return remote(part, part, send_sem.at[k], recv_sem.at[k], device)
+
+    def along():
+        own = got.at[pair, side, cross, core]
         return swap_all(
-            n_seq, seq, lambda s: w_ref, lambda s: got.at[opt, s],
-            lambda s: (s, opt), send_a, recv_a,
+            n_pairs, pair, lambda p: own, lambda p: got.at[p, side, cross, core],
+            lambda p: (p * 2 + side, opt), send_a, recv_a,
         )
 
-    def over_opt():
-        return swap_all(
-            n_opt, opt, lambda o: got.at[opt], lambda o: got.at[o],
-            lambda o: (seq, o), send_b, recv_b,
+    def second():
+        return (
+            same(got.at[:, side, cross, core, low], send_b, recv_b, 0, side_twin),
+            same(got.at[:, side, cross, core, high], send_b, recv_b, 1, cross_twin),
         )
 
+    def third():
+        return (
+            same(got.at[:, :, cross, core, low], send_c, recv_c, 0, cross_twin),
+            same(got.at[:, side, :, core, high], send_c, recv_c, 1, side_twin),
+        )
+
+    def to_core(k):
+        parts = (
+            lambda: got.at[:, side, cross, core],
+            lambda: got.at[:, 1 - side, cross, core, low],
+            lambda: got.at[:, side, 1 - cross, core, high],
+            lambda: got.at[:, :, 1 - cross, core, low],
+            lambda: got.at[:, 1 - side, :, core, high],
+        )
+        return same(parts[k](), send_d, recv_d, k, core_twin)
+
+    def from_core(k):
+        parts = (
+            lambda: got.at[:, side, cross, 1 - core],
+            lambda: got.at[:, 1 - side, cross, 1 - core, low],
+            lambda: got.at[:, side, 1 - cross, 1 - core, high],
+            lambda: got.at[:, :, 1 - cross, 1 - core, low],
+            lambda: got.at[:, 1 - side, :, 1 - core, high],
+        )
+        return same(parts[k](), send_d, recv_d, k, core_twin)
+
+    def load_layer():
+        return pltpu.make_async_copy(layer_ref, layer, load)
+
     @pl.when(h == 0)
     def _():
-        greet(n_seq * n_opt, seq * n_opt + opt, lambda i: (i // n_opt, lax.rem(i, n_opt)))
-        over_seq()[0]()
-        got[opt, seq] = w_ref[...]
+        got[pair, side, cross, core] = w_ref[...].astype(bf16)
+        greet_twins(n_pairs, seq, opt)
+        along()[0]()
+        load_layer().start()
         mix_ref[...] = jnp.zeros_like(mix_ref)
 
-    @pl.when(h == last // 2)
-    def _():
-        over_seq()[1]()
-        over_opt()[0]()
+    @pl.when(h == last * STEP_B // 32)
+    def _():
+        along()[1]()
+        for copy in second():
+            copy.start()
+        to_core(0).start()
+
+    @pl.when(h == last * STEP_C // 32)
+    def _():
+        for copy in second():
+            copy.wait()
+        for copy in third():
+            copy.start()
+        to_core(1).start()
+        to_core(2).start()
 
     row_pos = lax.broadcasted_iota(jnp.int32, (BLOCK, BLOCK), 0)
     col_pos = lax.broadcasted_iota(jnp.int32, (BLOCK, BLOCK), 1)
@@ -91,14 +143,46 @@
 
     @pl.when(h == last)
     def _():
-        over_opt()[1]()
-
-        def place(s, carry):
-            for o in range(n_opt):
-                w_out[s, o] = got[o, s]
-            return carry
-
-        lax.fori_loop(0, n_seq, place, 0)
+        for copy in third():
+            copy.wait()
+        to_core(3).start()
+        to_core(4).start()
+        load_layer().wait()
+        for k in range(5):
+            to_core(k).wait_send()
+            from_core(k).wait_recv()
+        total = None
+        for p in range(n_pairs):
+            w_part = got[p].reshape(-1, got.shape[-1])
+            depth = w_part.shape[0]
+            term = dot_nn(layer[:, p * depth : (p + 1) * depth], w_part)
+            total = term if total is None else total + term
+        proj_ref[...] = total.astype(bf16)
+
+
+def place_of(seq, opt):
+    side, core, cross = lax.rem(seq, 2), lax.rem(opt, 2), opt // 2
+    twins = (
+        (seq, opt + 1 - 2 * core), (seq, opt + 2 - 4 * cross), (seq + 1 - 2 * side, opt)
+    )
+    return seq // 2, side, cross, core, twins
+
+
+def greet_twins(n_pairs, seq, opt):
+    barrier = pltpu.get_barrier_semaphore()
+    pair, side, cross, core, twins = place_of(seq, opt)
+
+    def hello(device):
+        pl.semaphore_signal(barrier, inc=1, device_id=device, device_id_type=MESH)
+
+    def hello_pair(distance, carry):
+        hello((lax.rem(pair + distance, n_pairs) * 2 + side, opt))
+        return carry
+
+    for device in twins:
+        hello(device)
+    lax.fori_loop(1, n_pairs, hello_pair, 0)
+    pl.semaphore_wait(barrier, n_pairs + 2)
 
 
 def remote(src, dst, send_sem, recv_sem, device):
@@ -330,65 +414,155 @@
     return finish
 
 
-def greet(n, me, device_of):
-    barrier = pltpu.get_barrier_semaphore()
-
-    def signal(distance, carry):
-        other = lax.rem(me + distance, n)
-        pl.semaphore_signal(barrier, inc=1, device_id=device_of(other), device_id_type=MESH)
+def weight_kernel(group, layer_ref, grad_ref, gx_ref, part_ref, gx_out, turned, held, load, store):
+    pieces, tall, _ = held.shape
+    turned[...] = jnp.transpose(grad_ref[...].astype(f32)).astype(bf16)
+
+    def bring(k):
+        return pltpu.make_async_copy(gx_ref.at[pl.ds(k * tall, tall)], held.at[k], load.at[k])
+
+    def put(k):
+        return pltpu.make_async_copy(held.at[k], gx_out.at[pl.ds(k * tall, tall)], store.at[k])
+
+    for k in range(pieces):
+        bring(k).start()
+    spots, half, width = part_ref.shape[2:]
+    wide = 2 * group * width
+    steps = spots // group
+
+    def step(s, carry):
+        both = dot_nn(turned[...], layer_ref[:, pl.ds(pl.multiple_of(s * wide, wide), wide)])
+        both = both.astype(bf16)
+        for t in range(group):
+            for c in range(2):
+                lanes = slice((2 * t + c) * width, (2 * t + c + 1) * width)
+                for k in range(2):
+                    rows = slice(k * half, (k + 1) * half)
+                    part_ref[c, k, s * group + t] = both[rows, lanes]
         return carry
 
-    lax.fori_loop(1, n, signal, 0)
-    pl.semaphore_wait(barrier, n - 1)
+    lax.fori_loop(0, steps // 2, step, 0)
+    for k in range(pieces):
+        bring(k).wait()
+        put(k).start()
+    lax.fori_loop(steps // 2, steps, step, 0)
+    for k in range(pieces):
+        put(k).wait()
 
 
 def step_kernel(
     n_seq, n_opt, part_ref, w_ref, code_ref, scale_ref, row_ref, col_ref,
-    update_ref, code_out, scale_out, row_out, col_out,
-    got_a, mid, got_b, stats, all_stats, peak, all_peaks,
-    send_a, recv_a, send_b, recv_b, send_c, recv_c, send_d, recv_d,
+    update_ref, code_out, small_out,
+    take_core, give_two, keep_two, take_two, give_three, keep_three, take_three, give_pair, take_pair,
+    stats, all_stats, peak, all_peaks,
+    send_core, recv_core, send_two, recv_two, send_three, recv_three, send_pair, recv_pair,
+    send_c, recv_c, send_d, recv_d,
 ):
     seq = lax.axis_index("seq")
     opt = lax.axis_index("opt")
     n = n_seq * n_opt
+    n_pairs = n_seq // 2
     me = seq * n_opt + opt
+    pair, side, cross, core, twins = place_of(seq, opt)
+    core_twin, cross_twin, side_twin = twins
 
     def any_device(i):
         return (i // n_opt, lax.rem(i, n_opt))
 
-    greet(n, me, any_device)
-    begin_swap(
-        n_opt, opt, lambda o: part_ref.at[o], lambda o: got_a.at[o],
-        lambda o: (seq, o), send_a, recv_a,
-    )()
-    got_a[opt] = part_ref[opt]
-
-    def fold(s, carry):
-        total = got_a[0, s].astype(f32)
-        for o in range(1, n_opt):
-            total += got_a[o, s].astype(f32)
-        mid[s] = total.astype(bf16)
+    greet_twins(n_pairs, seq, opt)
+    to_core = remote(part_ref.at[1 - core], take_core, send_core, recv_core, core_twin)
+    to_core.start()
+    to_core.wait()
+
+    def chip_sum(k, spot):
+        return part_ref[core, k, spot].astype(f32) + take_core[k, spot].astype(f32)
+
+    targets = ((cross_twin, side_twin), (side_twin, cross_twin))
+    own = ((cross, side), (side, cross))
+
+    def spot_of(k, p, a, b):
+        return (p * 2 + a) * 2 + b if k == 0 else (p * 2 + b) * 2 + a
+
+    def fill_two(q, carry):
+        for k in range(2):
+            spot = spot_of(k, q // 2, lax.rem(q, 2), 1 - own[0][k])
+            give_two[k, q] = chip_sum(k, spot).astype(bf16)
         return carry
 
-    lax.fori_loop(0, n_seq, fold, 0)
-    begin_swap(
-        n_seq, seq, lambda s: mid.at[s], lambda s: got_b.at[s],
-        lambda s: (s, opt), send_b, recv_b,
-    )()
-    got_b[seq] = mid[seq]
-    grad = got_b[0].astype(f32)
-    for s in range(1, n_seq):
-        grad += got_b[s].astype(f32)
+    lax.fori_loop(0, 2 * n_pairs, fill_two, 0)
+    second = [
+        remote(give_two.at[k], take_two.at[k], send_two.at[k], recv_two.at[k], targets[0][k])
+        for k in range(2)
+    ]
+    for copy in second:
+        copy.start()
+
+    def stay_two(q, carry):
+        for k in range(2):
+            spot = spot_of(k, q // 2, lax.rem(q, 2), own[0][k])
+            keep_two[k, q] = chip_sum(k, spot)
+        return carry
+
+    lax.fori_loop(0, 2 * n_pairs, stay_two, 0)
+    for copy in second:
+        copy.wait()
+
+    def fill_three(p, carry):
+        for k in range(2):
+            q = 2 * p + 1 - own[1][k]
+            give_three[k, p] = (keep_two[k, q] + take_two[k, q].astype(f32)).astype(bf16)
+        return carry
+
+    lax.fori_loop(0, n_pairs, fill_three, 0)
+    third = [
+        remote(give_three.at[k], take_three.at[k], send_three.at[k], recv_three.at[k], targets[1][k])
+        for k in range(2)
+    ]
+    for copy in third:
+        copy.start()
+
+    def stay_three(p, carry):
+        for k in range(2):
+            q = 2 * p + own[1][k]
+            keep_three[k, p] = keep_two[k, q] + take_two[k, q].astype(f32)
+        return carry
+
+    lax.fori_loop(0, n_pairs, stay_three, 0)
+    for copy in third:
+        copy.wait()
+
+    def fill_pair(p, carry):
+        for k in range(2):
+            give_pair[p, k] = (keep_three[k, p] + take_three[k, p].astype(f32)).astype(bf16)
+        return carry
+
+    lax.fori_loop(0, n_pairs, fill_pair, 0)
+    end_pairs = begin_swap(
+        n_pairs, pair, lambda p: give_pair.at[p], lambda p: take_pair.at[p],
+        lambda p: (p * 2 + side, opt), send_pair, recv_pair,
+    )
+    take_pair[pair] = jnp.zeros_like(take_pair[pair])
+    totals = [keep_three[k, pair] + take_three[k, pair].astype(f32) for k in range(2)]
+    turned = jnp.concatenate(totals, axis=0)
+    end_pairs()
+
+    def gather_pair(p, total):
+        return total + jnp.concatenate([take_pair[p, k].astype(f32) for k in range(2)], axis=0)
+
+    turned = lax.fori_loop(0, n_pairs, gather_pair, turned)
+    grad = jnp.transpose(turned)
 
     rows, cols = grad.shape
     width = n * rows
-    squares_raw = grad * grad
-    stats[:, :cols] = jnp.sum(squares_raw, axis=0, keepdims=True)
+    stats[:, :cols] = jnp.sum(grad * grad, axis=0, keepdims=True)
     row_stat = row_ref[...]
-    stats[:, cols:] = jnp.broadcast_to(jnp.sum(row_stat, axis=0, keepdims=True), (1, LANES))
-    begin_swap(
+    stats[:, cols:] = jnp.broadcast_to(jnp.sum(row_stat, axis=1, keepdims=True), (1, LANES))
+    end_stats = begin_swap(
         n, me, lambda i: stats, lambda i: all_stats.at[i], any_device, send_c, recv_c
-    )()
+    )
+    row_raw = jnp.sum(turned * turned, axis=0, keepdims=True)
+    old_moment = beta_one * code_ref[...].astype(f32) * scale_ref[...]
+    end_stats()
     all_stats[me] = stats[...]
     sums = all_stats[0]
     for i in range(1, n):
@@ -397,8 +571,7 @@
     old_total = sums[:, cols : cols + 1]
     raw_total = jnp.sum(col_raw, axis=1, keepdims=True)
     factor = jnp.minimum(1.0, clip_norm / jnp.sqrt(raw_total + norm_floor))
-    scaled = grad * factor
-    moment = beta_one * code_ref[...].astype(f32) * scale_ref[...] + (1.0 - beta_one) * scaled
+    moment = old_moment + (1.0 - beta_one) * (grad * factor)
     peak[...] = jnp.max(jnp.abs(moment), axis=0, keepdims=True)
     end_peaks = begin_swap(
         n, me, lambda i: peak, lambda i: all_peaks.at[i], any_device, send_d, recv_d
@@ -407,24 +580,33 @@
         factor * factor * col_raw / width + tiny_square
     )
     row_next = beta_two * row_stat + (1.0 - beta_two) * (
-        jnp.sum(scaled * scaled, axis=1, keepdims=True) / cols + tiny_square
+        factor * factor * row_raw / cols + tiny_square
     )
     row_mean = (
         beta_two * old_total
         + (1.0 - beta_two) * (factor * factor * raw_total / cols + width * tiny_square)
     ) / width
-    second = row_next * col_next / row_mean
-    update_ref[...] = moment / (jnp.sqrt(second) + adam_floor) + weight_decay * w_ref[...]
-    row_out[...] = row_next
-    col_out[...] = col_next
+    small_out[1:2, :] = col_next
+    small_out[2:3, :rows] = row_next
+    row_column = jnp.transpose(jnp.broadcast_to(row_next / row_mean, (8, rows)))[:, :1]
+    second_moment = row_column * col_next
+    update_ref[...] = moment / (jnp.sqrt(second_moment) + adam_floor) + weight_decay * w_ref[...]
     end_peaks()
     all_peaks[me] = peak[...]
     scale_next = all_peaks[0]
     for i in range(1, n):
         scale_next = jnp.maximum(scale_next, all_peaks[i])
     scale_next = scale_next + peak_floor
-    scale_out[...] = scale_next
+    small_out[0:1, :] = scale_next
     code_out[...] = (moment / scale_next).astype(bf16)
+
+
+def hand_out(update_ref, code_ref, small_ref, update_out, code_out, scale_out, row_out, col_out):
+    update_out[...] = update_ref[...]
+    code_out[...] = code_ref[...]
+    scale_out[...] = small_ref[0:1, :]
+    col_out[...] = small_ref[1:2, :]
+    row_out[...] = small_ref[2:3, : row_out.shape[1]]
 
 
 def params(**more):
@@ -467,23 +649,26 @@
     b_spec = pl.BlockSpec((length, state_dim), lambda h: (0, 0))
     c_spec = pl.BlockSpec((length, state_dim), lambda h: (0, 1))
 
-    w_shape = (own_rows, 2 * state_dim)
-    mixing, w_all = pl.pallas_call(
+    mixing, proj = pl.pallas_call(
         functools.partial(mixing_kernel, count, n_seq, n_opt),
         grid=(heads,),
-        in_specs=[whole(), tokens, tokens, run_spec],
+        in_specs=[
+            whole(), pl.BlockSpec(memory_space=pltpu.MemorySpace.HBM), tokens, tokens, run_spec
+        ],
         out_specs=[mix_spec, whole()],
         out_shape=[
             jax.ShapeDtypeStruct((count, BLOCK, BLOCK), f32),
-            jax.ShapeDtypeStruct((n_seq, n_opt) + w_shape, bf16),
+            jax.ShapeDtypeStruct((length, 2 * state_dim), bf16),
         ],
-        scratch_shapes=[pltpu.VMEM((n_opt, n_seq) + w_shape, bf16)] + dma(n_seq, n_opt),
+        scratch_shapes=[
+            pltpu.VMEM((n_pairs, 2, 2, 2, own_rows, 2 * state_dim), bf16),
+            pltpu.VMEM((length, width), bf16),
+            pltpu.SemaphoreType.DMA,
+        ]
+        + dma(n_pairs, 2, 2, 5),
         compiler_params=params(collective_id=2, has_side_effects=True),
         name="gather_and_mixing",
-    )(w_bc.astype(bf16), x, dy, running)
-    w_all = w_all.reshape(width, 2 * state_dim)
-
-    proj = jnp.dot(layer_rows, w_all, preferred_element_type=f32).astype(bf16)
+    )(w_bc, layer_rows, x, dy, running)
 
     lag = LAG_SWAP + LAG_CHAIN * (n_pairs - 1)
     near = pl.BlockSpec((length, head_dim), lambda i: (0, jnp.minimum(i, heads - 1)))
@@ -529,37 +714,70 @@
     )(skip_gain, x, dy, x, dy, proj, proj, running, mixing)
 
     cols = 2 * state_dim
-    part = lax.dot_general(
-        layer_rows, grad_bc, (((0,), (0,)), ((), ())), preferred_element_type=f32
-    ).astype(bf16)
-    part = jnp.transpose(part.reshape(n_seq, n_opt, own_rows, cols), (1, 0, 2, 3))
-
     n = n_seq * n_opt
-    update, code_next, scale_next, row_next, col_next = pl.pallas_call(
+    spots = n // 2
+    group = max(2, 2 * LANES // own_rows)
+    in_hbm = pl.BlockSpec(memory_space=pltpu.MemorySpace.HBM)
+    pieces = 8
+    part, grad_input = pl.pallas_call(
+        functools.partial(weight_kernel, group),
+        in_specs=[whole(), whole(), in_hbm],
+        out_specs=[whole(), in_hbm],
+        out_shape=[
+            jax.ShapeDtypeStruct((2, 2, spots, state_dim, own_rows), bf16),
+            jax.ShapeDtypeStruct(x.shape, bf16),
+        ],
+        scratch_shapes=[
+            pltpu.VMEM((cols, length), bf16),
+            pltpu.VMEM((pieces, length // pieces, x.shape[1]), bf16),
+            pltpu.SemaphoreType.DMA((pieces,)),
+            pltpu.SemaphoreType.DMA((pieces,)),
+        ],
+        compiler_params=params(),
+        name="weight_gradient",
+    )(layer_rows, grad_bc, grad_input)
+
+    block = (state_dim, own_rows)
+    tall = jax.ShapeDtypeStruct((own_rows, cols), f32)
+    code = jax.ShapeDtypeStruct((own_rows, cols), bf16)
+    results = pl.pallas_call(
         functools.partial(step_kernel, n_seq, n_opt),
         in_specs=[whole()] * 6,
-        out_specs=[whole()] * 5,
-        out_shape=[
-            jax.ShapeDtypeStruct((own_rows, cols), f32),
-            jax.ShapeDtypeStruct((own_rows, cols), bf16),
-            jax.ShapeDtypeStruct((1, cols), f32),
-            jax.ShapeDtypeStruct((own_rows, 1), f32),
-            jax.ShapeDtypeStruct((1, cols), f32),
-        ],
+        out_specs=[whole()] * 3,
+        out_shape=[tall, code, jax.ShapeDtypeStruct((8, cols), f32)],
         scratch_shapes=[
-            pltpu.VMEM((n_opt, n_seq, own_rows, cols), bf16),
-            pltpu.VMEM((n_seq, own_rows, cols), bf16),
-            pltpu.VMEM((n_seq, own_rows, cols), bf16),
+            pltpu.VMEM((2, spots) + block, bf16),
+            pltpu.VMEM((2, n_seq) + block, bf16),
+            pltpu.VMEM((2, n_seq) + block, f32),
+            pltpu.VMEM((2, n_seq) + block, bf16),
+            pltpu.VMEM((2, n_pairs) + block, bf16),
+            pltpu.VMEM((2, n_pairs) + block, f32),
+            pltpu.VMEM((2, n_pairs) + block, bf16),
+            pltpu.VMEM((n_pairs, 2) + block, bf16),
+            pltpu.VMEM((n_pairs, 2) + block, bf16),
             pltpu.VMEM((1, cols + LANES), f32),
             pltpu.VMEM((n, 1, cols + LANES), f32),
             pltpu.VMEM((1, cols), f32),
             pltpu.VMEM((n, 1, cols), f32),
+            pltpu.SemaphoreType.DMA,
+            pltpu.SemaphoreType.DMA,
         ]
-        + dma(n_opt, n_seq, n, n),
+        + dma(2, 2, n_pairs, n, n),
         compiler_params=params(collective_id=1, has_side_effects=True),
         name="sum_and_step",
-    )(part, w_bc, m_code, m_scale[None, :], row_stat[:, None], col_stat[None, :])
-    return (grad_input[None], update, code_next, scale_next[0], row_next[:, 0], col_next[0])
+    )(part, w_bc, m_code, m_scale[None, :], row_stat[None, :], col_stat[None, :])
+    update, code_next, scale_next, row_next, col_next = pl.pallas_call(
+        hand_out,
+        in_specs=[whole()] * 3,
+        out_specs=[whole()] * 5,
+        out_shape=[
+            tall, code, jax.ShapeDtypeStruct((1, cols), f32),
+            jax.ShapeDtypeStruct((1, own_rows), f32), jax.ShapeDtypeStruct((1, cols), f32),
+        ],
+        compiler_params=params(),
+        name="hand_out",
+    )(*results)
+    return (grad_input[None], update, code_next, scale_next[0], row_next[0], col_next[0])
 
 
 def solution(mesh):

time: 191 us -> 152 us (0.80)
  Pallas kernels: 163 us -> 149 us
  local copies, waits for them, and re-layouts: 15 us -> 1.52 us
  matrix products: 8.59 us -> 0.21 us
  other arithmetic: 3.01 us -> 0 us
    pallas_call x1, Pallas kernels: 51.5 us -> 36.4 us  [per_device(): pl.pallas_call(functools.partial(step_kernel, n_seq, n_opt), in_specs=[wh...]
    pallas_call x0 -> x2, Pallas kernels: none -> 8.7 us  [the longest x1 7.06 us: per_device(): pl.pallas_call(functools.partial(weight_kernel, group), in_specs=[whole()...]
    dot_general x2 -> x0, matrix products: 8.38 us -> none  [the longest x1 4.82 us: per_device(): proj = jnp.dot(layer_rows, w_all, preferred_element_type=f32).astype(bf16)]
    unnamed x15 -> x0, local copies, waits for them, and re-layouts: 7.17 us -> none
    pallas_call x1, Pallas kernels: 42.1 us -> 36.8 us  [per_device(): pl.pallas_call(functools.partial(mixing_kernel, count, n_seq, n_opt), gri...]
    reshape x1 -> x0, local copies, waits for them, and re-layouts: 3.13 us -> none  [per_device(): part.reshape(n_seq, n_opt, own_rows, cols)]
    pallas_call x1, Pallas kernels: 69.6 us -> 66.8 us  [per_device(): pl.pallas_call(functools.partial(states_kernel, count, heads, n_pairs), g...]
    convert_element_type x1 -> x0, local copies, waits for them, and re-layouts: 2.46 us -> none  [per_device(): part = lax.dot_general(layer_rows, grad_bc, (((0,), (0,)), ((), ())), pre...]
where the time goes in v2:
time: 152 us; the launch traced here: 151 us
  Pallas kernels  149 us (98%)
  local copies, waits for them, and re-layouts  1.52 us (1%)
    pallas_call x1, Pallas kernels, per_device(): pl.pallas_call(functools.partial(states_kernel, count, heads, n_pairs), g...  66.8 us
    pallas_call x1, Pallas kernels, per_device(): pl.pallas_call(functools.partial(mixing_kernel, count, n_seq, n_opt), gri...  36.8 us
    pallas_call x1, Pallas kernels, per_device(): pl.pallas_call(functools.partial(step_kernel, n_seq, n_opt), in_specs=[wh...  36.4 us
    pallas_call x1, Pallas kernels, per_device(): pl.pallas_call(functools.partial(weight_kernel, group), in_specs=[whole()...  7.06 us

profile of v2, /device:TPU:0, one launch (start us, length us, event | category | flops | bytes accessed | tf_op | source)
XLA Modules:
  0.0 151.1 jit_solution(9678810018626522405)
XLA Ops:
  0.6 0.9 reshape_squeeze.3
  1.5 0.2 convolution_bitcast_fusion
  1.7 0.7 reshape.15.run_ref
  2.4 36.8 %gather_and_mixing.1 = (f32[2,256,256]{2,1,0:T(8,128)}, bf16[512,256]{1,0:T(8,128)(2,1)}) custom-call(f32[128,256]{1,0:T(8,128)} %w_ref.3, bf16[512,4096]{1,0:T(8,128)(2,1)} %bitcast.19, bf16[512,4096]{1,0:T(8,128)(2,1)} %bitcast.13, bf16[512,4096]{1,0:T(8,128)(2,1)} %bitcast.16, f32[32,2,256]{2,1,0:T(2,128)} %reshape.15.run_ref), custom_call_target="tpu_custom_call" | custom-call | tf_op jit(solution)/shard_map/gather_and_mixing/pallas_call | solution.py:652
  39.2 66.8 %states_and_grads.1 = (bf16[512,4096]{1,0:T(8,128)(2,1)}, bf16[512,256]{1,0:T(8,128)(2,1)}) custom-call(f32[32]{0:T(128)} %skip_ref.1, bf16[512,4096]{1,0:T(8,128)(2,1)} %bitcast.14, bf16[512,4096]{1,0:T(8,128)(2,1)} %bitcast.17, bf16[512,4096]{1,0:T(8,128)(2,1)} %bitcast.15, bf16[512,4096]{1,0:T(8,128)(2,1)} %bitcast.18, ...), custom_call_target="tpu_custom_call" | custom-call | tf_op jit(solution)/shard_map/states_and_grads/pallas_call | solution.py:679
  106.0 7.1 %weight_gradient.1 = (bf16[2,2,16,128,128]{4,3,2,1,0:T(8,128)(2,1)}, bf16[512,4096]{1,0:T(8,128)(2,1)}) custom-call(bf16[512,4096]{1,0:T(8,128)(2,1)} %bitcast.20, bf16[512,256]{1,0:T(8,128)(2,1)} %get-tuple-element.22.grad_ref, bf16[512,4096]{1,0:T(8,128)(2,1)} %get-tuple-element.23.gx_ref), custom_call_target="tpu_custom_call" | custom-call | tf_op jit(solution)/shard_map/weight_gradient/pallas_call | solution.py:722
  113.0 36.4 %sum_and_step.1 = (f32[128,256]{1,0:T(8,128)}, bf16[128,256]{1,0:T(8,128)(2,1)}, f32[8,256]{1,0:T(8,128)}) custom-call(bf16[2,2,16,128,128]{4,3,2,1,0:T(8,128)(2,1)} %get-tuple-element.25.part_ref, f32[128,256]{1,0:T(8,128)} %w_ref.3, bf16[128,256]{1,0:T(8,128)(2,1)} %code_ref.1, f32[1,256]{1,0:T(1,128)} %bitcast.21, f32[1,128]{1,0:T(1,128)} %bitcast.23, ...), custom_call_target="tpu_custom_call" | custom-call | tf_op jit(solution)/shard_map/sum_and_step/pallas_call | solution.py:743
  149.5 1.6 %hand_out.1 = (f32[128,256]{1,0:T(8,128)}, bf16[128,256]{1,0:T(8,128)(2,1)}, f32[1,256]{1,0:T(1,128)}, f32[1,128]{1,0:T(1,128)}, f32[1,256]{1,0:T(1,128)}) custom-call(f32[128,256]{1,0:T(8,128)} %get-tuple-element.26.update_ref, bf16[128,256]{1,0:T(8,128)(2,1)} %get-tuple-element.27.code_ref, f32[8,256]{1,0:T(8,128)} %get-tuple-element.28.small_ref), custom_call_target="tpu_custom_call" | custom-call | tf_op jit(solution)/shard_map/hand_out/pallas_call | solution.py:769

commit v3 on v2

--- a/solution.py
+++ b/solution.py
@@ -11,8 +11,6 @@
 LANES = 128
 LAG_SWAP = 3
 LAG_CHAIN = 2
-STEP_B = 20
-STEP_C = 30
 
 beta_one = 0.9
 beta_two = 0.95
@@ -49,115 +47,130 @@
     return jnp.concatenate([column] * (length // LANES), axis=1)
 
 
-def mixing_kernel(
-    count, n_seq, n_opt, w_ref, layer_ref, x_ref, dy_ref, run_ref, mix_ref, proj_ref,
-    got, layer, load, send_a, recv_a, send_b, recv_b, send_c, recv_c, send_d, recv_d,
+def gather_kernel(
+    count, n_seq, n_opt, w_ref, log_ref, layer_ref, proj_ref, run_ref,
+    got, layer, total, load, send_a, recv_a, send_b, recv_b, send_c, recv_c, send_d, recv_d,
 ):
     seq = lax.axis_index("seq")
     opt = lax.axis_index("opt")
-    h = pl.program_id(0)
-    last = pl.num_programs(0) - 1
     n_pairs = n_seq // 2
     pair, side, cross, core, twins = place_of(seq, opt)
     core_twin, cross_twin, side_twin = twins
     half = w_ref.shape[0] // 2
     low, high = slice(0, half), slice(half, 2 * half)
 
-    def same(part, send_sem, recv_sem, k, device):
-        return remote(part, part, send_sem.at[k], recv_sem.at[k], device)
-
-    def along():
-        own = got.at[pair, side, cross, core]
-        return swap_all(
-            n_pairs, pair, lambda p: own, lambda p: got.at[p, side, cross, core],
-            lambda p: (p * 2 + side, opt), send_a, recv_a,
-        )
-
-    def second():
-        return (
-            same(got.at[:, side, cross, core, low], send_b, recv_b, 0, side_twin),
-            same(got.at[:, side, cross, core, high], send_b, recv_b, 1, cross_twin),
-        )
-
-    def third():
-        return (
-            same(got.at[:, :, cross, core, low], send_c, recv_c, 0, cross_twin),
-            same(got.at[:, side, :, core, high], send_c, recv_c, 1, side_twin),
-        )
-
-    def to_core(k):
-        parts = (
-            lambda: got.at[:, side, cross, core],
-            lambda: got.at[:, 1 - side, cross, core, low],
-            lambda: got.at[:, side, 1 - cross, core, high],
-            lambda: got.at[:, :, 1 - cross, core, low],
-            lambda: got.at[:, 1 - side, :, core, high],
-        )
-        return same(parts[k](), send_d, recv_d, k, core_twin)
-
-    def from_core(k):
-        parts = (
-            lambda: got.at[:, side, cross, 1 - core],
-            lambda: got.at[:, 1 - side, cross, 1 - core, low],
-            lambda: got.at[:, side, 1 - cross, 1 - core, high],
-            lambda: got.at[:, :, 1 - cross, 1 - core, low],
-            lambda: got.at[:, 1 - side, :, 1 - core, high],
-        )
-        return same(parts[k](), send_d, recv_d, k, core_twin)
-
-    def load_layer():
-        return pltpu.make_async_copy(layer_ref, layer, load)
-
-    @pl.when(h == 0)
-    def _():
-        got[pair, side, cross, core] = w_ref[...].astype(bf16)
-        greet_twins(n_pairs, seq, opt)
-        along()[0]()
-        load_layer().start()
-        mix_ref[...] = jnp.zeros_like(mix_ref)
-
-    @pl.when(h == last * STEP_B // 32)
-    def _():
-        along()[1]()
-        for copy in second():
-            copy.start()
-        to_core(0).start()
-
-    @pl.when(h == last * STEP_C // 32)
-    def _():
-        for copy in second():
-            copy.wait()
-        for copy in third():
-            copy.start()
-        to_core(1).start()
-        to_core(2).start()
-
-    row_pos = lax.broadcasted_iota(jnp.int32, (BLOCK, BLOCK), 0)
-    col_pos = lax.broadcasted_iota(jnp.int32, (BLOCK, BLOCK), 1)
-    for b in range(count):
-        rows = slice(b * BLOCK, (b + 1) * BLOCK)
-        row = run_ref[0, b : b + 1, :]
-        spread = widened(as_column(row), BLOCK) - row
-        decays = jnp.exp(jnp.where(row_pos >= col_pos, spread, -jnp.inf))
-        mix_ref[b] += decays * dot_nt(dy_ref[rows, :], x_ref[rows, :])
-
-    @pl.when(h == last)
-    def _():
-        for copy in third():
-            copy.wait()
-        to_core(3).start()
-        to_core(4).start()
-        load_layer().wait()
-        for k in range(5):
-            to_core(k).wait_send()
-            from_core(k).wait_recv()
-        total = None
-        for p in range(n_pairs):
+    def same(part, send_sem, recv_sem, device):
+        return remote(part, part, send_sem, recv_sem, device)
+
+    def along(p, owner):
+        block = got.at[owner, side, cross, core]
+        other = (p * 2 + side, opt)
+        return remote(block, block, send_a.at[p], recv_a.at[owner], other)
+
+    def own_to(k, p, s, x):
+        device = (cross_twin, side_twin)[k]
+        return same(got.at[p, s, x, core], send_b.at[k, p], recv_b.at[k, p], device)
+
+    def relay_to(k, p, s, x):
+        device = (cross_twin, side_twin)[k]
+        part = got.at[p, s, x, core, (low, high)[k]]
+        return same(part, send_c.at[k, p], recv_c.at[k, p], device)
+
+    def to_core(k, p, c):
+        s = side if k % 2 == 0 else 1 - side
+        x = cross if k // 2 == 0 else 1 - cross
+        return same(got.at[p, s, x, c], send_d.at[k, p], recv_d.at[k, p], core_twin)
+
+    layer_copy = pltpu.make_async_copy(layer_ref, layer, load)
+    layer_copy.start()
+    got[pair, side, cross, core] = w_ref[...].astype(bf16)
+    greet_twins(n_pairs, seq, opt)
+
+    def send_along(distance, carry):
+        along(lax.rem(pair + distance, n_pairs), pair).start()
+        return carry
+
+    lax.fori_loop(1, n_pairs, send_along, 0)
+    ones = (
+        lax.broadcasted_iota(jnp.int32, (BLOCK, BLOCK), 0)
+        <= lax.broadcasted_iota(jnp.int32, (BLOCK, BLOCK), 1)
+    ).astype(f32)
+
+    def turn(d, carry):
+        @pl.when(d < n_pairs)
+        def _():
+            p = lax.rem(pair + d, n_pairs)
+
+            @pl.when(d > 0)
+            def _():
+                along(p, p).wait_recv()
+
+            own_to(0, p, side, cross).start()
+            own_to(1, p, side, cross).start()
+            to_core(0, p, core).start()
+
+        @pl.when(d == 0)
+        def _():
+            for b in range(count):
+                sums = jnp.dot(
+                    log_ref[:, b * BLOCK : (b + 1) * BLOCK], ones,
+                    precision=highest, preferred_element_type=f32,
+                )
+                run_ref[:, b : b + 1, :] = sums[:, None, :]
+            total[...] = jnp.zeros_like(total)
+
+        @pl.when(jnp.logical_and(d >= 1, d < n_pairs + 1))
+        def _():
+            p = lax.rem(pair + d - 1, n_pairs)
+            own_to(0, p, side, 1 - cross).wait_recv()
+            relay_to(1, p, side, 1 - cross).start()
+            own_to(1, p, 1 - side, cross).wait_recv()
+            relay_to(0, p, 1 - side, cross).start()
+            to_core(1, p, core).start()
+            to_core(2, p, core).start()
+
+        @pl.when(jnp.logical_and(d >= 2, d < n_pairs + 2))
+        def _():
+            p = lax.rem(pair + d - 2, n_pairs)
+            relay_to(0, p, 1 - side, 1 - cross).wait_recv()
+            relay_to(1, p, 1 - side, 1 - cross).wait_recv()
+            to_core(3, p, core).start()
+
+        @pl.when(d == 3)
+        def _():
+            layer_copy.wait()
+
+        @pl.when(d >= 3)
+        def _():
+            p = lax.rem(pair + d - 3, n_pairs)
+            for k in range(4):
+                to_core(k, p, 1 - core).wait_recv()
             w_part = got[p].reshape(-1, got.shape[-1])
             depth = w_part.shape[0]
-            term = dot_nn(layer[:, p * depth : (p + 1) * depth], w_part)
-            total = term if total is None else total + term
-        proj_ref[...] = total.astype(bf16)
+            columns = pl.ds(pl.multiple_of(p * depth, depth), depth)
+            total[...] += dot_nn(layer[:, columns], w_part)
+
+        return carry
+
+    lax.fori_loop(0, n_pairs + 3, turn, 0)
+    proj_ref[...] = total[...].astype(bf16)
+
+    def sent(d, carry):
+        p = lax.rem(pair + d, n_pairs)
+
+        @pl.when(d > 0)
+        def _():
+            along(p, pair).wait_send()
+
+        own_to(0, p, side, cross).wait_send()
+        own_to(1, p, side, cross).wait_send()
+        relay_to(0, p, 1 - side, cross).wait_send()
+        relay_to(1, p, side, 1 - cross).wait_send()
+        for k in range(4):
+            to_core(k, p, core).wait_send()
+        return carry
+
+    lax.fori_loop(0, n_pairs, sent, 0)
 
 
 def place_of(seq, opt):
@@ -193,9 +206,9 @@
 
 
 def states_kernel(
-    count, heads, n_pairs, skip_ref, x_ref, dy_ref, x_far, dy_far, b_ref, c_ref, run_ref, mix_ref,
+    count, heads, n_pairs, skip_ref, x_ref, dy_ref, x_far, dy_far, b_ref, c_ref, run_ref,
     gx_ref, gbc_ref,
-    b_turned, c_turned, affinity, acc_b, acc_c, starts, outs, mine, got, chain_in, chain_out,
+    b_turned, c_turned, affinity, mixing, acc_b, acc_c, starts, outs, mine, got, chain_in, chain_out,
     decay, decay_far, send_d, recv_d, send_y, recv_y, send_c, recv_c,
 ):
     i = pl.program_id(0)
@@ -244,6 +257,7 @@
             return carry
 
         lax.fori_loop(0, heads, decay_of, 0)
+        mixing[...] = jnp.zeros_like(mixing)
         acc_b[...] = jnp.zeros_like(acc_b)
         acc_c[...] = jnp.zeros_like(acc_c)
         b_turned[...] = jnp.transpose(b_ref[...].astype(f32))
@@ -353,6 +367,7 @@
             dy_blk = dy_far[rows, :]
             spread = row - widened(column, BLOCK)
             decays = jnp.exp(jnp.where(col_pos >= row_pos, spread, -jnp.inf))
+            mixing[b] += decays * dot_nt(x_blk, dy_blk)
             weighted = (decays * affinity[b]).astype(bf16)
             inner = dot_nn(weighted, dy_blk)
             outer = dot_nn(b_ref[rows, :], grad_in) * shrink
@@ -364,9 +379,9 @@
     def _():
         for b in range(count):
             rows = slice(b * BLOCK, (b + 1) * BLOCK)
-            mixing = mix_ref[b].astype(bf16)
-            gbc_ref[rows, :state_dim] = (acc_b[rows, :] + dot_tn(mixing, c_ref[rows, :])).astype(bf16)
-            gbc_ref[rows, state_dim:] = (acc_c[rows, :] + dot_nn(mixing, b_ref[rows, :])).astype(bf16)
+            mixed = mixing[b].astype(bf16)
+            gbc_ref[rows, :state_dim] = (acc_b[rows, :] + dot_nn(mixed, c_ref[rows, :])).astype(bf16)
+            gbc_ref[rows, state_dim:] = (acc_c[rows, :] + dot_tn(mixed, b_ref[rows, :])).astype(bf16)
         swap_decay().wait_send()
 
         def sent(h, carry):
@@ -426,19 +441,21 @@
 
     for k in range(pieces):
         bring(k).start()
-    spots, half, width = part_ref.shape[2:]
+    _, _, n_i, _, n_r, half, width = part_ref.shape
     wide = 2 * group * width
-    steps = spots // group
+    steps = 2 * n_i * n_r // group
 
     def step(s, carry):
         both = dot_nn(turned[...], layer_ref[:, pl.ds(pl.multiple_of(s * wide, wide), wide)])
         both = both.astype(bf16)
         for t in range(group):
+            spot = s * group + t
+            p = spot // n_r
             for c in range(2):
                 lanes = slice((2 * t + c) * width, (2 * t + c + 1) * width)
                 for k in range(2):
                     rows = slice(k * half, (k + 1) * half)
-                    part_ref[c, k, s * group + t] = both[rows, lanes]
+                    part_ref[c, k, p // 2, lax.rem(p, 2), lax.rem(spot, n_r)] = both[rows, lanes]
         return carry
 
     lax.fori_loop(0, steps // 2, step, 0)
@@ -470,81 +487,130 @@
         return (i // n_opt, lax.rem(i, n_opt))
 
     greet_twins(n_pairs, seq, opt)
-    to_core = remote(part_ref.at[1 - core], take_core, send_core, recv_core, core_twin)
-    to_core.start()
-    to_core.wait()
-
-    def chip_sum(k, spot):
-        return part_ref[core, k, spot].astype(f32) + take_core[k, spot].astype(f32)
-
+    n_i = n_pairs // 2
     targets = ((cross_twin, side_twin), (side_twin, cross_twin))
     own = ((cross, side), (side, cross))
-
-    def spot_of(k, p, a, b):
-        return (p * 2 + a) * 2 + b if k == 0 else (p * 2 + b) * 2 + a
-
-    def fill_two(q, carry):
-        for k in range(2):
-            spot = spot_of(k, q // 2, lax.rem(q, 2), 1 - own[0][k])
-            give_two[k, q] = chip_sum(k, spot).astype(bf16)
+    first = [
+        remote(
+            part_ref.at[1 - core, :, :, g], take_core.at[:, :, g],
+            send_core.at[g], recv_core.at[g], core_twin,
+        )
+        for g in range(2)
+    ]
+    second = [
+        [
+            remote(
+                give_two.at[k, g], take_two.at[k, g], send_two.at[k, g], recv_two.at[k, g],
+                targets[0][k],
+            )
+            for k in range(2)
+        ]
+        for g in range(2)
+    ]
+    third = [
+        [
+            remote(
+                give_three.at[k, g], take_three.at[k, g], send_three.at[k, g], recv_three.at[k, g],
+                targets[1][k],
+            )
+            for k in range(2)
+        ]
+        for g in range(2)
+    ]
+
+    def chip_sum(k, g, i, a, b):
+        r = a * 2 + b if k == 0 else b * 2 + a
+        return part_ref[core, k, i, g, r].astype(f32) + take_core[k, i, g, r].astype(f32)
+
+    def fill_two(g):
+        def body(q, carry):
+            for k in range(2):
+                total = chip_sum(k, g, q // 2, lax.rem(q, 2), 1 - own[0][k])
+                give_two[k, g, q] = total.astype(bf16)
+            return carry
+
+        lax.fori_loop(0, 2 * n_i, body, 0)
+
+    def stay_two(g):
+        def body(q, carry):
+            for k in range(2):
+                keep_two[k, g, q] = chip_sum(k, g, q // 2, lax.rem(q, 2), own[0][k])
+            return carry
+
+        lax.fori_loop(0, 2 * n_i, body, 0)
+
+    def fill_three(g):
+        def body(i, carry):
+            for k in range(2):
+                q = 2 * i + 1 - own[1][k]
+                total = keep_two[k, g, q] + take_two[k, g, q].astype(f32)
+                give_three[k, g, i] = total.astype(bf16)
+            return carry
+
+        lax.fori_loop(0, n_i, body, 0)
+
+    def stay_three(g):
+        def body(i, carry):
+            for k in range(2):
+                q = 2 * i + own[1][k]
+                keep_three[k, g, i] = keep_two[k, g, q] + take_two[k, g, q].astype(f32)
+            return carry
+
+        lax.fori_loop(0, n_i, body, 0)
+
+    def slice_sum(k, g, i):
+        return keep_three[k, g, i] + take_three[k, g, i].astype(f32)
+
+    def to_pair(p, source):
+        return remote(
+            give_pair.at[p], take_pair.at[source], send_pair.at[p], recv_pair.at[source],
+            (p * 2 + side, opt),
+        )
+
+    for copy in first:
+        copy.start()
+    for g in range(2):
+        first[g].wait()
+        fill_two(g)
+        for copy in second[g]:
+            copy.start()
+    for g in range(2):
+        stay_two(g)
+    for g in range(2):
+        for copy in second[g]:
+            copy.wait()
+        fill_three(g)
+        for copy in third[g]:
+            copy.start()
+    for g in range(2):
+        stay_three(g)
+    for g in range(2):
+        for copy in third[g]:
+            copy.wait()
+
+        def send_slices(i, carry):
+            p = 2 * i + g
+
+            @pl.when(p != pair)
+            def _():
+                for k in range(2):
+                    give_pair[p, k] = slice_sum(k, g, i).astype(bf16)
+                to_pair(p, pair).start()
+
+            return carry
+
+        lax.fori_loop(0, n_i, send_slices, 0)
+    take_pair[pair] = jnp.zeros_like(take_pair[pair])
+    group_of = lax.rem(pair, 2)
+    totals = [slice_sum(k, group_of, pair // 2) for k in range(2)]
+    turned = jnp.concatenate(totals, axis=0)
+
+    def end_slices(distance, carry):
+        p = lax.rem(pair + distance, n_pairs)
+        to_pair(p, p).wait()
         return carry
 
-    lax.fori_loop(0, 2 * n_pairs, fill_two, 0)
-    second = [
-        remote(give_two.at[k], take_two.at[k], send_two.at[k], recv_two.at[k], targets[0][k])
-        for k in range(2)
-    ]
-    for copy in second:
-        copy.start()
-
-    def stay_two(q, carry):
-        for k in range(2):
-            spot = spot_of(k, q // 2, lax.rem(q, 2), own[0][k])
-            keep_two[k, q] = chip_sum(k, spot)
-        return carry
-
-    lax.fori_loop(0, 2 * n_pairs, stay_two, 0)
-    for copy in second:
-        copy.wait()
-
-    def fill_three(p, carry):
-        for k in range(2):
-            q = 2 * p + 1 - own[1][k]
-            give_three[k, p] = (keep_two[k, q] + take_two[k, q].astype(f32)).astype(bf16)
-        return carry
-
-    lax.fori_loop(0, n_pairs, fill_three, 0)
-    third = [
-        remote(give_three.at[k], take_three.at[k], send_three.at[k], recv_three.at[k], targets[1][k])
-        for k in range(2)
-    ]
-    for copy in third:
-        copy.start()
-
-    def stay_three(p, carry):
-        for k in range(2):
-            q = 2 * p + own[1][k]
-            keep_three[k, p] = keep_two[k, q] + take_two[k, q].astype(f32)
-        return carry
-
-    lax.fori_loop(0, n_pairs, stay_three, 0)
-    for copy in third:
-        copy.wait()
-
-    def fill_pair(p, carry):
-        for k in range(2):
-            give_pair[p, k] = (keep_three[k, p] + take_three[k, p].astype(f32)).astype(bf16)
-        return carry
-
-    lax.fori_loop(0, n_pairs, fill_pair, 0)
-    end_pairs = begin_swap(
-        n_pairs, pair, lambda p: give_pair.at[p], lambda p: take_pair.at[p],
-        lambda p: (p * 2 + side, opt), send_pair, recv_pair,
-    )
-    take_pair[pair] = jnp.zeros_like(take_pair[pair])
-    totals = [keep_three[k, pair] + take_three[k, pair].astype(f32) for k in range(2)]
-    turned = jnp.concatenate(totals, axis=0)
-    end_pairs()
+    lax.fori_loop(1, n_pairs, end_slices, 0)
 
     def gather_pair(p, total):
         return total + jnp.concatenate([take_pair[p, k].astype(f32) for k in range(2)], axis=0)
@@ -636,40 +702,30 @@
     n_pairs = n_seq // 2
     own_rows = w_bc.shape[0]
 
-    ones = (
-        lax.broadcasted_iota(jnp.int32, (BLOCK, BLOCK), 0)
-        <= lax.broadcasted_iota(jnp.int32, (BLOCK, BLOCK), 1)
-    ).astype(f32)
-    running = jnp.dot(
-        log_decay[0].reshape(heads * count, BLOCK), ones, precision=highest
-    ).reshape(heads, count, BLOCK)
-    tokens = pl.BlockSpec((length, head_dim), lambda h: (0, h))
-    run_spec = pl.BlockSpec((1, count, BLOCK), lambda h: (h, 0, 0))
-    mix_spec = pl.BlockSpec((count, BLOCK, BLOCK), lambda h: (0, 0, 0))
-    b_spec = pl.BlockSpec((length, state_dim), lambda h: (0, 0))
-    c_spec = pl.BlockSpec((length, state_dim), lambda h: (0, 1))
-
-    mixing, proj = pl.pallas_call(
-        functools.partial(mixing_kernel, count, n_seq, n_opt),
-        grid=(heads,),
-        in_specs=[
-            whole(), pl.BlockSpec(memory_space=pltpu.MemorySpace.HBM), tokens, tokens, run_spec
-        ],
-        out_specs=[mix_spec, whole()],
+    in_hbm = pl.BlockSpec(memory_space=pltpu.MemorySpace.HBM)
+    proj, running = pl.pallas_call(
+        functools.partial(gather_kernel, count, n_seq, n_opt),
+        in_specs=[whole(), whole(), in_hbm],
+        out_specs=[whole(), whole()],
         out_shape=[
-            jax.ShapeDtypeStruct((count, BLOCK, BLOCK), f32),
             jax.ShapeDtypeStruct((length, 2 * state_dim), bf16),
+            jax.ShapeDtypeStruct((heads, count, BLOCK), f32),
         ],
         scratch_shapes=[
             pltpu.VMEM((n_pairs, 2, 2, 2, own_rows, 2 * state_dim), bf16),
             pltpu.VMEM((length, width), bf16),
+            pltpu.VMEM((length, 2 * state_dim), f32),
             pltpu.SemaphoreType.DMA,
         ]
-        + dma(n_pairs, 2, 2, 5),
+        + [pltpu.SemaphoreType.DMA((n_pairs,))] * 2
+        + [pltpu.SemaphoreType.DMA((2, n_pairs))] * 4
+        + [pltpu.SemaphoreType.DMA((4, n_pairs))] * 2,
         compiler_params=params(collective_id=2, has_side_effects=True),
-        name="gather_and_mixing",
-    )(w_bc, layer_rows, x, dy, running)
-
+        name="gather_and_project",
+    )(w_bc, log_decay[0], layer_rows)
+
+    b_spec = pl.BlockSpec((length, state_dim), lambda i: (0, 0))
+    c_spec = pl.BlockSpec((length, state_dim), lambda i: (0, 1))
     lag = LAG_SWAP + LAG_CHAIN * (n_pairs - 1)
     near = pl.BlockSpec((length, head_dim), lambda i: (0, jnp.minimum(i, heads - 1)))
     late = pl.BlockSpec((length, head_dim), lambda i: (0, jnp.maximum(i - lag, 0)))
@@ -681,7 +737,6 @@
         grid=(heads + lag,),
         in_specs=[
             pl.BlockSpec(memory_space=pltpu.SMEM), near, near, late, late, b_spec, c_spec, all_run,
-            mix_spec,
         ],
         out_specs=[late, pl.BlockSpec((length, 2 * state_dim), lambda h: (0, 0))],
         out_shape=[
@@ -691,6 +746,7 @@
         scratch_shapes=[
             pltpu.VMEM((state_dim, length), f32),
             pltpu.VMEM((state_dim, length), f32),
+            pltpu.VMEM((count, BLOCK, BLOCK), f32),
             pltpu.VMEM((count, BLOCK, BLOCK), f32),
             pltpu.VMEM((length, state_dim), f32),
             pltpu.VMEM((length, state_dim), f32),
@@ -711,20 +767,19 @@
         ],
         compiler_params=params(collective_id=0, has_side_effects=True),
         name="states_and_grads",
-    )(skip_gain, x, dy, x, dy, proj, proj, running, mixing)
+    )(skip_gain, x, dy, x, dy, proj, proj, running)
 
     cols = 2 * state_dim
     n = n_seq * n_opt
     spots = n // 2
     group = max(2, 2 * LANES // own_rows)
-    in_hbm = pl.BlockSpec(memory_space=pltpu.MemorySpace.HBM)
     pieces = 8
     part, grad_input = pl.pallas_call(
         functools.partial(weight_kernel, group),
         in_specs=[whole(), whole(), in_hbm],
         out_specs=[whole(), in_hbm],
         out_shape=[
-            jax.ShapeDtypeStruct((2, 2, spots, state_dim, own_rows), bf16),
+            jax.ShapeDtypeStruct((2, 2, n_pairs // 2, 2, 4, state_dim, own_rows), bf16),
             jax.ShapeDtypeStruct(x.shape, bf16),
         ],
         scratch_shapes=[
@@ -746,23 +801,23 @@
         out_specs=[whole()] * 3,
         out_shape=[tall, code, jax.ShapeDtypeStruct((8, cols), f32)],
         scratch_shapes=[
-            pltpu.VMEM((2, spots) + block, bf16),
-            pltpu.VMEM((2, n_seq) + block, bf16),
-            pltpu.VMEM((2, n_seq) + block, f32),
-            pltpu.VMEM((2, n_seq) + block, bf16),
-            pltpu.VMEM((2, n_pairs) + block, bf16),
-            pltpu.VMEM((2, n_pairs) + block, f32),
-            pltpu.VMEM((2, n_pairs) + block, bf16),
+            pltpu.VMEM((2, n_pairs // 2, 2, 4) + block, bf16),
+            pltpu.VMEM((2, 2, n_pairs) + block, bf16),
+            pltpu.VMEM((2, 2, n_pairs) + block, f32),
+            pltpu.VMEM((2, 2, n_pairs) + block, bf16),
+            pltpu.VMEM((2, 2, n_pairs // 2) + block, bf16),
+            pltpu.VMEM((2, 2, n_pairs // 2) + block, f32),
+            pltpu.VMEM((2, 2, n_pairs // 2) + block, bf16),
             pltpu.VMEM((n_pairs, 2) + block, bf16),
             pltpu.VMEM((n_pairs, 2) + block, bf16),
             pltpu.VMEM((1, cols + LANES), f32),
             pltpu.VMEM((n, 1, cols + LANES), f32),
             pltpu.VMEM((1, cols), f32),
             pltpu.VMEM((n, 1, cols), f32),
-            pltpu.SemaphoreType.DMA,
-            pltpu.SemaphoreType.DMA,
         ]
-        + dma(2, 2, n_pairs, n, n),
+        + dma(2)
+        + [pltpu.SemaphoreType.DMA((2, 2))] * 4
+        + dma(n_pairs, n, n),
         compiler_params=params(collective_id=1, has_side_effects=True),
         name="sum_and_step",
     )(part, w_bc, m_code, m_scale[None, :], row_stat[None, :], col_stat[None, :])

time: 152 us -> 136 us (0.89)
  Pallas kernels: 149 us -> 135 us
  local copies, waits for them, and re-layouts: 1.52 us -> 0 us
    pallas_call x1, Pallas kernels: 36.8 us -> 24.9 us  [per_device(): pl.pallas_call(functools.partial(gather_kernel, count, n_seq, n_opt), in_...]
    pallas_call x1, Pallas kernels: 36.4 us -> 33 us  [per_device(): pl.pallas_call(functools.partial(step_kernel, n_seq, n_opt), in_specs=[wh...]
where the time goes in v3:
time: 136 us; the launch traced here: 135 us
  Pallas kernels  135 us (99%)
    pallas_call x1, Pallas kernels, per_device(): pl.pallas_call(functools.partial(states_kernel, count, heads, n_pairs), g...  68 us
    pallas_call x1, Pallas kernels, per_device(): pl.pallas_call(functools.partial(step_kernel, n_seq, n_opt), in_specs=[wh...  33 us
    pallas_call x1, Pallas kernels, per_device(): pl.pallas_call(functools.partial(gather_kernel, count, n_seq, n_opt), in_...  24.9 us
    pallas_call x1, Pallas kernels, per_device(): pl.pallas_call(functools.partial(weight_kernel, group), in_specs=[whole()...  7.1 us

profile of v3, /device:TPU:0, one launch (start us, length us, event | category | flops | bytes accessed | tf_op | source)
XLA Modules:
  0.0 135.3 jit_solution(11038381135300235540)
XLA Ops:
  0.6 24.9 %gather_and_project.1 = (bf16[512,256]{1,0:T(8,128)(2,1)}, f32[32,2,256]{2,1,0:T(2,128)}) custom-call(f32[128,256]{1,0:T(8,128)} %w_ref.3, f32[32,512]{1,0:T(8,128)} %bitcast.17, bf16[512,4096]{1,0:T(8,128)(2,1)} %bitcast.15), custom_call_target="tpu_custom_call" | custom-call | tf_op jit(solution)/shard_map/gather_and_project/pallas_call | solution.py:706
  25.5 68.0 %states_and_grads.1 = (bf16[512,4096]{1,0:T(8,128)(2,1)}, bf16[512,256]{1,0:T(8,128)(2,1)}) custom-call(f32[32]{0:T(128)} %skip_ref.1, bf16[512,4096]{1,0:T(8,128)(2,1)} %bitcast.11, bf16[512,4096]{1,0:T(8,128)(2,1)} %bitcast.13, bf16[512,4096]{1,0:T(8,128)(2,1)} %bitcast.12, bf16[512,4096]{1,0:T(8,128)(2,1)} %bitcast.14, ...), custom_call_target="tpu_custom_call" | custom-call | tf_op jit(solution)/shard_map/states_and_grads/pallas_call | solution.py:735
  93.5 7.1 %weight_gradient.1 = (bf16[2,2,2,2,4,128,128]{6,5,4,3,2,1,0:T(8,128)(2,1)}, bf16[512,4096]{1,0:T(8,128)(2,1)}) custom-call(bf16[512,4096]{1,0:T(8,128)(2,1)} %bitcast.16, bf16[512,256]{1,0:T(8,128)(2,1)} %get-tuple-element.22.grad_ref, bf16[512,4096]{1,0:T(8,128)(2,1)} %get-tuple-element.23.gx_ref), custom_call_target="tpu_custom_call" | custom-call | tf_op jit(solution)/shard_map/weight_gradient/pallas_call | solution.py:777
  100.6 33.0 %sum_and_step.1 = (f32[128,256]{1,0:T(8,128)}, bf16[128,256]{1,0:T(8,128)(2,1)}, f32[8,256]{1,0:T(8,128)}) custom-call(bf16[2,2,2,2,4,128,128]{6,5,4,3,2,1,0:T(8,128)(2,1)} %get-tuple-element.25.part_ref, f32[128,256]{1,0:T(8,128)} %w_ref.3, bf16[128,256]{1,0:T(8,128)(2,1)} %code_ref.1, f32[1,256]{1,0:T(1,128)} %bitcast.18, f32[1,128]{1,0:T(1,128)} %bitcast.20, ...), custom_call_target="tpu_custom_call" | custom-call | tf_op jit(solution)/shard_map/sum_and_step/pallas_call | solution.py:798
  133.6 1.6 %hand_out.1 = (f32[128,256]{1,0:T(8,128)}, bf16[128,256]{1,0:T(8,128)(2,1)}, f32[1,256]{1,0:T(1,128)}, f32[1,128]{1,0:T(1,128)}, f32[1,256]{1,0:T(1,128)}) custom-call(f32[128,256]{1,0:T(8,128)} %get-tuple-element.26.update_ref, bf16[128,256]{1,0:T(8,128)(2,1)} %get-tuple-element.27.code_ref, f32[8,256]{1,0:T(8,128)} %get-tuple-element.28.small_ref), custom_call_target="tpu_custom_call" | custom-call | tf_op jit(solution)/shard_map/hand_out/pallas_call | solution.py:824

commit v4 on v3

--- a/solution.py
+++ b/solution.py
@@ -10,7 +10,7 @@
 BLOCK = 256
 LANES = 128
 LAG_SWAP = 3
-LAG_CHAIN = 2
+LAG_CHAIN = 3
 
 beta_one = 0.9
 beta_two = 0.95
@@ -22,7 +22,6 @@
 norm_floor = 1e-06
 highest = lax.Precision.HIGHEST
 MESH = pl.DeviceIdType.MESH
-VMEM_LIMIT = 60 * 1024 * 1024
 f32 = jnp.float32
 bf16 = jnp.bfloat16
 
@@ -48,8 +47,8 @@
 
 
 def gather_kernel(
-    count, n_seq, n_opt, w_ref, log_ref, layer_ref, proj_ref, run_ref,
-    got, layer, total, load, send_a, recv_a, send_b, recv_b, send_c, recv_c, send_d, recv_d,
+    count, n_seq, n_opt, w_ref, log_ref, layer_ref, proj_ref, run_ref, decay_ref,
+    got, layer, total, decay, load, send_e, recv_e, send_a, recv_a, send_b, recv_b, send_c, recv_c, send_d, recv_d,
 ):
     seq = lax.axis_index("seq")
     opt = lax.axis_index("opt")
@@ -81,6 +80,9 @@
         x = cross if k // 2 == 0 else 1 - cross
         return same(got.at[p, s, x, c], send_d.at[k, p], recv_d.at[k, p], core_twin)
 
+    def decay_copy():
+        return remote(decay.at[0], decay.at[1], send_e, recv_e, side_twin)
+
     layer_copy = pltpu.make_async_copy(layer_ref, layer, load)
     layer_copy.start()
     got[pair, side, cross, core] = w_ref[...].astype(bf16)
@@ -111,13 +113,21 @@
 
         @pl.when(d == 0)
         def _():
+            closing = None
             for b in range(count):
                 sums = jnp.dot(
                     log_ref[:, b * BLOCK : (b + 1) * BLOCK], ones,
                     precision=highest, preferred_element_type=f32,
                 )
                 run_ref[:, b : b + 1, :] = sums[:, None, :]
+                tail = sums[:, BLOCK - 1 :]
+                closing = tail if closing is None else closing + tail
+            decay[0] = jnp.broadcast_to(jnp.exp(closing), (closing.shape[0], LANES))[:, None, :]
             total[...] = jnp.zeros_like(total)
+
+        @pl.when(d == 1)
+        def _():
+            decay_copy().start()
 
         @pl.when(jnp.logical_and(d >= 1, d < n_pairs + 1))
         def _():
@@ -154,6 +164,8 @@
 
     lax.fori_loop(0, n_pairs + 3, turn, 0)
     proj_ref[...] = total[...].astype(bf16)
+    decay_copy().wait()
+    decay_ref[...] = decay[...]
 
     def sent(d, carry):
         p = lax.rem(pair + d, n_pairs)
@@ -206,21 +218,39 @@
 
 
 def states_kernel(
-    count, heads, n_pairs, skip_ref, x_ref, dy_ref, x_far, dy_far, b_ref, c_ref, run_ref,
+    count, heads, n_pairs, skip_ref, x_ref, dy_ref, proj_ref, run_ref, decay_ref,
     gx_ref, gbc_ref,
     b_turned, c_turned, affinity, mixing, acc_b, acc_c, starts, outs, mine, got, chain_in, chain_out,
-    decay, decay_far, send_d, recv_d, send_y, recv_y, send_c, recv_c,
+    send_y, recv_y, send_c, recv_c,
 ):
-    i = pl.program_id(0)
     seq = lax.axis_index("seq")
     opt = lax.axis_index("opt")
     pair = seq // 2
     side = lax.rem(seq, 2)
-    lag = LAG_SWAP + LAG_CHAIN * (n_pairs - 1)
-    state_dim = b_ref.shape[1]
+    state_dim = proj_ref.shape[1] // 2
+    head_dim = x_ref.shape[1] // heads
+    b_cols, c_cols = slice(0, state_dim), slice(state_dim, 2 * state_dim)
     twin = (seq + 1 - 2 * side, opt)
     ahead = (seq + 2, opt)
     behind = (seq - 2, opt)
+    has_source = (pair > 0, pair < n_pairs - 1)
+    has_target = (pair < n_pairs - 1, pair > 0)
+    places = (pair, n_pairs - 1 - pair)
+
+    late = heads // 4
+    early = 3 * heads // 16
+    reach = LAG_CHAIN * (n_pairs - 1)
+    wait = max(0, reach - heads + late)
+    swap_lag = late + LAG_SWAP
+    steps = max(heads - late + reach, heads + wait) + swap_lag
+
+    def head_of(slot):
+        return jnp.where(
+            slot < early, slot, jnp.where(slot < heads - late, slot + late, slot - heads + late + early)
+        )
+
+    def lanes_of(h):
+        return pl.ds(pl.multiple_of(h * head_dim, head_dim), head_dim)
 
     def closings_of(h):
         return [run_ref[h, b : b + 1, BLOCK - 1 : BLOCK] for b in range(count)]
@@ -228,54 +258,37 @@
     def swap(h):
         return remote(mine.at[h], got.at[h], send_y.at[h], recv_y.at[h], twin)
 
-    def swap_decay():
-        return remote(decay, decay_far, send_d, recv_d, twin)
+    def swap_late(h):
+        return remote(chain_out.at[2, h], got.at[h], send_y.at[h], recv_y.at[h], twin)
 
     def pass_on(way, h):
         return remote(
-            chain_out.at[way, h], chain_in.at[way, h], send_c.at[way, h], recv_c.at[way, h],
+            chain_out.at[way, h, 0], chain_in.at[way, h], send_c.at[way, h], recv_c.at[way, h],
             (ahead, behind)[way],
         )
 
-    has_source = (pair > 0, pair < n_pairs - 1)
-    has_target = (pair < n_pairs - 1, pair > 0)
-
-    @pl.when(i == 0)
-    def _():
-        barrier = pltpu.get_barrier_semaphore()
-        pl.semaphore_signal(barrier, inc=1, device_id=twin, device_id_type=MESH)
-        for way in range(2):
-            @pl.when(has_target[way])
-            def _():
-                pl.semaphore_signal(
-                    barrier, inc=1, device_id=(ahead, behind)[way], device_id_type=MESH
-                )
-
-        def decay_of(h, carry):
-            total = sum(closings_of(h), jnp.zeros((1, 1), f32))
-            decay[h] = jnp.broadcast_to(jnp.exp(total), (1, LANES))
-            return carry
-
-        lax.fori_loop(0, heads, decay_of, 0)
-        mixing[...] = jnp.zeros_like(mixing)
-        acc_b[...] = jnp.zeros_like(acc_b)
-        acc_c[...] = jnp.zeros_like(acc_c)
-        b_turned[...] = jnp.transpose(b_ref[...].astype(f32))
-        c_turned[...] = jnp.transpose(c_ref[...].astype(f32))
-        for b in range(count):
-            rows = slice(b * BLOCK, (b + 1) * BLOCK)
-            affinity[b] = dot_nt(b_ref[rows, :], c_ref[rows, :])
-        for way in range(2):
-            @pl.when(jnp.logical_not(has_source[way]))
-            def _():
-                chain_in[way] = jnp.zeros_like(chain_in[way])
-        neighbours = 1 + (pair > 0).astype(jnp.int32) + (pair < n_pairs - 1).astype(jnp.int32)
-        pl.semaphore_wait(barrier, neighbours)
-        swap_decay().start()
-
-    @pl.when(i < heads)
-    def _():
-        h = i
+    def hop(way, h, with_other):
+        @pl.when(has_source[way])
+        def _():
+            pass_on(way, h).wait_recv()
+
+        @pl.when(has_target[way])
+        def _():
+            own_decay = decay_ref[0, h]
+            other_decay = decay_ref[1, h]
+            first = side == way
+            own_scale = jnp.where(first, other_decay, 1.0)
+            total = (
+                own_decay * other_decay * chain_in[way, h].astype(f32)
+                + own_scale * mine[h, way].astype(f32)
+            )
+            if with_other:
+                other_scale = jnp.where(first, 1.0, own_decay)
+                total += other_scale * got[h, way].astype(f32)
+            chain_out[way, h, 0] = total.astype(bf16)
+            pass_on(way, h).start()
+
+    def local(h):
         adds = []
         for b in range(count):
             rows = slice(b * BLOCK, (b + 1) * BLOCK)
@@ -283,9 +296,9 @@
             closing = row[:, BLOCK - 1 : BLOCK]
             b_scaled = (b_turned[:, rows] * jnp.exp(closing - row)).astype(bf16)
             c_scaled = (c_turned[:, rows] * jnp.exp(row)).astype(bf16)
-            adds.append(
-                (jnp.exp(closing), dot_nn(b_scaled, x_ref[rows, :]), dot_nn(c_scaled, dy_ref[rows, :]))
-            )
+            x_blk = x_ref[rows, lanes_of(h)]
+            dy_blk = dy_ref[rows, lanes_of(h)]
+            adds.append((jnp.exp(closing), dot_nn(b_scaled, x_blk), dot_nn(c_scaled, dy_blk)))
         state = adds[0][1]
         for b in range(1, count):
             starts[h, b - 1] = state.astype(bf16)
@@ -296,55 +309,17 @@
             outs[h, b] = carried.astype(bf16)
             carried = adds[b][0] * carried + adds[b][2]
         mine[h, 1] = carried.astype(bf16)
-        swap(h).start()
-
-    @pl.when(i == LAG_SWAP)
-    def _():
-        swap_decay().wait_recv()
-
-    j = i - LAG_SWAP
-
-    @pl.when(jnp.logical_and(j >= 0, j < heads))
-    def _():
-        swap(j).wait_recv()
-
-    for way in range(2):
-        place = pair if way == 0 else n_pairs - 1 - pair
-        hop = j - LAG_CHAIN * place
-
-        @pl.when(jnp.logical_and(hop >= 0, hop < heads))
-        def _():
-            @pl.when(has_source[way])
-            def _():
-                pass_on(way, hop).wait_recv()
-
-            @pl.when(has_target[way])
-            def _():
-                own_decay = decay[hop]
-                other_decay = decay_far[hop]
-                first = side == way
-                own_scale = jnp.where(first, other_decay, 1.0)
-                other_scale = jnp.where(first, 1.0, own_decay)
-                total = (
-                    own_decay * other_decay * chain_in[way, hop].astype(f32)
-                    + own_scale * mine[hop, way].astype(f32)
-                    + other_scale * got[hop, way].astype(f32)
-                )
-                chain_out[way, hop] = total.astype(bf16)
-                pass_on(way, hop).start()
-
-    @pl.when(i >= lag)
-    def _():
-        h = i - lag
+
+    def finish(h, swapped_late):
         row_pos = lax.broadcasted_iota(jnp.int32, (BLOCK, BLOCK), 0)
         col_pos = lax.broadcasted_iota(jnp.int32, (BLOCK, BLOCK), 1)
         closings = closings_of(h)
-        other_decay = decay_far[h]
+        other_decay = decay_ref[1, h]
         fars = []
         for way in range(2):
             second = side != way
             scale = jnp.where(second, other_decay, 1.0)
-            extra = jnp.where(second, jnp.ones((1, LANES), f32), 0.0)
+            extra = jnp.where(jnp.logical_or(second, swapped_late), jnp.ones((1, LANES), f32), 0.0)
             fars.append(scale * chain_in[way, h].astype(f32) + extra * got[h, way].astype(f32))
         far_state, far_grad = fars
         for b in range(count):
@@ -363,36 +338,131 @@
                 grad_in = (outs[h, b].astype(f32) + jnp.exp(after) * far_grad).astype(bf16)
             grow = jnp.exp(column)
             shrink = jnp.exp(closings[b] - column)
-            x_blk = x_far[rows, :]
-            dy_blk = dy_far[rows, :]
+            x_blk = x_ref[rows, lanes_of(h)]
+            dy_blk = dy_ref[rows, lanes_of(h)]
             spread = row - widened(column, BLOCK)
             decays = jnp.exp(jnp.where(col_pos >= row_pos, spread, -jnp.inf))
             mixing[b] += decays * dot_nt(x_blk, dy_blk)
             weighted = (decays * affinity[b]).astype(bf16)
             inner = dot_nn(weighted, dy_blk)
-            outer = dot_nn(b_ref[rows, :], grad_in) * shrink
-            gx_ref[rows, :] = (inner + outer + skip_ref[h] * dy_blk.astype(f32)).astype(bf16)
+            outer = dot_nn(proj_ref[rows, b_cols], grad_in) * shrink
+            full = inner + outer + skip_ref[h] * dy_blk.astype(f32)
+            gx_ref[rows, lanes_of(h)] = full.astype(bf16)
             acc_c[rows, :] += grow * dot_nt(dy_blk, state_in)
             acc_b[rows, :] += shrink * dot_nt(x_blk, grad_in)
 
-    @pl.when(i == pl.num_programs(0) - 1)
-    def _():
-        for b in range(count):
-            rows = slice(b * BLOCK, (b + 1) * BLOCK)
-            mixed = mixing[b].astype(bf16)
-            gbc_ref[rows, :state_dim] = (acc_b[rows, :] + dot_nn(mixed, c_ref[rows, :])).astype(bf16)
-            gbc_ref[rows, state_dim:] = (acc_c[rows, :] + dot_tn(mixed, b_ref[rows, :])).astype(bf16)
-        swap_decay().wait_send()
-
-        def sent(h, carry):
+    barrier = pltpu.get_barrier_semaphore()
+    pl.semaphore_signal(barrier, inc=1, device_id=twin, device_id_type=MESH)
+    for way in range(2):
+        @pl.when(has_target[way])
+        def _():
+            pl.semaphore_signal(barrier, inc=1, device_id=(ahead, behind)[way], device_id_type=MESH)
+
+    b_turned[...] = jnp.transpose(proj_ref[:, b_cols].astype(f32))
+    c_turned[...] = jnp.transpose(proj_ref[:, c_cols].astype(f32))
+    for way in range(2):
+        @pl.when(jnp.logical_not(has_source[way]))
+        def _():
+            chain_in[way] = jnp.zeros_like(chain_in[way])
+    neighbours = 1 + (pair > 0).astype(jnp.int32) + (pair < n_pairs - 1).astype(jnp.int32)
+    pl.semaphore_wait(barrier, neighbours)
+
+    def step(i, carry):
+        is_late = jnp.logical_and(i >= early, i < early + late)
+
+        @pl.when(i < heads)
+        def _():
+            local(i)
+
+            @pl.when(jnp.logical_not(is_late))
+            def _():
+                swap(i).start()
+
+        @pl.when(i == early)
+        def _():
+            mixing[...] = jnp.zeros_like(mixing)
+            acc_b[...] = jnp.zeros_like(acc_b)
+            acc_c[...] = jnp.zeros_like(acc_c)
+            for b in range(count):
+                rows = slice(b * BLOCK, (b + 1) * BLOCK)
+                affinity[b] = dot_nt(proj_ref[rows, b_cols], proj_ref[rows, c_cols])
+
+        for way in range(2):
+            h = i - 1 - LAG_CHAIN * places[way]
+
+            @pl.when(jnp.logical_and(h >= early, h < early + late))
+            def _():
+                hop(way, h, False)
+
+        slot = i - late - wait
+
+        @pl.when(jnp.logical_and(slot >= heads - late, slot < heads))
+        def _():
+            h = head_of(slot)
+            own_decay = decay_ref[0, h]
+            for way in range(2):
+                first = side == way
+                scale = jnp.where(first, own_decay, 1.0)
+                extra = jnp.where(first, jnp.ones((1, LANES), f32), 0.0)
+                total = scale * chain_in[way, h].astype(f32) + extra * mine[h, way].astype(f32)
+                chain_out[2, h, way] = total.astype(bf16)
+            swap_late(h).start()
+
+        slot = i - swap_lag
+
+        @pl.when(jnp.logical_and(slot >= 0, slot < heads - late))
+        def _():
+            swap(head_of(slot)).wait_recv()
+
+        for way in range(2):
+            slot = i - swap_lag - LAG_CHAIN * places[way]
+
+            @pl.when(jnp.logical_and(slot >= 0, slot < heads - late))
+            def _():
+                hop(way, head_of(slot), True)
+
+        slot = i - swap_lag - reach
+
+        @pl.when(jnp.logical_and(slot >= 0, slot < heads - late))
+        def _():
+            finish(head_of(slot), False)
+
+        slot = i - swap_lag - wait
+
+        @pl.when(jnp.logical_and(slot >= heads - late, slot < heads))
+        def _():
+            h = head_of(slot)
+            swap_late(h).wait_recv()
+            finish(h, True)
+
+        return carry
+
+    lax.fori_loop(0, steps, step, 0)
+    for b in range(count):
+        rows = slice(b * BLOCK, (b + 1) * BLOCK)
+        mixed = mixing[b].astype(bf16)
+        gbc_ref[rows, b_cols] = (acc_b[rows, :] + dot_nn(mixed, proj_ref[rows, c_cols])).astype(bf16)
+        gbc_ref[rows, c_cols] = (acc_c[rows, :] + dot_tn(mixed, proj_ref[rows, b_cols])).astype(bf16)
+
+    def sent(h, carry):
+        is_late = jnp.logical_and(h >= early, h < early + late)
+
+        @pl.when(is_late)
+        def _():
+            swap_late(h).wait_send()
+
+        @pl.when(jnp.logical_not(is_late))
+        def _():
             swap(h).wait_send()
-            for way in range(2):
-                @pl.when(has_target[way])
-                def _():
-                    pass_on(way, h).wait_send()
-            return carry
-
-        lax.fori_loop(0, heads, sent, 0)
+
+        for way in range(2):
+            @pl.when(has_target[way])
+            def _():
+                pass_on(way, h).wait_send()
+
+        return carry
+
+    lax.fori_loop(0, heads, sent, 0)
 
 
 def swap_all(n, me, src_of, dst_of, device_of, send_sem, recv_sem):
@@ -429,18 +499,11 @@
     return finish
 
 
-def weight_kernel(group, layer_ref, grad_ref, gx_ref, part_ref, gx_out, turned, held, load, store):
-    pieces, tall, _ = held.shape
+def weight_kernel(group, layer_ref, grad_ref, gx_ref, part_ref, gx_out, turned, store):
+    put = pltpu.make_async_copy(gx_ref, gx_out, store)
+    put.start()
     turned[...] = jnp.transpose(grad_ref[...].astype(f32)).astype(bf16)
 
-    def bring(k):
-        return pltpu.make_async_copy(gx_ref.at[pl.ds(k * tall, tall)], held.at[k], load.at[k])
-
-    def put(k):
-        return pltpu.make_async_copy(held.at[k], gx_out.at[pl.ds(k * tall, tall)], store.at[k])
-
-    for k in range(pieces):
-        bring(k).start()
     _, _, n_i, _, n_r, half, width = part_ref.shape
     wide = 2 * group * width
     steps = 2 * n_i * n_r // group
@@ -458,13 +521,8 @@
                     part_ref[c, k, p // 2, lax.rem(p, 2), lax.rem(spot, n_r)] = both[rows, lanes]
         return carry
 
-    lax.fori_loop(0, steps // 2, step, 0)
-    for k in range(pieces):
-        bring(k).wait()
-        put(k).start()
-    lax.fori_loop(steps // 2, steps, step, 0)
-    for k in range(pieces):
-        put(k).wait()
+    lax.fori_loop(0, steps, step, 0)
+    put.wait()
 
 
 def step_kernel(
@@ -675,8 +733,8 @@
     row_out[...] = small_ref[2:3, : row_out.shape[1]]
 
 
-def params(**more):
-    return pltpu.CompilerParams(vmem_limit_bytes=VMEM_LIMIT, **more)
+def params(mebibytes, **more):
+    return pltpu.CompilerParams(vmem_limit_bytes=mebibytes * 1024 * 1024, **more)
 
 
 def whole():
@@ -703,42 +761,37 @@
     own_rows = w_bc.shape[0]
 
     in_hbm = pl.BlockSpec(memory_space=pltpu.MemorySpace.HBM)
-    proj, running = pl.pallas_call(
+    proj, running, decay = pl.pallas_call(
         functools.partial(gather_kernel, count, n_seq, n_opt),
         in_specs=[whole(), whole(), in_hbm],
-        out_specs=[whole(), whole()],
+        out_specs=[whole()] * 3,
         out_shape=[
             jax.ShapeDtypeStruct((length, 2 * state_dim), bf16),
             jax.ShapeDtypeStruct((heads, count, BLOCK), f32),
+            jax.ShapeDtypeStruct((2, heads, 1, LANES), f32),
         ],
         scratch_shapes=[
             pltpu.VMEM((n_pairs, 2, 2, 2, own_rows, 2 * state_dim), bf16),
             pltpu.VMEM((length, width), bf16),
             pltpu.VMEM((length, 2 * state_dim), f32),
+            pltpu.VMEM((2, heads, 1, LANES), f32),
+            pltpu.SemaphoreType.DMA,
+            pltpu.SemaphoreType.DMA,
             pltpu.SemaphoreType.DMA,
         ]
         + [pltpu.SemaphoreType.DMA((n_pairs,))] * 2
         + [pltpu.SemaphoreType.DMA((2, n_pairs))] * 4
         + [pltpu.SemaphoreType.DMA((4, n_pairs))] * 2,
-        compiler_params=params(collective_id=2, has_side_effects=True),
+        compiler_params=params(52, collective_id=2, has_side_effects=True),
         name="gather_and_project",
     )(w_bc, log_decay[0], layer_rows)
 
-    b_spec = pl.BlockSpec((length, state_dim), lambda i: (0, 0))
-    c_spec = pl.BlockSpec((length, state_dim), lambda i: (0, 1))
-    lag = LAG_SWAP + LAG_CHAIN * (n_pairs - 1)
-    near = pl.BlockSpec((length, head_dim), lambda i: (0, jnp.minimum(i, heads - 1)))
-    late = pl.BlockSpec((length, head_dim), lambda i: (0, jnp.maximum(i - lag, 0)))
-    all_run = pl.BlockSpec((heads, count, BLOCK), lambda i: (0, 0, 0))
     per_head = (heads, 2, state_dim, head_dim)
-    per_way = (2, heads, state_dim, head_dim)
+    inner_states = (heads, max(count - 1, 1), state_dim, head_dim)
     grad_input, grad_bc = pl.pallas_call(
         functools.partial(states_kernel, count, heads, n_pairs),
-        grid=(heads + lag,),
-        in_specs=[
-            pl.BlockSpec(memory_space=pltpu.SMEM), near, near, late, late, b_spec, c_spec, all_run,
-        ],
-        out_specs=[late, pl.BlockSpec((length, 2 * state_dim), lambda h: (0, 0))],
+        in_specs=[pl.BlockSpec(memory_space=pltpu.SMEM)] + [whole()] * 5,
+        out_specs=[whole()] * 2,
         out_shape=[
             jax.ShapeDtypeStruct(x.shape, bf16),
             jax.ShapeDtypeStruct((length, 2 * state_dim), bf16),
@@ -750,33 +803,28 @@
             pltpu.VMEM((count, BLOCK, BLOCK), f32),
             pltpu.VMEM((length, state_dim), f32),
             pltpu.VMEM((length, state_dim), f32),
-            pltpu.VMEM((heads, max(count - 1, 1), state_dim, head_dim), bf16),
-            pltpu.VMEM((heads, max(count - 1, 1), state_dim, head_dim), bf16),
+            pltpu.VMEM(inner_states, bf16),
+            pltpu.VMEM(inner_states, bf16),
             pltpu.VMEM(per_head, bf16),
             pltpu.VMEM(per_head, bf16),
-            pltpu.VMEM(per_way, bf16),
-            pltpu.VMEM(per_way, bf16),
-            pltpu.VMEM((heads, 1, LANES), f32),
-            pltpu.VMEM((heads, 1, LANES), f32),
-            pltpu.SemaphoreType.DMA,
-            pltpu.SemaphoreType.DMA,
+            pltpu.VMEM((2, heads, state_dim, head_dim), bf16),
+            pltpu.VMEM((3,) + per_head, bf16),
             pltpu.SemaphoreType.DMA((heads,)),
             pltpu.SemaphoreType.DMA((heads,)),
             pltpu.SemaphoreType.DMA((2, heads)),
             pltpu.SemaphoreType.DMA((2, heads)),
         ],
-        compiler_params=params(collective_id=0, has_side_effects=True),
+        compiler_params=params(26, collective_id=0, has_side_effects=True),
         name="states_and_grads",
-    )(skip_gain, x, dy, x, dy, proj, proj, running)
+    )(skip_gain, x, dy, proj, running, decay)
 
     cols = 2 * state_dim
     n = n_seq * n_opt
     spots = n // 2
     group = max(2, 2 * LANES // own_rows)
-    pieces = 8
     part, grad_input = pl.pallas_call(
         functools.partial(weight_kernel, group),
-        in_specs=[whole(), whole(), in_hbm],
+        in_specs=[whole()] * 3,
         out_specs=[whole(), in_hbm],
         out_shape=[
             jax.ShapeDtypeStruct((2, 2, n_pairs // 2, 2, 4, state_dim, own_rows), bf16),
@@ -784,11 +832,9 @@
         ],
         scratch_shapes=[
             pltpu.VMEM((cols, length), bf16),
-            pltpu.VMEM((pieces, length // pieces, x.shape[1]), bf16),
-            pltpu.SemaphoreType.DMA((pieces,)),
-            pltpu.SemaphoreType.DMA((pieces,)),
+            pltpu.SemaphoreType.DMA,
         ],
-        compiler_params=params(),
+        compiler_params=params(28),
         name="weight_gradient",
     )(layer_rows, grad_bc, grad_input)
 
@@ -818,7 +864,7 @@
         + dma(2)
         + [pltpu.SemaphoreType.DMA((2, 2))] * 4
         + dma(n_pairs, n, n),
-        compiler_params=params(collective_id=1, has_side_effects=True),
+        compiler_params=params(28, collective_id=1, has_side_effects=True),
         name="sum_and_step",
     )(part, w_bc, m_code, m_scale[None, :], row_stat[None, :], col_stat[None, :])
     update, code_next, scale_next, row_next, col_next = pl.pallas_call(
@@ -829,7 +875,7 @@
             tall, code, jax.ShapeDtypeStruct((1, cols), f32),
             jax.ShapeDtypeStruct((1, own_rows), f32), jax.ShapeDtypeStruct((1, cols), f32),
         ],
-        compiler_params=params(),
+        compiler_params=params(28),
         name="hand_out",
     )(*results)
     return (grad_input[None], update, code_next, scale_next[0], row_next[0], col_next[0])

time: 136 us -> 118 us (0.87)
  Pallas kernels: 135 us -> 112 us
  local copies, waits for them, and re-layouts: 0 us -> 4.37 us
    pallas_call x1, Pallas kernels: 68 us -> 53.8 us  [per_device(): pl.pallas_call(functools.partial(states_kernel, count, heads, n_pairs), i...]
    pallas_call x1, Pallas kernels: 7.1 us -> 2.69 us  [per_device(): pl.pallas_call(functools.partial(weight_kernel, group), in_specs=[whole()...]
    unnamed x0 -> x20, local copies, waits for them, and re-layouts: none -> 4.37 us
    pallas_call x1, Pallas kernels: 33 us -> 31.1 us  [per_device(): pl.pallas_call(functools.partial(step_kernel, n_seq, n_opt), in_specs=[wh...]
where the time goes in v4:
time: 118 us; the launch traced here: 117 us
  Pallas kernels  112 us (95%)
  local copies, waits for them, and re-layouts  4.37 us (4%)
    pallas_call x1, Pallas kernels, per_device(): pl.pallas_call(functools.partial(states_kernel, count, heads, n_pairs), i...  53.8 us
    pallas_call x1, Pallas kernels, per_device(): pl.pallas_call(functools.partial(step_kernel, n_seq, n_opt), in_specs=[wh...  31.1 us
    pallas_call x1, Pallas kernels, per_device(): pl.pallas_call(functools.partial(gather_kernel, count, n_seq, n_opt), in_...  24 us
    unnamed x20, local copies, waits for them, and re-layouts  4.37 us
    pallas_call x1, Pallas kernels, per_device(): pl.pallas_call(functools.partial(weight_kernel, group), in_specs=[whole()...  2.69 us

profile of v4, /device:TPU:0, one launch (start us, length us, event | category | flops | bytes accessed | tf_op | source)
XLA Modules:
  0.0 117.4 jit_solution(17373898670316865938)
XLA Ops:
  0.6 0.0 copy-start.1
  0.6 0.0 copy-start.3
  0.7 1.0 copy-done.3
  1.7 0.0 copy-start.4
  1.7 1.1 copy-done.4
  2.8 0.0 copy-start.8
  2.8 24.0 %gather_and_project.1 = (bf16[512,256]{1,0:T(8,128)(2,1)S(1)}, f32[32,2,256]{2,1,0:T(2,128)S(1)}, f32[2,32,1,128]{3,2,1,0:T(1,128)S(1)}) custom-call(f32[128,256]{1,0:T(8,128)S(1)} %copy-done.3, f32[32,512]{1,0:T(8,128)S(1)} %bitcast.15, bf16[512,4096]{1,0:T(8,128)(2,1)} %bitcast.11), custom_call_target="tpu_custom_call" | custom-call | tf_op jit(solution)/shard_map/gather_and_project/pallas_call | solution.py:764
  26.8 0.0 copy-done.1
  26.8 0.0 copy-done.8
  26.8 0.0 copy-start.2
  26.8 2.2 %copy-done.2 = bf16[1,512,4096]{2,1,0:T(8,128)(2,1)S(1)} copy-done((bf16[1,512,4096]{2,1,0:T(8,128)(2,1)S(1)}, bf16[1,512,4096]{2,1,0:T(8,128)(2,1)}, u32[]{:S(2)}) %copy-start.2) | copy-done | bytes 4194328
  29.0 53.8 %states_and_grads.1 = (bf16[512,4096]{1,0:T(8,128)(2,1)S(1)}, bf16[512,256]{1,0:T(8,128)(2,1)S(1)}) custom-call(f32[32]{0:T(128)S(1)} %copy-done.8, bf16[512,4096]{1,0:T(8,128)(2,1)S(1)} %bitcast.13, bf16[512,4096]{1,0:T(8,128)(2,1)S(1)} %bitcast.14, bf16[512,256]{1,0:T(8,128)(2,1)S(1)} %get-tuple-element.21.proj_ref, ...), custom_call_target="tpu_custom_call" | custom-call | tf_op jit(solution)/shard_map/states_and_grads/pallas_call | solution.py:791
  82.8 0.0 copy-done
  82.8 0.0 copy-start.5
  82.9 0.0 copy-start.6
  82.9 0.0 copy-start.7
  82.9 0.0 copy-start.9
  82.9 2.7 %weight_gradient.1 = (bf16[2,2,2,2,4,128,128]{6,5,4,3,2,1,0:T(8,128)(2,1)S(1)}, bf16[512,4096]{1,0:T(8,128)(2,1)}) custom-call(bf16[512,4096]{1,0:T(8,128)(2,1)S(1)} %bitcast.12, bf16[512,256]{1,0:T(8,128)(2,1)S(1)} %get-tuple-element.24.grad_ref, bf16[512,4096]{1,0:T(8,128)(2,1)S(1)} %get-tuple-element.25.gx_ref), custom_call_target="tpu_custom_call" | custom-call | tf_op jit(solution)/shard_map/weight_gradient/pallas_call | solution.py:825
  85.6 0.0 copy-done.5
  85.6 0.0 copy-done.6
  85.6 0.0 copy-done.7
  85.6 0.0 copy-done.9
  85.6 31.1 %sum_and_step.1 = (f32[128,256]{1,0:T(8,128)S(1)}, bf16[128,256]{1,0:T(8,128)(2,1)S(1)}, f32[8,256]{1,0:T(8,128)S(1)}) custom-call(bf16[2,2,2,2,4,128,128]{6,5,4,3,2,1,0:T(8,128)(2,1)S(1)} %get-tuple-element.27.part_ref, f32[128,256]{1,0:T(8,128)S(1)} %copy-done.3, bf16[128,256]{1,0:T(8,128)(2,1)S(1)} %copy-done.5, f32[1,256]{1,0:T(1,128)S(1)} %bitcast.16, ...), custom_call_target="tpu_custom_call" | custom-call | tf_op jit(solution)/shard_map/sum_and_step/pallas_call | solution.py:844
  116.7 0.7 hand_out.1
  (1 shorter events, 0.0 us)
Async XLA Ops:
  0.6 26.2 %copy-start.1 = (bf16[1,512,4096]{2,1,0:T(8,128)(2,1)S(1)}, bf16[1,512,4096]{2,1,0:T(8,128)(2,1)}, u32[]{:S(2)}) copy-start(bf16[1,512,4096]{2,1,0:T(8,128)(2,1)} %param.11) | copy-start | bytes 12582916
  0.6 1.1 copy-start.3
  1.7 1.1 copy-start.4
  2.8 24.0 %copy-start.8 = (f32[32]{0:T(128)S(1)}, f32[32]{0:T(128)}, u32[]{:S(2)}) copy-start(f32[32]{0:T(128)} %skip_ref.1) | copy-start | bytes 388
  26.8 2.2 %copy-start.2 = (bf16[1,512,4096]{2,1,0:T(8,128)(2,1)S(1)}, bf16[1,512,4096]{2,1,0:T(8,128)(2,1)}, u32[]{:S(2)}) copy-start(bf16[1,512,4096]{2,1,0:T(8,128)(2,1)} %param.12) | copy-start | bytes 12582916
  29.0 53.8 %copy-start = (bf16[1,512,4096]{2,1,0:T(8,128)(2,1)S(1)}, bf16[1,512,4096]{2,1,0:T(8,128)(2,1)}, u32[]{:S(2)}) copy-start(bf16[1,512,4096]{2,1,0:T(8,128)(2,1)} %param.10) | copy-start | bytes 12582916
  82.8 2.7 %copy-start.5 = (bf16[128,256]{1,0:T(8,128)(2,1)S(1)}, bf16[128,256]{1,0:T(8,128)(2,1)}, u32[]{:S(2)}) copy-start(bf16[128,256]{1,0:T(8,128)(2,1)} %code_ref.1) | copy-start | bytes 196612
  82.9 2.7 %copy-start.6 = (f32[256]{0:T(256)S(1)}, f32[256]{0:T(256)}, u32[]{:S(2)}) copy-start(f32[256]{0:T(256)} %param.17) | copy-start | bytes 3076
  82.9 2.7 %copy-start.7 = (f32[256]{0:T(256)S(1)}, f32[256]{0:T(256)}, u32[]{:S(2)}) copy-start(f32[256]{0:T(256)} %param.19) | copy-start | bytes 3076
  82.9 2.7 %copy-start.9 = (f32[128]{0:T(128)S(1)}, f32[128]{0:T(128)}, u32[]{:S(2)}) copy-start(f32[128]{0:T(128)} %param.18) | copy-start | bytes 1540

commit v5 on v4

--- a/solution.py
+++ b/solution.py
@@ -85,11 +85,12 @@
 
     layer_copy = pltpu.make_async_copy(layer_ref, layer, load)
     layer_copy.start()
+    greeted = greet_twins(n_pairs, seq, opt)
     got[pair, side, cross, core] = w_ref[...].astype(bf16)
-    greet_twins(n_pairs, seq, opt)
+    greeted()
 
     def send_along(distance, carry):
-        along(lax.rem(pair + distance, n_pairs), pair).start()
+        along(pair_at(pair, n_pairs - distance, n_pairs), pair).start()
         return carry
 
     lax.fori_loop(1, n_pairs, send_along, 0)
@@ -101,7 +102,7 @@
     def turn(d, carry):
         @pl.when(d < n_pairs)
         def _():
-            p = lax.rem(pair + d, n_pairs)
+            p = pair_at(pair, d, n_pairs)
 
             @pl.when(d > 0)
             def _():
@@ -131,7 +132,7 @@
 
         @pl.when(jnp.logical_and(d >= 1, d < n_pairs + 1))
         def _():
-            p = lax.rem(pair + d - 1, n_pairs)
+            p = pair_at(pair, d - 1, n_pairs)
             own_to(0, p, side, 1 - cross).wait_recv()
             relay_to(1, p, side, 1 - cross).start()
             own_to(1, p, 1 - side, cross).wait_recv()
@@ -141,7 +142,7 @@
 
         @pl.when(jnp.logical_and(d >= 2, d < n_pairs + 2))
         def _():
-            p = lax.rem(pair + d - 2, n_pairs)
+            p = pair_at(pair, d - 2, n_pairs)
             relay_to(0, p, 1 - side, 1 - cross).wait_recv()
             relay_to(1, p, 1 - side, 1 - cross).wait_recv()
             to_core(3, p, core).start()
@@ -152,7 +153,7 @@
 
         @pl.when(d >= 3)
         def _():
-            p = lax.rem(pair + d - 3, n_pairs)
+            p = pair_at(pair, d - 3, n_pairs)
             for k in range(4):
                 to_core(k, p, 1 - core).wait_recv()
             w_part = got[p].reshape(-1, got.shape[-1])
@@ -185,6 +186,11 @@
     lax.fori_loop(0, n_pairs, sent, 0)
 
 
+def pair_at(pair, distance, n_pairs):
+    step = jnp.where(2 * pair < n_pairs, distance, n_pairs - distance)
+    return lax.rem(pair + step, n_pairs)
+
+
 def place_of(seq, opt):
     side, core, cross = lax.rem(seq, 2), lax.rem(opt, 2), opt // 2
     twins = (
@@ -207,7 +213,7 @@
     for device in twins:
         hello(device)
     lax.fori_loop(1, n_pairs, hello_pair, 0)
-    pl.semaphore_wait(barrier, n_pairs + 2)
+    return lambda: pl.semaphore_wait(barrier, n_pairs + 2)
 
 
 def remote(src, dst, send_sem, recv_sem, device):
@@ -218,10 +224,10 @@
 
 
 def states_kernel(
-    count, heads, n_pairs, skip_ref, x_ref, dy_ref, proj_ref, run_ref, decay_ref,
+    count, heads, n_pairs, skip_ref, x_hbm, dy_hbm, proj_ref, run_ref, decay_ref,
     gx_ref, gbc_ref,
     b_turned, c_turned, affinity, mixing, acc_b, acc_c, starts, outs, mine, got, chain_in, chain_out,
-    send_y, recv_y, send_c, recv_c,
+    x_ref, dy_ref, load, send_y, recv_y, send_c, recv_c,
 ):
     seq = lax.axis_index("seq")
     opt = lax.axis_index("opt")
@@ -237,8 +243,8 @@
     has_target = (pair < n_pairs - 1, pair > 0)
     places = (pair, n_pairs - 1 - pair)
 
-    late = heads // 4
-    early = 3 * heads // 16
+    late = 5 * heads // 16
+    early = heads // 4
     reach = LAG_CHAIN * (n_pairs - 1)
     wait = max(0, reach - heads + late)
     swap_lag = late + LAG_SWAP
@@ -351,6 +357,20 @@
             acc_c[rows, :] += grow * dot_nt(dy_blk, state_in)
             acc_b[rows, :] += shrink * dot_nt(x_blk, grad_in)
 
+    pieces = load.shape[1]
+    piece_heads = heads // pieces
+
+    def bring(k):
+        lanes = pl.ds(pl.multiple_of(k * piece_heads * head_dim, head_dim), piece_heads * head_dim)
+        pairs = ((x_hbm, x_ref), (dy_hbm, dy_ref))
+        return [
+            pltpu.make_async_copy(source.at[:, lanes], held.at[:, lanes], load.at[n, k])
+            for n, (source, held) in enumerate(pairs)
+        ]
+
+    for k in range(pieces):
+        for copy in bring(k):
+            copy.start()
     barrier = pltpu.get_barrier_semaphore()
     pl.semaphore_signal(barrier, inc=1, device_id=twin, device_id_type=MESH)
     for way in range(2):
@@ -369,6 +389,11 @@
 
     def step(i, carry):
         is_late = jnp.logical_and(i >= early, i < early + late)
+
+        @pl.when(jnp.logical_and(i < heads, lax.rem(i, piece_heads) == 0))
+        def _():
+            for copy in bring(i // piece_heads):
+                copy.wait()
 
         @pl.when(i < heads)
         def _():
@@ -499,36 +524,10 @@
     return finish
 
 
-def weight_kernel(group, layer_ref, grad_ref, gx_ref, part_ref, gx_out, turned, store):
-    put = pltpu.make_async_copy(gx_ref, gx_out, store)
-    put.start()
-    turned[...] = jnp.transpose(grad_ref[...].astype(f32)).astype(bf16)
-
-    _, _, n_i, _, n_r, half, width = part_ref.shape
-    wide = 2 * group * width
-    steps = 2 * n_i * n_r // group
-
-    def step(s, carry):
-        both = dot_nn(turned[...], layer_ref[:, pl.ds(pl.multiple_of(s * wide, wide), wide)])
-        both = both.astype(bf16)
-        for t in range(group):
-            spot = s * group + t
-            p = spot // n_r
-            for c in range(2):
-                lanes = slice((2 * t + c) * width, (2 * t + c + 1) * width)
-                for k in range(2):
-                    rows = slice(k * half, (k + 1) * half)
-                    part_ref[c, k, p // 2, lax.rem(p, 2), lax.rem(spot, n_r)] = both[rows, lanes]
-        return carry
-
-    lax.fori_loop(0, steps, step, 0)
-    put.wait()
-
-
 def step_kernel(
-    n_seq, n_opt, part_ref, w_ref, code_ref, scale_ref, row_ref, col_ref,
+    n_seq, n_opt, layer_ref, grad_ref, w_ref, code_ref, scale_ref, row_ref, col_ref,
     update_ref, code_out, small_out,
-    take_core, give_two, keep_two, take_two, give_three, keep_three, take_three, give_pair, take_pair,
+    grad_turned, part_ref, take_core, give_two, keep_two, take_two, give_three, keep_three, take_three, give_pair, take_pair,
     stats, all_stats, peak, all_peaks,
     send_core, recv_core, send_two, recv_two, send_three, recv_three, send_pair, recv_pair,
     send_c, recv_c, send_d, recv_d,
@@ -544,80 +543,35 @@
     def any_device(i):
         return (i // n_opt, lax.rem(i, n_opt))
 
-    greet_twins(n_pairs, seq, opt)
-    n_i = n_pairs // 2
+    greeted = greet_twins(n_pairs, seq, opt)
     targets = ((cross_twin, side_twin), (side_twin, cross_twin))
     own = ((cross, side), (side, cross))
-    first = [
-        remote(
-            part_ref.at[1 - core, :, :, g], take_core.at[:, :, g],
-            send_core.at[g], recv_core.at[g], core_twin,
+    order = [pair_at(pair, n_pairs - 1 - d, n_pairs) for d in range(n_pairs)]
+
+    def first(p):
+        return remote(
+            part_ref.at[1 - core, :, p], take_core.at[:, p], send_core.at[p], recv_core.at[p],
+            core_twin,
         )
-        for g in range(2)
-    ]
-    second = [
-        [
-            remote(
-                give_two.at[k, g], take_two.at[k, g], send_two.at[k, g], recv_two.at[k, g],
-                targets[0][k],
-            )
-            for k in range(2)
-        ]
-        for g in range(2)
-    ]
-    third = [
-        [
-            remote(
-                give_three.at[k, g], take_three.at[k, g], send_three.at[k, g], recv_three.at[k, g],
-                targets[1][k],
-            )
-            for k in range(2)
-        ]
-        for g in range(2)
-    ]
-
-    def chip_sum(k, g, i, a, b):
+
+    def second(k, p):
+        return remote(
+            give_two.at[k, p], take_two.at[k, p], send_two.at[k, p], recv_two.at[k, p],
+            targets[0][k],
+        )
+
+    def third(k, p):
+        return remote(
+            give_three.at[k, p], take_three.at[k, p], send_three.at[k, p], recv_three.at[k, p],
+            targets[1][k],
+        )
+
+    def chip_sum(k, p, a, b):
         r = a * 2 + b if k == 0 else b * 2 + a
-        return part_ref[core, k, i, g, r].astype(f32) + take_core[k, i, g, r].astype(f32)
-
-    def fill_two(g):
-        def body(q, carry):
-            for k in range(2):
-                total = chip_sum(k, g, q // 2, lax.rem(q, 2), 1 - own[0][k])
-                give_two[k, g, q] = total.astype(bf16)
-            return carry
-
-        lax.fori_loop(0, 2 * n_i, body, 0)
-
-    def stay_two(g):
-        def body(q, carry):
-            for k in range(2):
-                keep_two[k, g, q] = chip_sum(k, g, q // 2, lax.rem(q, 2), own[0][k])
-            return carry
-
-        lax.fori_loop(0, 2 * n_i, body, 0)
-
-    def fill_three(g):
-        def body(i, carry):
-            for k in range(2):
-                q = 2 * i + 1 - own[1][k]
-                total = keep_two[k, g, q] + take_two[k, g, q].astype(f32)
-                give_three[k, g, i] = total.astype(bf16)
-            return carry
-
-        lax.fori_loop(0, n_i, body, 0)
-
-    def stay_three(g):
-        def body(i, carry):
-            for k in range(2):
-                q = 2 * i + own[1][k]
-                keep_three[k, g, i] = keep_two[k, g, q] + take_two[k, g, q].astype(f32)
-            return carry
-
-        lax.fori_loop(0, n_i, body, 0)
-
-    def slice_sum(k, g, i):
-        return keep_three[k, g, i] + take_three[k, g, i].astype(f32)
+        return part_ref[core, k, p, r].astype(f32) + take_core[k, p, r].astype(f32)
+
+    def slice_sum(k, p):
+        return keep_three[k, p] + take_three[k, p].astype(f32)
 
     def to_pair(p, source):
         return remote(
@@ -625,42 +579,58 @@
             (p * 2 + side, opt),
         )
 
-    for copy in first:
-        copy.start()
-    for g in range(2):
-        first[g].wait()
-        fill_two(g)
-        for copy in second[g]:
-            copy.start()
-    for g in range(2):
-        stay_two(g)
-    for g in range(2):
-        for copy in second[g]:
-            copy.wait()
-        fill_three(g)
-        for copy in third[g]:
-            copy.start()
-    for g in range(2):
-        stay_three(g)
-    for g in range(2):
-        for copy in third[g]:
-            copy.wait()
-
-        def send_slices(i, carry):
-            p = 2 * i + g
-
-            @pl.when(p != pair)
-            def _():
+    grad_turned[...] = jnp.transpose(grad_ref[...].astype(f32)).astype(bf16)
+    _, _, _, n_r, half, own_rows = part_ref.shape
+    reach = 2 * n_r * own_rows
+
+    def fill_part(p):
+        columns = pl.ds(pl.multiple_of(p * reach, reach), reach)
+        both = dot_nn(grad_turned[...], layer_ref[:, columns]).astype(bf16)
+        for t in range(n_r):
+            for c in range(2):
+                lanes = slice((2 * t + c) * own_rows, (2 * t + c + 1) * own_rows)
                 for k in range(2):
-                    give_pair[p, k] = slice_sum(k, g, i).astype(bf16)
-                to_pair(p, pair).start()
-
-            return carry
-
-        lax.fori_loop(0, n_i, send_slices, 0)
+                    part_ref[c, k, p, t] = both[k * half : (k + 1) * half, lanes]
+
+    for n_done, p in enumerate(order):
+        fill_part(p)
+        if n_done == 0:
+            greeted()
+        first(p).start()
+    for p in order:
+        first(p).wait()
+        for k in range(2):
+            for a in range(2):
+                give_two[k, p, a] = chip_sum(k, p, a, 1 - own[0][k]).astype(bf16)
+            second(k, p).start()
+    for p in order:
+        for k in range(2):
+            for a in range(2):
+                keep_two[k, p, a] = chip_sum(k, p, a, own[0][k])
+
+    def finish_third(p):
+        for k in range(2):
+            third(k, p).wait()
+
+        if p is not order[-1]:
+            for k in range(2):
+                give_pair[p, k] = slice_sum(k, p).astype(bf16)
+            to_pair(p, pair).start()
+
+    for n_done, p in enumerate(order):
+        for k in range(2):
+            second(k, p).wait()
+            a = 1 - own[1][k]
+            total = keep_two[k, p, a] + take_two[k, p, a].astype(f32)
+            give_three[k, p] = total.astype(bf16)
+            third(k, p).start()
+            a = own[1][k]
+            keep_three[k, p] = keep_two[k, p, a] + take_two[k, p, a].astype(f32)
+        if n_done > 0:
+            finish_third(order[n_done - 1])
+    finish_third(order[-1])
     take_pair[pair] = jnp.zeros_like(take_pair[pair])
-    group_of = lax.rem(pair, 2)
-    totals = [slice_sum(k, group_of, pair // 2) for k in range(2)]
+    totals = [slice_sum(k, pair) for k in range(2)]
     turned = jnp.concatenate(totals, axis=0)
 
     def end_slices(distance, carry):
@@ -725,12 +695,18 @@
     code_out[...] = (moment / scale_next).astype(bf16)
 
 
-def hand_out(update_ref, code_ref, small_ref, update_out, code_out, scale_out, row_out, col_out):
+def hand_out(
+    gx_ref, update_ref, code_ref, small_ref,
+    gx_out, update_out, code_out, scale_out, row_out, col_out, store,
+):
+    put = pltpu.make_async_copy(gx_ref, gx_out, store)
+    put.start()
     update_out[...] = update_ref[...]
     code_out[...] = code_ref[...]
     scale_out[...] = small_ref[0:1, :]
     col_out[...] = small_ref[1:2, :]
     row_out[...] = small_ref[2:3, : row_out.shape[1]]
+    put.wait()
 
 
 def params(mebibytes, **more):
@@ -790,7 +766,7 @@
     inner_states = (heads, max(count - 1, 1), state_dim, head_dim)
     grad_input, grad_bc = pl.pallas_call(
         functools.partial(states_kernel, count, heads, n_pairs),
-        in_specs=[pl.BlockSpec(memory_space=pltpu.SMEM)] + [whole()] * 5,
+        in_specs=[pl.BlockSpec(memory_space=pltpu.SMEM), in_hbm, in_hbm] + [whole()] * 3,
         out_specs=[whole()] * 2,
         out_shape=[
             jax.ShapeDtypeStruct(x.shape, bf16),
@@ -809,51 +785,38 @@
             pltpu.VMEM(per_head, bf16),
             pltpu.VMEM((2, heads, state_dim, head_dim), bf16),
             pltpu.VMEM((3,) + per_head, bf16),
+            pltpu.VMEM(x.shape, bf16),
+            pltpu.VMEM(x.shape, bf16),
+            pltpu.SemaphoreType.DMA((2, 8)),
             pltpu.SemaphoreType.DMA((heads,)),
             pltpu.SemaphoreType.DMA((heads,)),
             pltpu.SemaphoreType.DMA((2, heads)),
             pltpu.SemaphoreType.DMA((2, heads)),
         ],
-        compiler_params=params(26, collective_id=0, has_side_effects=True),
+        compiler_params=params(46, collective_id=0, has_side_effects=True),
         name="states_and_grads",
     )(skip_gain, x, dy, proj, running, decay)
 
     cols = 2 * state_dim
     n = n_seq * n_opt
-    spots = n // 2
-    group = max(2, 2 * LANES // own_rows)
-    part, grad_input = pl.pallas_call(
-        functools.partial(weight_kernel, group),
-        in_specs=[whole()] * 3,
-        out_specs=[whole(), in_hbm],
-        out_shape=[
-            jax.ShapeDtypeStruct((2, 2, n_pairs // 2, 2, 4, state_dim, own_rows), bf16),
-            jax.ShapeDtypeStruct(x.shape, bf16),
-        ],
-        scratch_shapes=[
-            pltpu.VMEM((cols, length), bf16),
-            pltpu.SemaphoreType.DMA,
-        ],
-        compiler_params=params(28),
-        name="weight_gradient",
-    )(layer_rows, grad_bc, grad_input)
-
     block = (state_dim, own_rows)
     tall = jax.ShapeDtypeStruct((own_rows, cols), f32)
     code = jax.ShapeDtypeStruct((own_rows, cols), bf16)
     results = pl.pallas_call(
         functools.partial(step_kernel, n_seq, n_opt),
-        in_specs=[whole()] * 6,
+        in_specs=[whole()] * 7,
         out_specs=[whole()] * 3,
         out_shape=[tall, code, jax.ShapeDtypeStruct((8, cols), f32)],
         scratch_shapes=[
-            pltpu.VMEM((2, n_pairs // 2, 2, 4) + block, bf16),
-            pltpu.VMEM((2, 2, n_pairs) + block, bf16),
-            pltpu.VMEM((2, 2, n_pairs) + block, f32),
-            pltpu.VMEM((2, 2, n_pairs) + block, bf16),
-            pltpu.VMEM((2, 2, n_pairs // 2) + block, bf16),
-            pltpu.VMEM((2, 2, n_pairs // 2) + block, f32),
-            pltpu.VMEM((2, 2, n_pairs // 2) + block, bf16),
+            pltpu.VMEM((cols, length), bf16),
+            pltpu.VMEM((2, 2, n_pairs, 4) + block, bf16),
+            pltpu.VMEM((2, n_pairs, 4) + block, bf16),
+            pltpu.VMEM((2, n_pairs, 2) + block, bf16),
+            pltpu.VMEM((2, n_pairs, 2) + block, f32),
+            pltpu.VMEM((2, n_pairs, 2) + block, bf16),
+            pltpu.VMEM((2, n_pairs) + block, bf16),
+            pltpu.VMEM((2, n_pairs) + block, f32),
+            pltpu.VMEM((2, n_pairs) + block, bf16),
             pltpu.VMEM((n_pairs, 2) + block, bf16),
             pltpu.VMEM((n_pairs, 2) + block, bf16),
             pltpu.VMEM((1, cols + LANES), f32),
@@ -861,23 +824,24 @@
             pltpu.VMEM((1, cols), f32),
             pltpu.VMEM((n, 1, cols), f32),
         ]
-        + dma(2)
-        + [pltpu.SemaphoreType.DMA((2, 2))] * 4
+        + dma(n_pairs)
+        + [pltpu.SemaphoreType.DMA((2, n_pairs))] * 4
         + dma(n_pairs, n, n),
-        compiler_params=params(28, collective_id=1, has_side_effects=True),
+        compiler_params=params(40, collective_id=1, has_side_effects=True),
         name="sum_and_step",
-    )(part, w_bc, m_code, m_scale[None, :], row_stat[None, :], col_stat[None, :])
-    update, code_next, scale_next, row_next, col_next = pl.pallas_call(
+    )(layer_rows, grad_bc, w_bc, m_code, m_scale[None, :], row_stat[None, :], col_stat[None, :])
+    grad_input, update, code_next, scale_next, row_next, col_next = pl.pallas_call(
         hand_out,
-        in_specs=[whole()] * 3,
-        out_specs=[whole()] * 5,
+        in_specs=[whole()] * 4,
+        out_specs=[in_hbm] + [whole()] * 5,
         out_shape=[
-            tall, code, jax.ShapeDtypeStruct((1, cols), f32),
+            jax.ShapeDtypeStruct(x.shape, bf16), tall, code, jax.ShapeDtypeStruct((1, cols), f32),
             jax.ShapeDtypeStruct((1, own_rows), f32), jax.ShapeDtypeStruct((1, cols), f32),
         ],
+        scratch_shapes=[pltpu.SemaphoreType.DMA],
         compiler_params=params(28),
         name="hand_out",
-    )(*results)
+    )(grad_input, *results)
     return (grad_input[None], update, code_next, scale_next[0], row_next[0], col_next[0])
 
 

time: 118 us -> 113 us (0.958)
  local copies, waits for them, and re-layouts: 4.37 us -> 1.78 us
  Pallas kernels: 112 us -> 110 us
    unnamed x20 -> x18, local copies, waits for them, and re-layouts: 4.37 us -> 1.78 us
    pallas_call x2 -> x1, Pallas kernels: 3.39 us -> 2.71 us  [per_device(): pl.pallas_call(hand_out, in_specs=[whole()] * 4, out_specs=[in_hbm] + [wh...]
where the time goes in v5:
time: 113 us
  Pallas kernels  110 us (97%)
  local copies, waits for them, and re-layouts  1.78 us (2%)
    pallas_call x1, Pallas kernels, per_device(): pl.pallas_call(functools.partial(states_kernel, count, heads, n_pairs), i...  53.4 us
    pallas_call x1, Pallas kernels, per_device(): pl.pallas_call(functools.partial(step_kernel, n_seq, n_opt), in_specs=[wh...  30.4 us
    pallas_call x1, Pallas kernels, per_device(): pl.pallas_call(functools.partial(gather_kernel, count, n_seq, n_opt), in_...  24 us
    pallas_call x1, Pallas kernels, per_device(): pl.pallas_call(hand_out, in_specs=[whole()] * 4, out_specs=[in_hbm] + [wh...  2.71 us

profile of v5, /device:TPU:0, one launch (start us, length us, event | category | flops | bytes accessed | tf_op | source)
XLA Modules:
  0.0 112.9 jit_solution(14524617354437675935)
XLA Ops:
  0.6 0.0 copy-start.7
  0.6 0.0 copy-start.1
  0.7 0.9 copy-done.1
  1.6 0.0 copy-start.3
  1.6 0.8 copy-done.3
  2.4 24.0 %gather_and_project.1 = (bf16[512,256]{1,0:T(8,128)(2,1)S(1)}, f32[32,2,256]{2,1,0:T(2,128)S(1)}, f32[2,32,1,128]{3,2,1,0:T(1,128)S(1)}) custom-call(f32[128,256]{1,0:T(8,128)S(1)} %copy-done.1, f32[32,512]{1,0:T(8,128)S(1)} %bitcast.13, bf16[512,4096]{1,0:T(8,128)(2,1)} %bitcast.11), custom_call_target="tpu_custom_call" | custom-call | tf_op jit(solution)/shard_map/gather_and_project/pallas_call | solution.py:740
  26.4 0.0 copy-done.7
  26.4 0.0 copy-start
  26.4 0.0 copy-start.2
  26.4 0.0 copy-start.4
  26.4 0.0 copy-start.5
  26.4 0.0 copy-start.6
  26.4 0.0 copy-start.8
  26.4 53.4 %states_and_grads.1 = (bf16[512,4096]{1,0:T(8,128)(2,1)S(1)}, bf16[512,256]{1,0:T(8,128)(2,1)S(1)}) custom-call(f32[32]{0:T(128)S(1)} %copy-done.7, bf16[512,4096]{1,0:T(8,128)(2,1)} %bitcast.17, bf16[512,4096]{1,0:T(8,128)(2,1)} %bitcast.18, bf16[512,256]{1,0:T(8,128)(2,1)S(1)} %get-tuple-element.20.proj_ref, f32[32,2,256]{2,1,0:T(2,128)S(1)} %get-tuple-element.21.run_ref, ...), custom_call_target="tpu_custom_call" | custom-call | tf_op jit(solution)/shard_map/states_and_grads/pallas_call | solution.py:767
  79.8 0.0 copy-done
  79.8 0.0 copy-done.2
  79.8 0.0 copy-done.4
  79.8 0.0 copy-done.5
  79.8 0.0 copy-done.6
  79.8 0.0 copy-done.8
  79.9 30.4 %sum_and_step.1 = (f32[128,256]{1,0:T(8,128)S(1)}, bf16[128,256]{1,0:T(8,128)(2,1)S(1)}, f32[8,256]{1,0:T(8,128)S(1)}) custom-call(bf16[512,4096]{1,0:T(8,128)(2,1)S(1)} %bitcast.12, bf16[512,256]{1,0:T(8,128)(2,1)S(1)} %get-tuple-element.24.grad_ref, f32[128,256]{1,0:T(8,128)S(1)} %copy-done.2, bf16[128,256]{1,0:T(8,128)(2,1)S(1)} %copy-done.4, ...), custom_call_target="tpu_custom_call" | custom-call | tf_op jit(solution)/shard_map/sum_and_step/pallas_call | solution.py:805
  110.2 2.7 %hand_out.1 = (bf16[512,4096]{1,0:T(8,128)(2,1)}, f32[128,256]{1,0:T(8,128)}, bf16[128,256]{1,0:T(8,128)(2,1)}, f32[1,256]{1,0:T(1,128)}, f32[1,128]{1,0:T(1,128)}, /*index=5*/f32[1,256]{1,0:T(1,128)}) custom-call(bf16[512,4096]{1,0:T(8,128)(2,1)S(1)} %get-tuple-element.23.gx_ref, f32[128,256]{1,0:T(8,128)S(1)} %get-tuple-element.25.update_ref, ...), custom_call_target="tpu_custom_call" | custom-call | tf_op jit(solution)/shard_map/hand_out/pallas_call | solution.py:833
Async XLA Ops:
  0.6 25.7 %copy-start.7 = (f32[32]{0:T(128)S(1)}, f32[32]{0:T(128)}, u32[]{:S(2)}) copy-start(f32[32]{0:T(128)} %skip_ref.1) | copy-start | bytes 388
  0.6 0.9 copy-start.1
  1.6 0.8 copy-start.3
  26.4 53.4 %copy-start = (bf16[1,512,4096]{2,1,0:T(8,128)(2,1)S(1)}, bf16[1,512,4096]{2,1,0:T(8,128)(2,1)}, u32[]{:S(2)}) copy-start(bf16[1,512,4096]{2,1,0:T(8,128)(2,1)} %param.10) | copy-start | bytes 12582916
  26.4 53.4 %copy-start.2 = (f32[128,256]{1,0:T(8,128)S(1)}, f32[128,256]{1,0:T(8,128)}, u32[]{:S(2)}) copy-start(f32[128,256]{1,0:T(8,128)} %w_ref.3) | copy-start | bytes 393220
  26.4 53.4 %copy-start.4 = (bf16[128,256]{1,0:T(8,128)(2,1)S(1)}, bf16[128,256]{1,0:T(8,128)(2,1)}, u32[]{:S(2)}) copy-start(bf16[128,256]{1,0:T(8,128)(2,1)} %code_ref.1) | copy-start | bytes 196612
  26.4 53.4 %copy-start.5 = (f32[256]{0:T(256)S(1)}, f32[256]{0:T(256)}, u32[]{:S(2)}) copy-start(f32[256]{0:T(256)} %param.17) | copy-start | bytes 3076
  26.4 53.4 %copy-start.6 = (f32[256]{0:T(256)S(1)}, f32[256]{0:T(256)}, u32[]{:S(2)}) copy-start(f32[256]{0:T(256)} %param.19) | copy-start | bytes 3076
  26.4 53.4 %copy-start.8 = (f32[128]{0:T(128)S(1)}, f32[128]{0:T(128)}, u32[]{:S(2)}) copy-start(f32[128]{0:T(128)} %param.18) | copy-start | bytes 1540

commit v6 on v5

--- a/solution.py
+++ b/solution.py
@@ -11,6 +11,7 @@
 LANES = 128
 LAG_SWAP = 3
 LAG_CHAIN = 3
+GATHER_SCRATCH = 14
 
 beta_one = 0.9
 beta_two = 0.95
@@ -46,9 +47,9 @@
     return jnp.concatenate([column] * (length // LANES), axis=1)
 
 
-def gather_kernel(
-    count, n_seq, n_opt, w_ref, log_ref, layer_ref, proj_ref, run_ref, decay_ref,
-    got, layer, total, decay, load, send_e, recv_e, send_a, recv_a, send_b, recv_b, send_c, recv_c, send_d, recv_d,
+def gather_part(
+    count, n_seq, n_opt, bring_all, w_ref, log_ref, layer_ref, proj_ref, run_ref, decay,
+    got, layer, total, load, send_e, recv_e, send_a, recv_a, send_b, recv_b, send_c, recv_c, send_d, recv_d,
 ):
     seq = lax.axis_index("seq")
     opt = lax.axis_index("opt")
@@ -94,6 +95,7 @@
         return carry
 
     lax.fori_loop(1, n_pairs, send_along, 0)
+    bring_all()
     ones = (
         lax.broadcasted_iota(jnp.int32, (BLOCK, BLOCK), 0)
         <= lax.broadcasted_iota(jnp.int32, (BLOCK, BLOCK), 1)
@@ -166,7 +168,6 @@
     lax.fori_loop(0, n_pairs + 3, turn, 0)
     proj_ref[...] = total[...].astype(bf16)
     decay_copy().wait()
-    decay_ref[...] = decay[...]
 
     def sent(d, carry):
         p = lax.rem(pair + d, n_pairs)
@@ -183,7 +184,7 @@
             to_core(k, p, core).wait_send()
         return carry
 
-    lax.fori_loop(0, n_pairs, sent, 0)
+    return lambda: lax.fori_loop(0, n_pairs, sent, 0)
 
 
 def pair_at(pair, distance, n_pairs):
@@ -223,9 +224,8 @@
     )
 
 
-def states_kernel(
-    count, heads, n_pairs, skip_ref, x_hbm, dy_hbm, proj_ref, run_ref, decay_ref,
-    gx_ref, gbc_ref,
+def states_part(
+    count, heads, n_pairs, bring, skip_ref, proj_ref, run_ref, decay_ref, gx_ref, gbc_ref,
     b_turned, c_turned, affinity, mixing, acc_b, acc_c, starts, outs, mine, got, chain_in, chain_out,
     x_ref, dy_ref, load, send_y, recv_y, send_c, recv_c,
 ):
@@ -244,7 +244,7 @@
     places = (pair, n_pairs - 1 - pair)
 
     late = 5 * heads // 16
-    early = heads // 4
+    early = 5 * heads // 16
     reach = LAG_CHAIN * (n_pairs - 1)
     wait = max(0, reach - heads + late)
     swap_lag = late + LAG_SWAP
@@ -293,6 +293,12 @@
                 total += other_scale * got[h, way].astype(f32)
             chain_out[way, h, 0] = total.astype(bf16)
             pass_on(way, h).start()
+
+    def end_hops(h):
+        for way in range(2):
+            @pl.when(has_target[way])
+            def _():
+                pass_on(way, h).wait_send()
 
     def local(h):
         adds = []
@@ -357,36 +363,10 @@
             acc_c[rows, :] += grow * dot_nt(dy_blk, state_in)
             acc_b[rows, :] += shrink * dot_nt(x_blk, grad_in)
 
-    pieces = load.shape[1]
-    piece_heads = heads // pieces
-
-    def bring(k):
-        lanes = pl.ds(pl.multiple_of(k * piece_heads * head_dim, head_dim), piece_heads * head_dim)
-        pairs = ((x_hbm, x_ref), (dy_hbm, dy_ref))
-        return [
-            pltpu.make_async_copy(source.at[:, lanes], held.at[:, lanes], load.at[n, k])
-            for n, (source, held) in enumerate(pairs)
-        ]
-
-    for k in range(pieces):
-        for copy in bring(k):
-            copy.start()
-    barrier = pltpu.get_barrier_semaphore()
-    pl.semaphore_signal(barrier, inc=1, device_id=twin, device_id_type=MESH)
-    for way in range(2):
-        @pl.when(has_target[way])
-        def _():
-            pl.semaphore_signal(barrier, inc=1, device_id=(ahead, behind)[way], device_id_type=MESH)
+    piece_heads = heads // load.shape[1]
 
     b_turned[...] = jnp.transpose(proj_ref[:, b_cols].astype(f32))
     c_turned[...] = jnp.transpose(proj_ref[:, c_cols].astype(f32))
-    for way in range(2):
-        @pl.when(jnp.logical_not(has_source[way]))
-        def _():
-            chain_in[way] = jnp.zeros_like(chain_in[way])
-    neighbours = 1 + (pair > 0).astype(jnp.int32) + (pair < n_pairs - 1).astype(jnp.int32)
-    pl.semaphore_wait(barrier, neighbours)
-
     def step(i, carry):
         is_late = jnp.logical_and(i >= early, i < early + late)
 
@@ -437,7 +417,7 @@
 
         @pl.when(jnp.logical_and(slot >= 0, slot < heads - late))
         def _():
-            swap(head_of(slot)).wait_recv()
+            swap(head_of(slot)).wait()
 
         for way in range(2):
             slot = i - swap_lag - LAG_CHAIN * places[way]
@@ -451,14 +431,16 @@
         @pl.when(jnp.logical_and(slot >= 0, slot < heads - late))
         def _():
             finish(head_of(slot), False)
+            end_hops(head_of(slot))
 
         slot = i - swap_lag - wait
 
         @pl.when(jnp.logical_and(slot >= heads - late, slot < heads))
         def _():
             h = head_of(slot)
-            swap_late(h).wait_recv()
+            swap_late(h).wait()
             finish(h, True)
+            end_hops(h)
 
         return carry
 
@@ -468,26 +450,6 @@
         mixed = mixing[b].astype(bf16)
         gbc_ref[rows, b_cols] = (acc_b[rows, :] + dot_nn(mixed, proj_ref[rows, c_cols])).astype(bf16)
         gbc_ref[rows, c_cols] = (acc_c[rows, :] + dot_tn(mixed, proj_ref[rows, b_cols])).astype(bf16)
-
-    def sent(h, carry):
-        is_late = jnp.logical_and(h >= early, h < early + late)
-
-        @pl.when(is_late)
-        def _():
-            swap_late(h).wait_send()
-
-        @pl.when(jnp.logical_not(is_late))
-        def _():
-            swap(h).wait_send()
-
-        for way in range(2):
-            @pl.when(has_target[way])
-            def _():
-                pass_on(way, h).wait_send()
-
-        return carry
-
-    lax.fori_loop(0, heads, sent, 0)
 
 
 def swap_all(n, me, src_of, dst_of, device_of, send_sem, recv_sem):
@@ -516,6 +478,45 @@
         return carry
 
     return lambda: lax.fori_loop(1, n, start, 0), lambda: lax.fori_loop(1, n, finish, 0)
+
+
+def main_kernel(
+    count, heads, n_seq, n_opt, skip_ref, w_ref, log_ref, layer_hbm, x_hbm, dy_hbm, gx_ref, gbc_ref,
+    proj, running, decay, *scratch,
+):
+    gather_scratch, states_scratch = scratch[:GATHER_SCRATCH], scratch[GATHER_SCRATCH:]
+    chain_in = states_scratch[10]
+    x_ref, dy_ref, load = states_scratch[12:15]
+    pieces = load.shape[1]
+    wide = x_ref.shape[1] // pieces
+
+    def bring(k):
+        lanes = pl.ds(pl.multiple_of(k * wide, wide), wide)
+        pairs = ((x_hbm, x_ref), (dy_hbm, dy_ref))
+        return [
+            pltpu.make_async_copy(source.at[:, lanes], held.at[:, lanes], load.at[n, k])
+            for n, (source, held) in enumerate(pairs)
+        ]
+
+    def bring_all():
+        for k in range(pieces):
+            for copy in bring(k):
+                copy.start()
+        pair = lax.axis_index("seq") // 2
+        for way, end in enumerate((0, n_seq // 2 - 1)):
+            @pl.when(pair == end)
+            def _():
+                chain_in[way] = jnp.zeros_like(chain_in[way])
+
+    end_sends = gather_part(
+        count, n_seq, n_opt, bring_all, w_ref, log_ref, layer_hbm, proj, running, decay,
+        *gather_scratch,
+    )
+    states_part(
+        count, heads, n_seq // 2, bring, skip_ref, proj, running, decay, gx_ref, gbc_ref,
+        *states_scratch,
+    )
+    end_sends()
 
 
 def begin_swap(*args):
@@ -699,14 +700,23 @@
     gx_ref, update_ref, code_ref, small_ref,
     gx_out, update_out, code_out, scale_out, row_out, col_out, store,
 ):
-    put = pltpu.make_async_copy(gx_ref, gx_out, store)
-    put.start()
+    pieces = store.shape[0]
+    tall = gx_ref.shape[0] // pieces
+    puts = [
+        pltpu.make_async_copy(
+            gx_ref.at[k * tall : (k + 1) * tall], gx_out.at[k * tall : (k + 1) * tall], store.at[k]
+        )
+        for k in range(pieces)
+    ]
+    for put in puts:
+        put.start()
     update_out[...] = update_ref[...]
     code_out[...] = code_ref[...]
     scale_out[...] = small_ref[0:1, :]
     col_out[...] = small_ref[1:2, :]
     row_out[...] = small_ref[2:3, : row_out.shape[1]]
-    put.wait()
+    for put in puts:
+        put.wait()
 
 
 def params(mebibytes, **more):
@@ -737,65 +747,60 @@
     own_rows = w_bc.shape[0]
 
     in_hbm = pl.BlockSpec(memory_space=pltpu.MemorySpace.HBM)
-    proj, running, decay = pl.pallas_call(
-        functools.partial(gather_kernel, count, n_seq, n_opt),
-        in_specs=[whole(), whole(), in_hbm],
-        out_specs=[whole()] * 3,
-        out_shape=[
-            jax.ShapeDtypeStruct((length, 2 * state_dim), bf16),
-            jax.ShapeDtypeStruct((heads, count, BLOCK), f32),
-            jax.ShapeDtypeStruct((2, heads, 1, LANES), f32),
-        ],
-        scratch_shapes=[
+    per_head = (heads, 2, state_dim, head_dim)
+    inner_states = (heads, max(count - 1, 1), state_dim, head_dim)
+    gather_scratch = (
+        [
             pltpu.VMEM((n_pairs, 2, 2, 2, own_rows, 2 * state_dim), bf16),
             pltpu.VMEM((length, width), bf16),
             pltpu.VMEM((length, 2 * state_dim), f32),
-            pltpu.VMEM((2, heads, 1, LANES), f32),
             pltpu.SemaphoreType.DMA,
             pltpu.SemaphoreType.DMA,
             pltpu.SemaphoreType.DMA,
         ]
         + [pltpu.SemaphoreType.DMA((n_pairs,))] * 2
         + [pltpu.SemaphoreType.DMA((2, n_pairs))] * 4
-        + [pltpu.SemaphoreType.DMA((4, n_pairs))] * 2,
-        compiler_params=params(52, collective_id=2, has_side_effects=True),
-        name="gather_and_project",
-    )(w_bc, log_decay[0], layer_rows)
-
-    per_head = (heads, 2, state_dim, head_dim)
-    inner_states = (heads, max(count - 1, 1), state_dim, head_dim)
+        + [pltpu.SemaphoreType.DMA((4, n_pairs))] * 2
+    )
+    states_scratch = [
+        pltpu.VMEM((state_dim, length), f32),
+        pltpu.VMEM((state_dim, length), f32),
+        pltpu.VMEM((count, BLOCK, BLOCK), f32),
+        pltpu.VMEM((count, BLOCK, BLOCK), f32),
+        pltpu.VMEM((length, state_dim), f32),
+        pltpu.VMEM((length, state_dim), f32),
+        pltpu.VMEM(inner_states, bf16),
+        pltpu.VMEM(inner_states, bf16),
+        pltpu.VMEM(per_head, bf16),
+        pltpu.VMEM(per_head, bf16),
+        pltpu.VMEM((2, heads, state_dim, head_dim), bf16),
+        pltpu.VMEM((3,) + per_head, bf16),
+        pltpu.VMEM(x.shape, bf16),
+        pltpu.VMEM(x.shape, bf16),
+        pltpu.SemaphoreType.DMA((2, 8)),
+        pltpu.SemaphoreType.DMA((heads,)),
+        pltpu.SemaphoreType.DMA((heads,)),
+        pltpu.SemaphoreType.DMA((2, heads)),
+        pltpu.SemaphoreType.DMA((2, heads)),
+    ]
     grad_input, grad_bc = pl.pallas_call(
-        functools.partial(states_kernel, count, heads, n_pairs),
-        in_specs=[pl.BlockSpec(memory_space=pltpu.SMEM), in_hbm, in_hbm] + [whole()] * 3,
+        functools.partial(main_kernel, count, heads, n_seq, n_opt),
+        in_specs=[pl.BlockSpec(memory_space=pltpu.SMEM), whole(), whole(), in_hbm, in_hbm, in_hbm],
         out_specs=[whole()] * 2,
         out_shape=[
             jax.ShapeDtypeStruct(x.shape, bf16),
             jax.ShapeDtypeStruct((length, 2 * state_dim), bf16),
         ],
         scratch_shapes=[
-            pltpu.VMEM((state_dim, length), f32),
-            pltpu.VMEM((state_dim, length), f32),
-            pltpu.VMEM((count, BLOCK, BLOCK), f32),
-            pltpu.VMEM((count, BLOCK, BLOCK), f32),
-            pltpu.VMEM((length, state_dim), f32),
-            pltpu.VMEM((length, state_dim), f32),
-            pltpu.VMEM(inner_states, bf16),
-            pltpu.VMEM(inner_states, bf16),
-            pltpu.VMEM(per_head, bf16),
-            pltpu.VMEM(per_head, bf16),
-            pltpu.VMEM((2, heads, state_dim, head_dim), bf16),
-            pltpu.VMEM((3,) + per_head, bf16),
-            pltpu.VMEM(x.shape, bf16),
-            pltpu.VMEM(x.shape, bf16),
-            pltpu.SemaphoreType.DMA((2, 8)),
-            pltpu.SemaphoreType.DMA((heads,)),
-            pltpu.SemaphoreType.DMA((heads,)),
-            pltpu.SemaphoreType.DMA((2, heads)),
-            pltpu.SemaphoreType.DMA((2, heads)),
-        ],
+            pltpu.VMEM((length, 2 * state_dim), bf16),
+            pltpu.VMEM((heads, count, BLOCK), f32),
+            pltpu.VMEM((2, heads, 1, LANES), f32),
+        ]
+        + gather_scratch
+        + states_scratch,
         compiler_params=params(46, collective_id=0, has_side_effects=True),
-        name="states_and_grads",
-    )(skip_gain, x, dy, proj, running, decay)
+        name="gather_states_and_grads",
+    )(skip_gain, w_bc, log_decay[0], layer_rows, x, dy)
 
     cols = 2 * state_dim
     n = n_seq * n_opt
@@ -838,7 +843,7 @@
             jax.ShapeDtypeStruct(x.shape, bf16), tall, code, jax.ShapeDtypeStruct((1, cols), f32),
             jax.ShapeDtypeStruct((1, own_rows), f32), jax.ShapeDtypeStruct((1, cols), f32),
         ],
-        scratch_shapes=[pltpu.SemaphoreType.DMA],
+        scratch_shapes=[pltpu.SemaphoreType.DMA((8,))],
         compiler_params=params(28),
         name="hand_out",
     )(grad_input, *results)

time: 113 us -> 112 us (level)
    pallas_call x2 -> x1, Pallas kernels: 77.3 us -> 74.9 us  [per_device(): pl.pallas_call(functools.partial(main_kernel, count, heads, n_seq, n_opt)...]
    unnamed x18 -> x16, local copies, waits for them, and re-layouts: 1.78 us -> 2.41 us
where the time goes in v6:
time: 112 us
  Pallas kernels  109 us (97%)
  local copies, waits for them, and re-layouts  2.41 us (2%)
    pallas_call x1, Pallas kernels, per_device(): pl.pallas_call(functools.partial(main_kernel, count, heads, n_seq, n_opt)...  74.9 us
    pallas_call x1, Pallas kernels, per_device(): pl.pallas_call(functools.partial(step_kernel, n_seq, n_opt), in_specs=[wh...  31.2 us
    pallas_call x1, Pallas kernels, per_device(): pl.pallas_call(hand_out, in_specs=[whole()] * 4, out_specs=[in_hbm] + [wh...  2.76 us
    unnamed x16, local copies, waits for them, and re-layouts  2.41 us

profile of v6, /device:TPU:0, one launch (start us, length us, event | category | flops | bytes accessed | tf_op | source)
XLA Modules:
  0.0 111.9 jit_solution(14739750296644725988)
XLA Ops:
  0.6 0.0 copy-start.1
  0.6 0.9 copy-done.1
  1.5 0.0 copy-start.2
  1.5 0.8 copy-done.2
  2.4 0.0 copy-start.6
  2.4 0.7 copy-done.6
  3.0 0.0 copy-start
  3.0 0.0 copy-start.3
  3.0 0.0 copy-start.4
  3.0 0.0 copy-start.5
  3.0 0.0 copy-start.7
  3.1 74.9 %gather_states_and_grads.1 = (bf16[512,4096]{1,0:T(8,128)(2,1)S(1)}, bf16[512,256]{1,0:T(8,128)(2,1)S(1)}) custom-call(f32[32]{0:T(128)S(1)} %copy-done.6, f32[128,256]{1,0:T(8,128)S(1)} %copy-done.1, f32[32,512]{1,0:T(8,128)S(1)} %bitcast.13, bf16[512,4096]{1,0:T(8,128)(2,1)} %bitcast.11, bf16[512,4096]{1,0:T(8,128)(2,1)} %bitcast.17, ...), custom_call_target="tpu_custom_call" | custom-call | tf_op jit(solution)/shard_map/gather_states_and_grads/pallas_call | solution.py:786
  78.0 0.0 copy-done
  78.0 0.0 copy-done.3
  78.0 0.0 copy-done.4
  78.0 0.0 copy-done.5
  78.0 0.0 copy-done.7
  78.0 31.2 %sum_and_step.1 = (f32[128,256]{1,0:T(8,128)S(1)}, bf16[128,256]{1,0:T(8,128)(2,1)S(1)}, f32[8,256]{1,0:T(8,128)S(1)}) custom-call(bf16[512,4096]{1,0:T(8,128)(2,1)S(1)} %bitcast.12, bf16[512,256]{1,0:T(8,128)(2,1)S(1)} %get-tuple-element.18.grad_ref, f32[128,256]{1,0:T(8,128)S(1)} %copy-done.1, bf16[128,256]{1,0:T(8,128)(2,1)S(1)} %copy-done.3, ...), custom_call_target="tpu_custom_call" | custom-call | tf_op jit(solution)/shard_map/sum_and_step/pallas_call | solution.py:810
  109.2 2.8 %hand_out.1 = (bf16[512,4096]{1,0:T(8,128)(2,1)}, f32[128,256]{1,0:T(8,128)}, bf16[128,256]{1,0:T(8,128)(2,1)}, f32[1,256]{1,0:T(1,128)}, f32[1,128]{1,0:T(1,128)}, /*index=5*/f32[1,256]{1,0:T(1,128)}) custom-call(bf16[512,4096]{1,0:T(8,128)(2,1)S(1)} %get-tuple-element.17.gx_ref, f32[128,256]{1,0:T(8,128)S(1)} %get-tuple-element.19.update_ref, ...), custom_call_target="tpu_custom_call" | custom-call | tf_op jit(solution)/shard_map/hand_out/pallas_call | solution.py:838
Async XLA Ops:
  0.6 0.9 copy-start.1
  1.5 0.8 copy-start.2
  2.4 0.7 copy-start.6
  3.0 74.9 %copy-start = (bf16[1,512,4096]{2,1,0:T(8,128)(2,1)S(1)}, bf16[1,512,4096]{2,1,0:T(8,128)(2,1)}, u32[]{:S(2)}) copy-start(bf16[1,512,4096]{2,1,0:T(8,128)(2,1)} %param.10) | copy-start | bytes 12582916
  3.0 74.9 %copy-start.3 = (bf16[128,256]{1,0:T(8,128)(2,1)S(1)}, bf16[128,256]{1,0:T(8,128)(2,1)}, u32[]{:S(2)}) copy-start(bf16[128,256]{1,0:T(8,128)(2,1)} %code_ref.1) | copy-start | bytes 196612
  3.0 74.9 %copy-start.4 = (f32[256]{0:T(256)S(1)}, f32[256]{0:T(256)}, u32[]{:S(2)}) copy-start(f32[256]{0:T(256)} %param.17) | copy-start | bytes 3076
  3.0 74.9 %copy-start.5 = (f32[256]{0:T(256)S(1)}, f32[256]{0:T(256)}, u32[]{:S(2)}) copy-start(f32[256]{0:T(256)} %param.19) | copy-start | bytes 3076
  3.0 75.0 %copy-start.7 = (f32[128]{0:T(128)S(1)}, f32[128]{0:T(128)}, u32[]{:S(2)}) copy-start(f32[128]{0:T(128)} %param.18) | copy-start | bytes 1540

commit v7 on v6

--- a/solution.py
+++ b/solution.py
@@ -471,13 +471,15 @@
         copy_to(distance).start()
         return carry
 
-    def finish(distance, carry):
-        copy = copy_from(distance)
-        copy.wait_send()
-        copy.wait_recv()
+    def arrived(distance, carry):
+        copy_from(distance).wait_recv()
         return carry
 
-    return lambda: lax.fori_loop(1, n, start, 0), lambda: lax.fori_loop(1, n, finish, 0)
+    def left(distance, carry):
+        copy_from(distance).wait_send()
+        return carry
+
+    return [functools.partial(lax.fori_loop, 1, n, body, 0) for body in (start, arrived, left)]
 
 
 def main_kernel(
@@ -520,9 +522,9 @@
 
 
 def begin_swap(*args):
-    start, finish = swap_all(*args)
+    start, arrived, left = swap_all(*args)
     start()
-    return finish
+    return arrived, left
 
 
 def step_kernel(
@@ -652,7 +654,7 @@
     stats[:, :cols] = jnp.sum(grad * grad, axis=0, keepdims=True)
     row_stat = row_ref[...]
     stats[:, cols:] = jnp.broadcast_to(jnp.sum(row_stat, axis=1, keepdims=True), (1, LANES))
-    end_stats = begin_swap(
+    end_stats, stats_left = begin_swap(
         n, me, lambda i: stats, lambda i: all_stats.at[i], any_device, send_c, recv_c
     )
     row_raw = jnp.sum(turned * turned, axis=0, keepdims=True)
@@ -668,7 +670,7 @@
     factor = jnp.minimum(1.0, clip_norm / jnp.sqrt(raw_total + norm_floor))
     moment = old_moment + (1.0 - beta_one) * (grad * factor)
     peak[...] = jnp.max(jnp.abs(moment), axis=0, keepdims=True)
-    end_peaks = begin_swap(
+    end_peaks, peaks_left = begin_swap(
         n, me, lambda i: peak, lambda i: all_peaks.at[i], any_device, send_d, recv_d
     )
     col_next = beta_two * col_ref[...] + (1.0 - beta_two) * (
@@ -686,6 +688,7 @@
     row_column = jnp.transpose(jnp.broadcast_to(row_next / row_mean, (8, rows)))[:, :1]
     second_moment = row_column * col_next
     update_ref[...] = moment / (jnp.sqrt(second_moment) + adam_floor) + weight_decay * w_ref[...]
+    stats_left()
     end_peaks()
     all_peaks[me] = peak[...]
     scale_next = all_peaks[0]
@@ -694,6 +697,7 @@
     scale_next = scale_next + peak_floor
     small_out[0:1, :] = scale_next
     code_out[...] = (moment / scale_next).astype(bf16)
+    peaks_left()
 
 
 def hand_out(

time: 112 us -> 112 us (level)
  no operation moved by 1% of the time
where the time goes in v7:
time: 112 us
  Pallas kernels  109 us (97%)
  local copies, waits for them, and re-layouts  2.41 us (2%)
    pallas_call x1, Pallas kernels, per_device(): pl.pallas_call(functools.partial(main_kernel, count, heads, n_seq, n_opt)...  74.9 us
    pallas_call x1, Pallas kernels, per_device(): pl.pallas_call(functools.partial(step_kernel, n_seq, n_opt), in_specs=[wh...  31.5 us
    pallas_call x1, Pallas kernels, per_device(): pl.pallas_call(hand_out, in_specs=[whole()] * 4, out_specs=[in_hbm] + [wh...  2.76 us
    unnamed x16, local copies, waits for them, and re-layouts  2.41 us

profile of v7, /device:TPU:0, one launch (start us, length us, event | category | flops | bytes accessed | tf_op | source)
XLA Modules:
  0.0 112.3 jit_solution(644911715826187923)
XLA Ops:
  0.6 0.0 copy-start.1
  0.6 0.9 copy-done.1
  1.5 0.0 copy-start.2
  1.5 0.8 copy-done.2
  2.4 0.0 copy-start.6
  2.4 0.7 copy-done.6
  3.0 0.0 copy-start
  3.0 0.0 copy-start.3
  3.0 0.0 copy-start.4
  3.0 0.0 copy-start.5
  3.0 0.0 copy-start.7
  3.1 74.9 %gather_states_and_grads.1 = (bf16[512,4096]{1,0:T(8,128)(2,1)S(1)}, bf16[512,256]{1,0:T(8,128)(2,1)S(1)}) custom-call(f32[32]{0:T(128)S(1)} %copy-done.6, f32[128,256]{1,0:T(8,128)S(1)} %copy-done.1, f32[32,512]{1,0:T(8,128)S(1)} %bitcast.13, bf16[512,4096]{1,0:T(8,128)(2,1)} %bitcast.11, bf16[512,4096]{1,0:T(8,128)(2,1)} %bitcast.17, ...), custom_call_target="tpu_custom_call" | custom-call | tf_op jit(solution)/shard_map/gather_states_and_grads/pallas_call | solution.py:790
  78.0 0.0 copy-done
  78.0 0.0 copy-done.3
  78.0 0.0 copy-done.4
  78.0 0.0 copy-done.5
  78.0 0.0 copy-done.7
  78.0 31.5 %sum_and_step.1 = (f32[128,256]{1,0:T(8,128)S(1)}, bf16[128,256]{1,0:T(8,128)(2,1)S(1)}, f32[8,256]{1,0:T(8,128)S(1)}) custom-call(bf16[512,4096]{1,0:T(8,128)(2,1)S(1)} %bitcast.12, bf16[512,256]{1,0:T(8,128)(2,1)S(1)} %get-tuple-element.18.grad_ref, f32[128,256]{1,0:T(8,128)S(1)} %copy-done.1, bf16[128,256]{1,0:T(8,128)(2,1)S(1)} %copy-done.3, ...), custom_call_target="tpu_custom_call" | custom-call | tf_op jit(solution)/shard_map/sum_and_step/pallas_call | solution.py:814
  109.5 2.8 %hand_out.1 = (bf16[512,4096]{1,0:T(8,128)(2,1)}, f32[128,256]{1,0:T(8,128)}, bf16[128,256]{1,0:T(8,128)(2,1)}, f32[1,256]{1,0:T(1,128)}, f32[1,128]{1,0:T(1,128)}, /*index=5*/f32[1,256]{1,0:T(1,128)}) custom-call(bf16[512,4096]{1,0:T(8,128)(2,1)S(1)} %get-tuple-element.17.gx_ref, f32[128,256]{1,0:T(8,128)S(1)} %get-tuple-element.19.update_ref, ...), custom_call_target="tpu_custom_call" | custom-call | tf_op jit(solution)/shard_map/hand_out/pallas_call | solution.py:842
Async XLA Ops:
  0.6 0.9 copy-start.1
  1.5 0.8 copy-start.2
  2.4 0.7 copy-start.6
  3.0 74.9 %copy-start = (bf16[1,512,4096]{2,1,0:T(8,128)(2,1)S(1)}, bf16[1,512,4096]{2,1,0:T(8,128)(2,1)}, u32[]{:S(2)}) copy-start(bf16[1,512,4096]{2,1,0:T(8,128)(2,1)} %param.10) | copy-start | bytes 12582916
  3.0 74.9 %copy-start.3 = (bf16[128,256]{1,0:T(8,128)(2,1)S(1)}, bf16[128,256]{1,0:T(8,128)(2,1)}, u32[]{:S(2)}) copy-start(bf16[128,256]{1,0:T(8,128)(2,1)} %code_ref.1) | copy-start | bytes 196612
  3.0 74.9 %copy-start.4 = (f32[256]{0:T(256)S(1)}, f32[256]{0:T(256)}, u32[]{:S(2)}) copy-start(f32[256]{0:T(256)} %param.17) | copy-start | bytes 3076
  3.0 74.9 %copy-start.5 = (f32[256]{0:T(256)S(1)}, f32[256]{0:T(256)}, u32[]{:S(2)}) copy-start(f32[256]{0:T(256)} %param.19) | copy-start | bytes 3076
  3.0 75.0 %copy-start.7 = (f32[128]{0:T(128)S(1)}, f32[128]{0:T(128)}, u32[]{:S(2)}) copy-start(f32[128]{0:T(128)} %param.18) | copy-start | bytes 1540
